TPU v7x, 8 devices: a whole 2x2x1 slice. The times are simulated.
8 devices in a mesh: dp: 2 (over z, y), sp: 4 (over x, core).
Axes of the slice: x: 2, y: 2, z: 1, core: 2. Of those that a mesh axis runs over, the one named last changes fastest.
Arguments:
- image_tokens: bfloat16 [32, 1024, 1536], P('dp', 'sp'), parts along dimension 0
- ln1_gain: float32 [2, 1536], replicated
- ln1_shift: float32 [2, 1536], replicated
- w_qkv: bfloat16 [2, 1536, 3, 16, 96], replicated
- b_qkv: float32 [2, 3, 16, 96], replicated
- w_out: bfloat16 [2, 16, 96, 1536], replicated
- b_out: float32 [2, 1536], replicated
- ln2_gain: float32 [2, 1536], replicated
- ln2_shift: float32 [2, 1536], replicated
- w_up: bfloat16 [2, 1536, 6144], replicated
- b_up: float32 [2, 6144], replicated
- w_down: bfloat16 [2, 6144, 1536], replicated
- b_down: float32 [2, 1536], replicated
Outputs:
- output: bfloat16 [32, 1024, 1536], P('dp', 'sp'), parts along dimension 0
There are 2 independent parts. A program takes and returns all parts, laid end to end along the dimension named above; an argument that names none is the same for every part.
All inputs are finite; a program needn't handle non-finite values.
Results may differ from a plain program's by a relative error of at most 0.014479.
Values are sent between devices in bfloat16 or wider.
A program may use at most 1 GiB of HBM per device.

v0:
```python
import jax
import jax.numpy as jnp
from jax import lax
from jax.sharding import PartitionSpec as P

LN_EPS = 1e-6


def layer_norm(tokens, ln_gain, ln_shift):
    values = tokens.astype(jnp.float32)
    mean_val = jnp.mean(values, axis=-1, keepdims=True)
    centred = values - mean_val
    var_val = jnp.mean(centred * centred, axis=-1, keepdims=True)
    return (centred * lax.rsqrt(var_val + LN_EPS) * ln_gain + ln_shift).astype(jnp.bfloat16)


def attend(q_part, k_part, v_part):
    score_scale = q_part.shape[-1] ** -0.5
    scores = jnp.einsum('bqhe,bkhe->bhqk', q_part, k_part, preferred_element_type=jnp.float32) * score_scale
    row_peak = jnp.max(scores, axis=-1, keepdims=True)
    prob_vals = jnp.exp(scores - row_peak)
    row_total = jnp.sum(prob_vals, axis=-1, keepdims=True)
    mixed_vals = jnp.einsum('bhqk,bkhe->bhqe', prob_vals.astype(jnp.bfloat16), v_part, preferred_element_type=jnp.float32)
    return (mixed_vals / row_total).astype(jnp.bfloat16)


def mlp_block(mid_state, ln2_gain, ln2_shift, w_up, b_up, w_down, b_down):
    normed = layer_norm(mid_state, ln2_gain, ln2_shift)
    up_proj = jnp.einsum('bsd,df->bsf', normed, w_up, preferred_element_type=jnp.float32) + b_up
    active = jax.nn.gelu(up_proj, approximate=True).astype(jnp.bfloat16)
    down_proj = jnp.einsum('bsf,fd->bsd', active, w_down, preferred_element_type=jnp.float32) + b_down
    return (mid_state.astype(jnp.float32) + down_proj).astype(jnp.bfloat16)


def solution(mesh):
    token_spec = P('dp', 'sp', None)

    def device_step(image_tokens, ln1_gain, ln1_shift, w_qkv, b_qkv, w_out, b_out, ln2_gain, ln2_shift, w_up, b_up, w_down, b_down):
        hidden = image_tokens
        for layer_idx in range(w_qkv.shape[0]):
            normed = layer_norm(hidden, ln1_gain[layer_idx], ln1_shift[layer_idx])
            qkv_local = (jnp.einsum('bsd,dthe->bsthe', normed, w_qkv[layer_idx], preferred_element_type=jnp.float32) + b_qkv[layer_idx]).astype(jnp.bfloat16)
            qkv_heads = lax.all_to_all(qkv_local, 'sp', 3, 1, tiled=True)
            attn_heads = attend(qkv_heads[:, :, 0], qkv_heads[:, :, 1], qkv_heads[:, :, 2])
            attn_tokens = lax.all_to_all(attn_heads, 'sp', 2, 1, tiled=True)
            attn_proj = jnp.einsum('bhse,hed->bsd', attn_tokens, w_out[layer_idx], preferred_element_type=jnp.float32) + b_out[layer_idx]
            mid_state = (hidden.astype(jnp.float32) + attn_proj).astype(jnp.bfloat16)
            hidden = mlp_block(mid_state, ln2_gain[layer_idx], ln2_shift[layer_idx], w_up[layer_idx], b_up[layer_idx], w_down[layer_idx], b_down[layer_idx])
        return hidden

    return jax.shard_map(device_step, mesh=mesh, in_specs=(token_spec,) + (P(),) * 12, out_specs=token_spec, check_vma=False)
```

profile of v0, /device:TPU:0, one launch (start us, length us, event | category | flops | bytes accessed | tf_op | source)
XLA Modules:
  0.0 2775.9 jit_solution(7272988790817529227)
XLA Ops:
  0.0 6.3 convert_reduce_fusion.3
  6.3 8.0 fusion.48
  14.3 0.0 copy-done
  14.4 0.6 slice_bitcast_fusion.16
  15.0 0.0 copy-done.4
  15.0 0.0 copy-done.5
  15.0 0.7 slice_reduce_fusion.4
  15.6 71.6 %add_convert_fusion.1 = bf16[16,256,3,16,96]{1,4,3,2,0:T(8,128)(2,1)} fusion(f32[3,16,96]{2,1,0:T(8,128)S(1)} %get-tuple-element.20, bf16[2,1536,3,16,96]{1,4,3,2,0:T(8,128)(2,1)} %param.16, bf16[16,256,1536]{2,1,0:T(8,128)(2,1)} %param.13, f32[1536]{0:T(1024)S(1)} %get-tuple-element.16, f32[1536]{0:T(1024)S(1)} %get-tuple-element.31, ...), kind=kOutput, calls=%fused_computation.33 | convolution fusion | flops 58057555968 | bytes 64550912 | tf_op jit(solution)/shard_map/bsd,dthe->bsthe/dot_general | solution.py:42
  87.3 25.0 copy.20
  112.2 428.7 %all_to_all.72 = bf16[16,256,3,16,96]{1,4,2,0,3:T(8,128)(2,1)} all-to-all(bf16[16,256,3,16,96]{1,4,2,0,3:T(8,128)(2,1)} %copy.20), channel_id=1, replica_groups=mesh['dp'=2,'sp'=4] {'sp'}, dimensions={3} | all-to-all | bytes 75497472 | tf_op jit(solution)/shard_map/all_to_all | solution.py:43
  540.9 47.5 %copy.39 = bf16[16,256,3,4,4,96]{1,3,5,4,0,2:T(4,128)(2,1)} copy(bf16[16,256,3,4,4,96]{1,5,2,0,4,3:T(8,128)(2,1)} %bitcast.158) | data formatting | bytes 75497472 | tf_op jit(solution)/shard_map/all_to_all | solution.py:43
  588.4 60.2 %all_to_all.55 = bf16[16,1024,3,4,96]{1,4,3,0,2:T(8,128)(2,1)} reshape(bf16[16,4,256,3,4,96]{2,1,5,4,0,3:T(4,128)(2,1)} %bitcast.159) | data formatting | bytes 75497472 | tf_op jit(solution)/shard_map/all_to_all | solution.py:43
  648.6 94.3 %multiply_reduce_fusion.1 = (f32[16,4,1024]{2,1,0:T(4,128)S(1)}, f32[16,4,1024,1024]{2,3,1,0:T(8,128)}) fusion(bf16[16,1024,3,4,96]{1,4,3,0,2:T(8,128)(2,1)} %all_to_all.55), kind=kOutput, calls=%fused_computation.3 | convolution fusion | flops 13019054080 | bytes 293863424 | tf_op jit(solution)/shard_map/bqhe,bkhe->bhqk/dot_general | solution.py:19
  742.9 80.6 %fusion = f32[16,4,1024]{2,1,0:T(4,128)S(1)} fusion(f32[16,4,1024,1024]{2,3,1,0:T(8,128)} %get-tuple-element.22, f32[16,4,1024]{2,1,0:T(4,128)S(1)} %get-tuple-element.21), kind=kLoop, calls=%fused_computation.4 | loop fusion | flops 201261056 | bytes 268959744 | tf_op jit(solution)/shard_map/reduce_sum | solution.py:22
  823.6 89.6 %divide_convert_fusion.1 = bf16[16,4,1024,96]{2,3,1,0:T(8,128)(2,1)} fusion(f32[16,4,1024]{2,1,0:T(4,128)S(1)} %fusion, f32[16,4,1024,1024]{2,3,1,0:T(8,128)} %get-tuple-element.22, f32[16,4,1024]{2,1,0:T(4,128)S(1)} %get-tuple-element.21, bf16[16,1024,3,4,96]{1,4,3,0,2:T(8,128)(2,1)} %all_to_all.55), kind=kOutput, calls=%fused_computation.79 | convolution fusion | flops 13098811392 | bytes 294125568 | tf_op jit(solution)/shard_map/bhqk,bkhe->bhqe/dot_general | solution.py:23
  913.1 0.0 copy-start.9
  913.1 0.0 copy-start.1
  913.2 27.2 copy.23
  940.3 7.4 all-to-all-start.1
  947.8 0.6 slice_reduce_fusion.3
  948.4 0.6 slice_reduce_fusion.2
  949.0 0.0 copy-done.9
  949.0 0.7 slice_reduce_fusion
  949.7 0.6 fusion.126
  950.3 180.2 %all-to-all-done.1 = bf16[16,4,1024,96]{3,1,0,2:T(4,128)(2,1)} async-done(((bf16[16,4,1024,96]{3,1,0,2:T(4,128)(2,1)}), bf16[16,4,1024,96]{3,1,0,2:T(4,128)(2,1)}, u32[]{:S(2)}, u32[]{:S(2)}) %all-to-all-start.1) | async-done | bytes 12582944 | tf_op jit(solution)/shard_map/all_to_all | solution.py:45
  1130.5 24.5 copy.24
  1154.9 30.6 %convert_reduce_fusion.2 = (f32[16,256]{1,0:T(8,128)S(1)}, bf16[16,256,1536]{2,1,0:T(8,128)(2,1)}) fusion(f32[1536]{0:T(1024)S(1)} %get-tuple-element.12, bf16[16,16,256,96]{2,3,1,0:T(8,128)(2,1)} %bitcast.164, bf16[2,16,96,1536]{3,2,1,0:T(8,128)(2,1)} %param.18, bf16[16,256,1536]{2,1,0:T(8,128)(2,1)} %param.13), kind=kOutput, calls=%fused_computation.42 | convolution fusion | flops 19365097472 | bytes 42489856 | tf_op jit(solution)/shard_map/bhse,hed->bsd/dot_general | solution.py:46
  1185.5 8.0 fusion.44
  1193.6 106.5 %fusion.19.clone.1.clone.5 = bf16[16,256,6144]{2,1,0:T(8,128)(2,1)} fusion(f32[6144]{0:T(1024)S(1)} %bitcast.166, bf16[2,1536,6144]{2,1,0:T(8,128)(2,1)} %param.22, bf16[16,256,1536]{2,1,0:T(8,128)(2,1)} %get-tuple-element.24, f32[1536]{0:T(1024)S(1)} %get-tuple-element.33, f32[1536]{0:T(1024)S(1)} %get-tuple-element.6, ...), kind=kOutput, calls=%fused_computation.23.clone.clone.clone.clone.clone.2 | convolution fusion | flops 77598818304 | bytes 81858560 | tf_op jit(solution)/shard_map/bsd,df->bsf/dot_general | solution.py:29
  1300.1 0.0 copy-done.16
  1300.1 0.0 copy-start.14
  1300.1 90.3 %convert_reduce_fusion.1 = (f32[16,256]{1,0:T(8,128)S(1)}, bf16[16,256,1536]{2,1,0:T(8,128)(2,1)}) fusion(f32[1536]{0:T(1024)S(1)} %copy-done.16, bf16[2,6144,1536]{2,1,0:T(8,128)(2,1)} %param.24, bf16[16,256,1536]{2,1,0:T(8,128)(2,1)} %get-tuple-element.24, bf16[16,256,6144]{2,1,0:T(8,128)(2,1)} %fusion.19.clone.1.clone.5), kind=kOutput, calls=%fused_computation.39 | convolution fusion | flops 77347160064 | bytes 94394368 | tf_op jit(solution)/shard_map/bsf,fd->bsd/dot_general | solution.py:31
  1390.4 8.0 fusion.40
  1398.5 71.8 %add_convert_fusion = bf16[16,256,3,16,96]{1,4,3,2,0:T(8,128)(2,1)} fusion(f32[3,16,96]{2,1,0:T(8,128)S(1)} %copy-done.2, bf16[2,1536,3,16,96]{1,4,3,2,0:T(8,128)(2,1)} %param.16, bf16[16,256,1536]{2,1,0:T(8,128)(2,1)} %get-tuple-element.26, f32[1536]{0:T(1024)S(1)} %copy-done.13, f32[1536]{0:T(1024)S(1)} %copy-done.14, f32[16,256]{1,0:T(8,128)S(1)} %add_rsqrt_fusion.1, ...), kind=kOutput, calls=%fused_computation.32 | convolution fusion | flops 58057555968 | bytes 64550912 | tf_op jit(solution)/shard_map/bsd,dthe->bsthe/dot_general | solution.py:42
  1470.3 25.0 copy.25
  1495.3 427.5 %all_to_all.73 = bf16[16,256,3,16,96]{1,4,2,0,3:T(8,128)(2,1)} all-to-all(bf16[16,256,3,16,96]{1,4,2,0,3:T(8,128)(2,1)} %copy.25), channel_id=1, replica_groups=mesh['dp'=2,'sp'=4] {'sp'}, dimensions={3} | all-to-all | bytes 75497472 | tf_op jit(solution)/shard_map/all_to_all | solution.py:43
  1922.8 47.5 %copy.38 = bf16[16,256,3,4,4,96]{1,3,5,4,0,2:T(4,128)(2,1)} copy(bf16[16,256,3,4,4,96]{1,5,2,0,4,3:T(8,128)(2,1)} %bitcast.160) | data formatting | bytes 75497472 | tf_op jit(solution)/shard_map/all_to_all | solution.py:43
  1970.3 60.2 %all_to_all.63 = bf16[16,1024,3,4,96]{1,4,3,0,2:T(8,128)(2,1)} reshape(bf16[16,4,256,3,4,96]{2,1,5,4,0,3:T(4,128)(2,1)} %bitcast.161) | data formatting | bytes 75497472 | tf_op jit(solution)/shard_map/all_to_all | solution.py:43
  2030.5 94.3 %multiply_reduce_fusion = (f32[16,4,1024]{2,1,0:T(4,128)S(1)}, f32[16,4,1024,1024]{2,3,1,0:T(8,128)}) fusion(bf16[16,1024,3,4,96]{1,4,3,0,2:T(8,128)(2,1)} %all_to_all.63), kind=kOutput, calls=%fused_computation.2 | convolution fusion | flops 13019054080 | bytes 293863424 | tf_op jit(solution)/shard_map/bqhe,bkhe->bhqk/dot_general | solution.py:19
  2124.8 80.6 %fusion.2 = f32[16,4,1024]{2,1,0:T(4,128)S(1)} fusion(f32[16,4,1024,1024]{2,3,1,0:T(8,128)} %get-tuple-element.28, f32[16,4,1024]{2,1,0:T(4,128)S(1)} %get-tuple-element.27), kind=kLoop, calls=%fused_computation.6 | loop fusion | flops 201261056 | bytes 268959744 | tf_op jit(solution)/shard_map/reduce_sum | solution.py:22
  2205.5 89.6 %divide_convert_fusion = bf16[16,4,1024,96]{2,3,1,0:T(8,128)(2,1)} fusion(f32[16,4,1024]{2,1,0:T(4,128)S(1)} %fusion.2, f32[16,4,1024,1024]{2,3,1,0:T(8,128)} %get-tuple-element.28, f32[16,4,1024]{2,1,0:T(4,128)S(1)} %get-tuple-element.27, bf16[16,1024,3,4,96]{1,4,3,0,2:T(8,128)(2,1)} %all_to_all.63), kind=kOutput, calls=%fused_computation.78 | convolution fusion | flops 13098811392 | bytes 294125568 | tf_op jit(solution)/shard_map/bhqk,bkhe->bhqe/dot_general | solution.py:23
  2295.1 27.2 copy.28
  2322.2 194.1 %all_to_all.74 = bf16[16,4,1024,96]{3,1,0,2:T(4,128)(2,1)} all-to-all(bf16[16,4,1024,96]{3,1,0,2:T(4,128)(2,1)} %copy.28), channel_id=1, replica_groups=mesh['dp'=2,'sp'=4] {'sp'}, dimensions={2} | all-to-all | bytes 25165824 | tf_op jit(solution)/shard_map/all_to_all | solution.py:45
  2516.3 24.5 copy.29
  2540.8 30.5 %convert_reduce_fusion = (f32[16,256]{1,0:T(8,128)S(1)}, bf16[16,256,1536]{2,1,0:T(8,128)(2,1)}) fusion(f32[1536]{0:T(1024)S(1)} %copy-done.15, bf16[16,16,256,96]{2,3,1,0:T(8,128)(2,1)} %bitcast.163, bf16[2,16,96,1536]{3,2,1,0:T(8,128)(2,1)} %param.18, bf16[16,256,1536]{2,1,0:T(8,128)(2,1)} %get-tuple-element.26), kind=kOutput, calls=%fused_computation.36 | convolution fusion | flops 19365097472 | bytes 42489856 | tf_op jit(solution)/shard_map/bhse,hed->bsd/dot_general | solution.py:46
  2571.3 8.0 fusion.36
  2579.4 106.7 %fusion.27.clone.5 = bf16[16,256,6144]{2,1,0:T(8,128)(2,1)} fusion(f32[6144]{0:T(1024)S(1)} %bitcast.165, bf16[2,1536,6144]{2,1,0:T(8,128)(2,1)} %param.22, bf16[16,256,1536]{2,1,0:T(8,128)(2,1)} %get-tuple-element.30, f32[1536]{0:T(1024)S(1)} %copy-done.12, f32[1536]{0:T(1024)S(1)} %copy-done.11, f32[16,256]{1,0:T(8,128)S(1)} %add_rsqrt_fusion, ...), kind=kOutput, calls=%fused_computation.31.clone.clone.clone.2 | convolution fusion | flops 77598818304 | bytes 81858560 | tf_op jit(solution)/shard_map/bsd,df->bsf/dot_general | solution.py:29
  2686.1 89.3 %fusion.55 = bf16[16,256,1536]{2,1,0:T(8,128)(2,1)} fusion(bf16[16,256,1536]{2,1,0:T(8,128)(2,1)} %get-tuple-element.30, bf16[2,6144,1536]{2,1,0:T(8,128)(2,1)} %param.24, f32[1536]{0:T(1024)S(1)} %copy-done.10, bf16[16,256,6144]{2,1,0:T(8,128)(2,1)} %fusion.27.clone.5), kind=kOutput, calls=%fused_computation.75 | convolution fusion | flops 77334577152 | bytes 94377984 | tf_op jit(solution)/shard_map/bsf,fd->bsd/dot_general | solution.py:31
  (34 shorter events, 0.1 us)
Async XLA Ops:
  0.0 14.4 copy-start
  0.0 15.0 copy-start.4
  0.0 15.0 copy-start.5
  913.1 34.6 %copy-start.6 = (f32[2,1536]{1,0:T(2,128)S(1)}, f32[2,1536]{1,0:T(2,128)}, u32[]{:S(2)}) copy-start(f32[2,1536]{1,0:T(2,128)} %param.19) | copy-start | bytes 36868
  913.1 35.3 %copy-start.7 = (f32[2,1536]{1,0:T(2,128)S(1)}, f32[2,1536]{1,0:T(2,128)}, u32[]{:S(2)}) copy-start(f32[2,1536]{1,0:T(2,128)} %param.20) | copy-start | bytes 36868
  913.1 35.9 %copy-start.8 = (f32[2,1536]{1,0:T(2,128)S(1)}, f32[2,1536]{1,0:T(2,128)}, u32[]{:S(2)}) copy-start(f32[2,1536]{1,0:T(2,128)} %param.25) | copy-start | bytes 36868
  913.1 35.9 %copy-start.9 = (f32[2,1536]{1,0:T(2,128)S(1)}, f32[2,1536]{1,0:T(2,128)}, u32[]{:S(2)}) copy-start(f32[2,1536]{1,0:T(2,128)} %param.21) | copy-start | bytes 36868
  913.1 36.5 %copy-start.1 = (f32[2,6144]{1,0:T(2,128)S(1)}, f32[2,6144]{1,0:T(2,128)}, u32[]{:S(2)}) copy-start(f32[2,6144]{1,0:T(2,128)} %param.23) | copy-start | bytes 147460
  940.3 190.1 %all-to-all-start.1 = ((bf16[16,4,1024,96]{3,1,0,2:T(4,128)(2,1)}), bf16[16,4,1024,96]{3,1,0,2:T(4,128)(2,1)}, u32[]{:S(2)}, u32[]{:S(2)}) async-start(bf16[16,4,1024,96]{3,1,0,2:T(4,128)(2,1)} %copy.23), calls=%async_computation.1 | async-start | bytes 33554432 | tf_op jit(solution)/shard_map/all_to_all | solution.py:45
  1193.5 106.5 %copy-start.16 = (f32[1536]{0:T(1024)S(1)}, f32[1536]{0:T(1024)}, u32[]{:S(2)}) copy-start(f32[1536]{0:T(1024)} %get-tuple-element.10) | copy-start | bytes 18436
  1300.1 98.4 %copy-start.2 = (f32[3,16,96]{2,1,0:T(8,128)S(1)}, f32[3,16,96]{2,1,0:T(8,128)}, u32[]{:S(2)}) copy-start(f32[3,16,96]{2,1,0:T(8,128)} %get-tuple-element.19) | copy-start | bytes 55300
  1300.1 98.4 %copy-start.13 = (f32[1536]{0:T(1024)S(1)}, f32[1536]{0:T(1024)}, u32[]{:S(2)}) copy-start(f32[1536]{0:T(1024)} %get-tuple-element.15) | copy-start | bytes 18436
  1300.1 98.4 %copy-start.14 = (f32[1536]{0:T(1024)S(1)}, f32[1536]{0:T(1024)}, u32[]{:S(2)}) copy-start(f32[1536]{0:T(1024)} %get-tuple-element.32) | copy-start | bytes 18436
  2322.2 218.5 %copy-start.15 = (f32[1536]{0:T(1024)S(1)}, f32[1536]{0:T(1024)}, u32[]{:S(2)}) copy-start(f32[1536]{0:T(1024)} %get-tuple-element.11) | copy-start | bytes 18436
  2540.8 38.6 %copy-start.3 = (f32[1,6144]{1,0:T(1,128)S(1)}, f32[1,6144]{1,0:T(1,128)}, u32[]{:S(2)}) copy-start(f32[1,6144]{1,0:T(1,128)} %get-tuple-element.17) | copy-start | bytes 73732
  2540.8 38.6 %copy-start.11 = (f32[1536]{0:T(1024)S(1)}, f32[1536]{0:T(1024)}, u32[]{:S(2)}) copy-start(f32[1536]{0:T(1024)} %get-tuple-element.5) | copy-start | bytes 18436
  2540.8 38.6 %copy-start.12 = (f32[1536]{0:T(1024)S(1)}, f32[1536]{0:T(1024)}, u32[]{:S(2)}) copy-start(f32[1536]{0:T(1024)} %get-tuple-element.34) | copy-start | bytes 18436
  2579.4 106.7 %copy-start.10 = (f32[1536]{0:T(1024)S(1)}, f32[1536]{0:T(1024)}, u32[]{:S(2)}) copy-start(f32[1536]{0:T(1024)} %get-tuple-element.9) | copy-start | bytes 18436
where the time goes:
time: 2790 us; the launch traced here: 2780 us
  blocking collectives  1050 us (38%)
  matrix products  965 us (35%)
  local copies, waits for them, and re-layouts  373 us (13%)
  other arithmetic  200 us (7%)
  waiting for transfers between devices  180 us (6%)
    all_to_all x2, blocking collectives, device_step(): qkv_heads = lax.all_to_all(qkv_local, 'sp', 3, 1, tiled=True)  856 us
    all_to_all x4, local copies, waits for them, and re-layouts, device_step(): qkv_heads = lax.all_to_all(qkv_local, 'sp', 3, 1, tiled=True)  215 us
    dot_general x2, matrix products, mlp_block(): jnp.einsum('bsd,df->bsf', normed, w_up, preferred_element_type=jnp.float32)  213 us
    all_to_all x1, blocking collectives, device_step(): attn_tokens = lax.all_to_all(attn_heads, 'sp', 2, 1, tiled=True)  194 us
    dot_general x2, matrix products, attend(): jnp.einsum('bqhe,bkhe->bhqk', q_part, k_part, preferred_element_type=jnp....  189 us
    all_to_all x1, waiting for transfers between devices, device_step(): attn_tokens = lax.all_to_all(attn_heads, 'sp', 2, 1, tiled=True)  180 us
    dot_general x2, matrix products, mlp_block(): jnp.einsum('bsf,fd->bsd', active, w_down, preferred_element_type=jnp.floa...  180 us
    dot_general x2, matrix products, attend(): jnp.einsum('bhqk,bkhe->bhqe', prob_vals.astype(jnp.bfloat16), v_part, pre...  179 us
  transfers between devices with their start and end apart: 1, of which 1 were waited for; matrix products, arithmetic and copies ran while one was open for 0% of the time, Pallas kernels for 0%

commit v1 on v0

--- a/solution.py
+++ b/solution.py
@@ -36,16 +36,14 @@
     token_spec = P('dp', 'sp', None)
 
     def device_step(image_tokens, ln1_gain, ln1_shift, w_qkv, b_qkv, w_out, b_out, ln2_gain, ln2_shift, w_up, b_up, w_down, b_down):
-        hidden = image_tokens
+        hidden = lax.all_to_all(image_tokens, 'sp', 0, 1, tiled=True)
         for layer_idx in range(w_qkv.shape[0]):
             normed = layer_norm(hidden, ln1_gain[layer_idx], ln1_shift[layer_idx])
-            qkv_local = (jnp.einsum('bsd,dthe->bsthe', normed, w_qkv[layer_idx], preferred_element_type=jnp.float32) + b_qkv[layer_idx]).astype(jnp.bfloat16)
-            qkv_heads = lax.all_to_all(qkv_local, 'sp', 3, 1, tiled=True)
-            attn_heads = attend(qkv_heads[:, :, 0], qkv_heads[:, :, 1], qkv_heads[:, :, 2])
-            attn_tokens = lax.all_to_all(attn_heads, 'sp', 2, 1, tiled=True)
-            attn_proj = jnp.einsum('bhse,hed->bsd', attn_tokens, w_out[layer_idx], preferred_element_type=jnp.float32) + b_out[layer_idx]
+            qkv = (jnp.einsum('bsd,dthe->bsthe', normed, w_qkv[layer_idx], preferred_element_type=jnp.float32) + b_qkv[layer_idx]).astype(jnp.bfloat16)
+            attn = attend(qkv[:, :, 0], qkv[:, :, 1], qkv[:, :, 2])
+            attn_proj = jnp.einsum('bhse,hed->bsd', attn, w_out[layer_idx], preferred_element_type=jnp.float32) + b_out[layer_idx]
             mid_state = (hidden.astype(jnp.float32) + attn_proj).astype(jnp.bfloat16)
             hidden = mlp_block(mid_state, ln2_gain[layer_idx], ln2_shift[layer_idx], w_up[layer_idx], b_up[layer_idx], w_down[layer_idx], b_down[layer_idx])
-        return hidden
+        return lax.all_to_all(hidden, 'sp', 1, 0, tiled=True)
 
     return jax.shard_map(device_step, mesh=mesh, in_specs=(token_spec,) + (P(),) * 12, out_specs=token_spec, check_vma=False)

time: 2790 us -> 1500 us (0.54)
  blocking collectives: 1050 us -> 141 us
  local copies, waits for them, and re-layouts: 373 us -> 39.3 us
  waiting for transfers between devices: 180 us -> 135 us
    all_to_all x3 -> x1, blocking collectives: 1050 us -> 141 us  [device_step(): return lax.all_to_all(hidden, 'sp', 1, 0, tiled=True)]
    all_to_all x6 -> x1, local copies, waits for them, and re-layouts: 264 us -> 5.86 us  [device_step(): return lax.all_to_all(hidden, 'sp', 1, 0, tiled=True)]
    convert_element_type x4 -> x2, local copies, waits for them, and re-layouts: 104 us -> 29.5 us  [the longest x1 14.9 us: device_step(): mid_state = (hidden.astype(jnp.float32) + attn_proj).astype(jnp.bfloat16)]
    all_to_all x1, waiting for transfers between devices: 180 us -> 135 us  [device_step(): hidden = lax.all_to_all(image_tokens, 'sp', 0, 1, tiled=True)]
where the time goes in v1:
time: 1500 us; the launch traced here: 1490 us
  matrix products  958 us (64%)
  other arithmetic  208 us (14%)
  blocking collectives  141 us (9%)
  waiting for transfers between devices  135 us (9%)
  local copies, waits for them, and re-layouts  39.3 us (3%)
    dot_general x2, matrix products, mlp_block(): jnp.einsum('bsd,df->bsf', normed, w_up, preferred_element_type=jnp.float32)  212 us
    dot_general x2, matrix products, attend(): jnp.einsum('bqhe,bkhe->bhqk', q_part, k_part, preferred_element_type=jnp....  189 us
    dot_general x2, matrix products, attend(): jnp.einsum('bhqk,bkhe->bhqe', prob_vals.astype(jnp.bfloat16), v_part, pre...  180 us
    dot_general x2, matrix products, mlp_block(): jnp.einsum('bsf,fd->bsd', active, w_down, preferred_element_type=jnp.floa...  180 us
    reduce_sum x2, other arithmetic, attend(): row_total = jnp.sum(prob_vals, axis=-1, keepdims=True)  161 us
    all_to_all x1, blocking collectives, device_step(): return lax.all_to_all(hidden, 'sp', 1, 0, tiled=True)  141 us
    dot_general x2, matrix products, device_step(): jnp.einsum('bsd,dthe->bsthe', normed, w_qkv[layer_idx], preferred_element...  135 us
    all_to_all x1, waiting for transfers between devices, device_step(): hidden = lax.all_to_all(image_tokens, 'sp', 0, 1, tiled=True)  135 us
  transfers between devices with their start and end apart: 1, of which 1 were waited for; matrix products, arithmetic and copies ran while one was open for 0% of the time, Pallas kernels for 0%

profile of v1, /device:TPU:0, one launch (start us, length us, event | category | flops | bytes accessed | tf_op | source)
XLA Modules:
  0.0 1488.2 jit_solution(8912148049859924214)
XLA Ops:
  0.0 0.0 copy-start.9
  0.0 0.0 copy-start
  0.0 0.0 copy-start.1
  0.0 6.4 all-to-all-start
  6.5 0.0 copy-done.5
  6.5 0.6 slice_reduce_fusion.3
  7.1 0.0 copy-done.6
  7.1 0.6 slice_reduce_fusion
  7.8 0.0 copy-done.8
  7.8 0.0 copy-done.7
  7.8 0.7 slice_reduce_fusion.4
  8.4 0.0 copy-done.10
  8.4 0.0 copy-done.9
  8.4 0.7 slice_reduce_fusion.1
  9.1 0.0 copy-done
  9.1 0.6 slice_bitcast_fusion.20
  9.7 0.0 copy-done.1
  9.7 0.6 fusion.96
  10.3 135.0 %all-to-all-done = bf16[16,256,1536]{2,1,0:T(8,128)(2,1)} async-done(((bf16[16,256,1536]{2,1,0:T(8,128)(2,1)}), bf16[16,256,1536]{2,1,0:T(8,128)(2,1)}, u32[]{:S(2)}, u32[]{:S(2)}) %all-to-all-start) | async-done | bytes 12582944 | tf_op jit(solution)/shard_map/all_to_all | solution.py:39
  145.3 7.5 bitcast_convert_fusion
  152.8 2.2 bitcast_reduce_fusion
  155.0 4.5 multiply_reduce_fusion.2
  159.5 8.6 add_convert_fusion.2
  168.1 64.2 %add_convert_fusion.1 = bf16[4,1024,3,16,96]{1,4,3,2,0:T(8,128)(2,1)} fusion(f32[3,16,96]{2,1,0:T(8,128)S(1)} %get-tuple-element.20, bf16[4,1024,1536,1,1]{2,1,4,3,0:T(8,128)(2,1)S(1)} %bitcast.169, bf16[2,1536,3,16,96]{1,4,3,2,0:T(8,128)(2,1)} %param.16), kind=kOutput, calls=%fused_computation.33 | convolution fusion | flops 58019807232 | bytes 64505856 | tf_op jit(solution)/shard_map/bsd,dthe->bsthe/dot_general | solution.py:42
  232.2 94.3 %multiply_reduce_fusion.1 = (f32[4,16,1024]{2,1,0:T(8,128)S(1)}, f32[4,16,1024,1024]{2,3,1,0:T(8,128)}) fusion(bf16[4,1024,3,16,96]{1,4,3,2,0:T(8,128)(2,1)} %add_convert_fusion.1), kind=kOutput, calls=%fused_computation.3 | convolution fusion | flops 13019054080 | bytes 293863424 | tf_op jit(solution)/shard_map/bqhe,bkhe->bhqk/dot_general | solution.py:19
  326.5 80.6 %fusion = f32[4,16,1024]{2,1,0:T(8,128)S(1)} fusion(f32[4,16,1024,1024]{2,3,1,0:T(8,128)} %get-tuple-element.22, f32[4,16,1024]{2,1,0:T(8,128)S(1)} %get-tuple-element.21), kind=kLoop, calls=%fused_computation.4 | loop fusion | flops 201261056 | bytes 268959744 | tf_op jit(solution)/shard_map/reduce_sum | solution.py:22
  407.1 90.0 %divide_convert_fusion.3.clone.5 = bf16[4,16,1024,96]{2,3,1,0:T(8,128)(2,1)} fusion(f32[4,16,1024]{2,1,0:T(8,128)S(1)} %fusion, f32[4,16,1024,1024]{2,3,1,0:T(8,128)} %get-tuple-element.22, f32[4,16,1024]{2,1,0:T(8,128)S(1)} %get-tuple-element.21, bf16[4,1024,3,16,96]{1,4,3,2,0:T(8,128)(2,1)} %add_convert_fusion.1), kind=kOutput, calls=%fused_computation.71.clone.clone.clone.clone.2 | convolution fusion | flops 13098811392 | bytes 294125568 | tf_op jit(solution)/shard_map/bhqk,bkhe->bhqe/dot_general | solution.py:23
  497.1 14.9 %copy.16 = f32[4,4,256,1536]{3,2,0,1:T(8,128)} copy(bf16[4,4,256,1536]{3,2,1,0:T(8,128)(2,1)} %bitcast.41) | data formatting | bytes 37748736 | tf_op jit(solution)/shard_map/convert_element_type | solution.py:45
  512.0 31.5 %convert_reduce_fusion.2 = (f32[4,1024]{1,0:T(4,128)S(1)}, bf16[4,1024,1536]{2,1,0:T(8,128)(2,1)}) fusion(f32[1536]{0:T(1024)S(1)} %copy-done.18, bf16[2,16,96,1536]{3,2,1,0:T(8,128)(2,1)} %param.18, f32[4,4,256,1536]{3,2,0,1:T(8,128)} %copy.16, bf16[4,16,1024,96]{2,3,1,0:T(8,128)(2,1)} %divide_convert_fusion.3.clone.5), kind=kOutput, calls=%fused_computation.42 | convolution fusion | flops 19358806016 | bytes 55072768 | tf_op jit(solution)/shard_map/bhse,hed->bsd/dot_general | solution.py:44
  543.5 8.0 fusion.42
  551.6 0.0 copy-done.4
  551.6 0.0 copy-done.19
  551.6 0.0 copy-done.20
  551.6 0.0 copy-start.17
  551.6 106.2 %fusion.19 = bf16[4,1024,6144]{2,1,0:T(8,128)(2,1)} fusion(f32[6144]{0:T(1024)S(1)} %bitcast.171, bf16[2,1536,6144]{2,1,0:T(8,128)(2,1)} %param.22, bf16[4,1024,1536]{2,1,0:T(8,128)(2,1)} %get-tuple-element.24, f32[1536]{0:T(1024)S(1)} %copy-done.19, f32[1536]{0:T(1024)S(1)} %copy-done.20, f32[4,1024]{1,0:T(4,128)S(1)} %add_rsqrt_fusion.2, ...), kind=kOutput, calls=%fused_computation.23 | convolution fusion | flops 77598818304 | bytes 81858560 | tf_op jit(solution)/shard_map/bsd,df->bsf/dot_general | solution.py:29
  657.9 90.3 %convert_reduce_fusion.1 = (f32[4,1024]{1,0:T(4,128)S(1)}, bf16[4,1024,1536]{2,1,0:T(8,128)(2,1)}) fusion(f32[1536]{0:T(1024)S(1)} %copy-done.17, bf16[4,1024,6144]{2,1,0:T(8,128)(2,1)} %fusion.19, bf16[2,6144,1536]{2,1,0:T(8,128)(2,1)} %param.24, bf16[4,1024,1536]{2,1,0:T(8,128)(2,1)} %get-tuple-element.24), kind=kOutput, calls=%fused_computation.39 | convolution fusion | flops 77347160064 | bytes 94394368 | tf_op jit(solution)/shard_map/bsf,fd->bsd/dot_general | solution.py:31
  748.2 8.0 fusion.38
  756.2 71.0 %add_convert_fusion = bf16[4,1024,3,16,96]{1,4,3,2,0:T(8,128)(2,1)} fusion(f32[3,16,96]{2,1,0:T(8,128)S(1)} %copy-done.3, bf16[2,1536,3,16,96]{1,4,3,2,0:T(8,128)(2,1)} %param.16, bf16[4,1024,1536]{2,1,0:T(8,128)(2,1)} %get-tuple-element.26, f32[1536]{0:T(1024)S(1)} %copy-done.15, f32[1536]{0:T(1024)S(1)} %copy-done.16, f32[4,1024]{1,0:T(4,128)S(1)} %add_rsqrt_fusion.1, ...), kind=kOutput, calls=%fused_computation.32 | convolution fusion | flops 58057555968 | bytes 64550912 | tf_op jit(solution)/shard_map/bsd,dthe->bsthe/dot_general | solution.py:42
  827.3 94.3 %multiply_reduce_fusion = (f32[4,16,1024]{2,1,0:T(8,128)S(1)}, f32[4,16,1024,1024]{2,3,1,0:T(8,128)}) fusion(bf16[4,1024,3,16,96]{1,4,3,2,0:T(8,128)(2,1)} %add_convert_fusion), kind=kOutput, calls=%fused_computation.2 | convolution fusion | flops 13019054080 | bytes 293863424 | tf_op jit(solution)/shard_map/bqhe,bkhe->bhqk/dot_general | solution.py:19
  921.5 80.6 %fusion.2 = f32[4,16,1024]{2,1,0:T(8,128)S(1)} fusion(f32[4,16,1024,1024]{2,3,1,0:T(8,128)} %get-tuple-element.28, f32[4,16,1024]{2,1,0:T(8,128)S(1)} %get-tuple-element.27), kind=kLoop, calls=%fused_computation.6 | loop fusion | flops 201261056 | bytes 268959744 | tf_op jit(solution)/shard_map/reduce_sum | solution.py:22
  1002.1 89.8 %divide_convert_fusion.2.clone.5 = bf16[4,16,1024,96]{2,3,1,0:T(8,128)(2,1)} fusion(f32[4,16,1024]{2,1,0:T(8,128)S(1)} %fusion.2, f32[4,16,1024,1024]{2,3,1,0:T(8,128)} %get-tuple-element.28, f32[4,16,1024]{2,1,0:T(8,128)S(1)} %get-tuple-element.27, bf16[4,1024,3,16,96]{1,4,3,2,0:T(8,128)(2,1)} %add_convert_fusion), kind=kOutput, calls=%fused_computation.70.clone.clone.clone.clone.2 | convolution fusion | flops 13098811392 | bytes 294125568 | tf_op jit(solution)/shard_map/bhqk,bkhe->bhqe/dot_general | solution.py:23
  1091.9 30.7 %convert_reduce_fusion = (f32[4,1024]{1,0:T(4,128)S(1)}, bf16[4,1024,1536]{2,1,0:T(8,128)(2,1)}) fusion(f32[1536]{0:T(1024)S(1)} %copy-done.12, bf16[2,16,96,1536]{3,2,1,0:T(8,128)(2,1)} %param.18, bf16[4,1024,1536]{2,1,0:T(8,128)(2,1)} %get-tuple-element.26, bf16[4,16,1024,96]{2,3,1,0:T(8,128)(2,1)} %divide_convert_fusion.2.clone.5), kind=kOutput, calls=%fused_computation.36 | convolution fusion | flops 19365097472 | bytes 42489856 | tf_op jit(solution)/shard_map/bhse,hed->bsd/dot_general | solution.py:44
  1122.7 8.0 fusion.34
  1130.7 106.3 %fusion.27 = bf16[4,1024,6144]{2,1,0:T(8,128)(2,1)} fusion(f32[6144]{0:T(1024)S(1)} %bitcast.170, bf16[2,1536,6144]{2,1,0:T(8,128)(2,1)} %param.22, bf16[4,1024,1536]{2,1,0:T(8,128)(2,1)} %get-tuple-element.30, f32[1536]{0:T(1024)S(1)} %copy-done.13, f32[1536]{0:T(1024)S(1)} %copy-done.14, f32[4,1024]{1,0:T(4,128)S(1)} %add_rsqrt_fusion, ...), kind=kOutput, calls=%fused_computation.31 | convolution fusion | flops 77598818304 | bytes 81858560 | tf_op jit(solution)/shard_map/bsd,df->bsf/dot_general | solution.py:29
  1237.0 89.3 %fusion.48 = bf16[4,1024,1536]{2,1,0:T(8,128)(2,1)} fusion(bf16[4,1024,1536]{2,1,0:T(8,128)(2,1)} %get-tuple-element.30, bf16[4,1024,6144]{2,1,0:T(8,128)(2,1)} %fusion.27, bf16[2,6144,1536]{2,1,0:T(8,128)(2,1)} %param.24, f32[1536]{0:T(1024)S(1)} %copy-done.11), kind=kOutput, calls=%fused_computation.63 | convolution fusion | flops 77334577152 | bytes 94377984 | tf_op jit(solution)/shard_map/bsf,fd->bsd/dot_general | solution.py:31
  1326.3 14.6 copy.17
  1340.9 141.0 %all_to_all.27 = bf16[4,1024,1536]{2,0,1:T(4,128)(2,1)S(1)} all-to-all(bf16[4,1024,1536]{2,0,1:T(4,128)(2,1)S(1)} %copy.17), channel_id=1, replica_groups=mesh['dp'=2,'sp'=4] {'sp'}, dimensions={1} | all-to-all | bytes 25165824 | tf_op jit(solution)/shard_map/all_to_all | solution.py:47
  1481.9 5.9 copy.18
  (35 shorter events, 0.1 us)
Async XLA Ops:
  0.0 6.5 copy-start.5
  0.0 7.1 copy-start.6
  0.0 7.8 copy-start.8
  0.0 7.8 copy-start.7
  0.0 8.4 copy-start.10
  0.0 8.4 copy-start.9
  0.0 9.1 copy-start
  0.0 9.7 copy-start.1
  0.0 145.3 %all-to-all-start = ((bf16[16,256,1536]{2,1,0:T(8,128)(2,1)}), bf16[16,256,1536]{2,1,0:T(8,128)(2,1)}, u32[]{:S(2)}, u32[]{:S(2)}) async-start(bf16[16,256,1536]{2,1,0:T(8,128)(2,1)} %param.13), calls=%async_computation | async-start | bytes 25165824 | tf_op jit(solution)/shard_map/all_to_all | solution.py:39
  497.1 14.9 %copy-start.18 = (f32[1536]{0:T(1024)S(1)}, f32[1536]{0:T(1024)}, u32[]{:S(2)}) copy-start(f32[1536]{0:T(1024)} %get-tuple-element.16) | copy-start | bytes 18436
  512.0 39.6 %copy-start.4 = (f32[1,6144]{1,0:T(1,128)S(1)}, f32[1,6144]{1,0:T(1,128)}, u32[]{:S(2)}) copy-start(f32[1,6144]{1,0:T(1,128)} %get-tuple-element.18) | copy-start | bytes 73732
  512.0 39.6 %copy-start.19 = (f32[1536]{0:T(1024)S(1)}, f32[1536]{0:T(1024)}, u32[]{:S(2)}) copy-start(f32[1536]{0:T(1024)} %get-tuple-element.10) | copy-start | bytes 18436
  512.0 39.6 %copy-start.20 = (f32[1536]{0:T(1024)S(1)}, f32[1536]{0:T(1024)}, u32[]{:S(2)}) copy-start(f32[1536]{0:T(1024)} %get-tuple-element.33) | copy-start | bytes 18436
  551.6 106.3 %copy-start.17 = (f32[1536]{0:T(1024)S(1)}, f32[1536]{0:T(1024)}, u32[]{:S(2)}) copy-start(f32[1536]{0:T(1024)} %get-tuple-element.6) | copy-start | bytes 18436
  657.8 98.4 %copy-start.3 = (f32[3,16,96]{2,1,0:T(8,128)S(1)}, f32[3,16,96]{2,1,0:T(8,128)}, u32[]{:S(2)}) copy-start(f32[3,16,96]{2,1,0:T(8,128)} %get-tuple-element.19) | copy-start | bytes 55300
  657.9 98.4 %copy-start.15 = (f32[1536]{0:T(1024)S(1)}, f32[1536]{0:T(1024)}, u32[]{:S(2)}) copy-start(f32[1536]{0:T(1024)} %get-tuple-element.13) | copy-start | bytes 18436
  657.9 98.4 %copy-start.16 = (f32[1536]{0:T(1024)S(1)}, f32[1536]{0:T(1024)}, u32[]{:S(2)}) copy-start(f32[1536]{0:T(1024)} %get-tuple-element.32) | copy-start | bytes 18436
  1002.1 89.8 %copy-start.12 = (f32[1536]{0:T(1024)S(1)}, f32[1536]{0:T(1024)}, u32[]{:S(2)}) copy-start(f32[1536]{0:T(1024)} %get-tuple-element.15) | copy-start | bytes 18436
  1091.9 38.8 %copy-start.2 = (f32[1,6144]{1,0:T(1,128)S(1)}, f32[1,6144]{1,0:T(1,128)}, u32[]{:S(2)}) copy-start(f32[1,6144]{1,0:T(1,128)} %get-tuple-element.17) | copy-start | bytes 73732
  1091.9 38.8 %copy-start.13 = (f32[1536]{0:T(1024)S(1)}, f32[1536]{0:T(1024)}, u32[]{:S(2)}) copy-start(f32[1536]{0:T(1024)} %get-tuple-element.9) | copy-start | bytes 18436
  1091.9 38.8 %copy-start.14 = (f32[1536]{0:T(1024)S(1)}, f32[1536]{0:T(1024)}, u32[]{:S(2)}) copy-start(f32[1536]{0:T(1024)} %get-tuple-element.34) | copy-start | bytes 18436
  1130.7 106.3 %copy-start.11 = (f32[1536]{0:T(1024)S(1)}, f32[1536]{0:T(1024)}, u32[]{:S(2)}) copy-start(f32[1536]{0:T(1024)} %get-tuple-element.5) | copy-start | bytes 18436

commit v2 on v1

v2 whole, which is shorter than its diff:
```python
import functools
import jax
import jax.numpy as jnp
from jax import lax
from jax.experimental import pallas as pl
from jax.experimental.pallas import tpu as pltpu
from jax.sharding import PartitionSpec as P

LN_EPS = 1e-6
HD = 96
HEADS = 16
D = 1536
F = 6144
SEQ = 1024
C = HD ** -0.5 * 1.4426950408889634
LOW = 2.0 ** -80
VMEM_MAX = 67043328
f32, bf16 = jnp.float32, jnp.bfloat16

def dot_nt(a, b):
    return lax.dot_general(a, b, (((1,), (1,)), ((), ())), preferred_element_type=f32)

def dot_tn(a, b):
    return lax.dot_general(a, b, (((0,), (0,)), ((), ())), preferred_element_type=f32)

def dot(a, b):
    return jnp.dot(a, b, preferred_element_type=f32)

def ln_rows(load, store, gain, shift, rows, step=16):
    for r in range(0, rows, step):
        v = load(r, step)
        mu = jnp.sum(v, axis=-1, keepdims=True) * (1.0 / D)
        c = v - mu
        var = jnp.sum(c * c, axis=-1, keepdims=True) * (1.0 / D)
        store(r, step, (c * lax.rsqrt(var + LN_EPS) * gain + shift).astype(bf16))

def qkv_kernel(x_ref, xn_ref, g_ref, s_ref, w_hbm, b_ref, q_ref, k_ref, v_ref, nq_ref, nk_ref, w, na, nb, sem, *, layer, tm):
    i = pl.program_id(0)
    ch = 4 * HD
    per = D // ch
    cuts = (0, ch, 4 * ch, 12 * ch)
    order = [1, 0, 2]
    use = [t * D + c * ch for t in order for c in range(per)]
    def copy(n):
        return pltpu.make_async_copy(w_hbm.at[layer, pl.ds(use[n], ch)], w.at[pl.ds(use[n], ch)], sem.at[n])
    gain, shift = g_ref[...], s_ref[...]
    def norm(src, r0, dst):
        def st(r, n, v):
            dst[r:r + n, :] = v
        return lambda lo, n: ln_rows(lambda r, m: src[r0 + lo + r:r0 + lo + r + m, :].astype(f32), lambda r, m, v: st(lo + r, m, v), gain, shift, n)
    @pl.when(i == 0)
    def _():
        for n in range(len(use)):
            copy(n).start()
        norm(x_ref, 0, na)(0, tm)
        copy(0).wait()
    waits = {1: (1, 4), 4: (4, 12)}
    for sub, n_s in ((0, na), (1, nb)):
        nxt = norm(x_ref, tm, nb) if sub == 0 else norm(xn_ref, 0, na)
        cols = slice(sub * tm, (sub + 1) * tm)
        for n in range(len(use)):
            if sub == 0 and n in waits:
                @pl.when(i == 0)
                def _():
                    for c in range(*waits[n]):
                        copy(c).wait()
            t, c = order[n // per], n % per
            r0 = use[n]
            y = dot_nt(w[r0:r0 + ch, :], n_s[...])
            bias = jnp.concatenate([b_ref[r0:r0 + ch, :]] * (tm // 128), axis=1)
            yb = (y + bias).astype(bf16)
            if t == 2:
                v_ref[c * ch:(c + 1) * ch, cols] = yb
            else:
                if t == 0:
                    q_ref[c * ch:(c + 1) * ch, cols] = yb
                for h in range(4):
                    hh = c * 4 + h
                    yh = yb[h * HD:(h + 1) * HD, :]
                    yf = yh.astype(f32)
                    nn = jnp.sum(yf * yf, axis=0, keepdims=True)
                    if t == 0:
                        nq_ref[hh:hh + 1, cols] = nn
                    else:
                        nk_ref[hh:hh + 1, cols] = nn
                        one = (lax.broadcasted_iota(jnp.int32, (32, tm), 0) == 0).astype(f32).astype(bf16)
                        k_ref[hh, cols, :] = jnp.concatenate([yh, one], axis=0).T
            if sub == 0 and n >= 4:
                lo = (n - 4) * (tm // 8)
                nxt(lo, tm // 8)
        if sub == 1:
            nxt(0, tm)

def qkv(x, g, s, wt, b, layer, flags=None):
    T = x.shape[0]
    tm = 512
    n = T // (2 * tm)
    row = pl.BlockSpec((1, D), lambda i: (0, 0))
    col = lambda r: pl.BlockSpec((r, 2 * tm), lambda i: (0, i))
    sd = jax.ShapeDtypeStruct
    return pl.pallas_call(
        functools.partial(qkv_kernel, layer=layer, tm=tm),
        out_shape=(sd((D, T), bf16), sd((HEADS, T, 128), bf16), sd((D, T), bf16), sd((HEADS, T), f32), sd((HEADS, T), f32)),
        grid=(n,),
        in_specs=[pl.BlockSpec((2 * tm, D), lambda i: (i, 0)),
                  pl.BlockSpec((tm, D), lambda i: (jnp.minimum(2 * (i + 1), 2 * n - 1), 0)),
                  row, row, pl.BlockSpec(memory_space=pltpu.HBM), pl.BlockSpec((3 * D, 128), lambda i: (0, 0))],
        out_specs=(col(D), pl.BlockSpec((HEADS, 2 * tm, 128), lambda i: (0, i, 0)), col(D), col(HEADS), col(HEADS)),
        scratch_shapes=[pltpu.VMEM((3 * D, D), bf16), pltpu.VMEM((tm, D), bf16), pltpu.VMEM((tm, D), bf16),
                        pltpu.SemaphoreType.DMA((12,))],
        compiler_params=pltpu.CompilerParams(vmem_limit_bytes=VMEM_MAX, dimension_semantics=("arbitrary",), **({"flags": flags} if flags else {})),
        cost_estimate=pl.CostEstimate(flops=2 * T * D * 3 * D, bytes_accessed=3 * D * D * 2 + T * D * 10, transcendentals=0),
        name="qkv",
    )(x, x, g, s, wt, b)

def attn_kernel(q_ref, k_ref, v_ref, nq_ref, nk_ref, o_ref, *, hp, nq, kb, lag):
    S = q_ref.shape[-1]
    nk = S // kb
    units = [(h, q, k) for h in range(hp) for q in range(S // nq) for k in range(nk)]
    st, lows, acc, rhs = {}, [], {}, {}
    def rows(h):
        return slice(h * HD, (h + 1) * HD)
    def shift_rows(h, q):
        kmax = jnp.max(nk_ref[h:h + 1, :], axis=1, keepdims=True)
        m = jnp.sqrt(nq_ref[h:h + 1, q * nq:(q + 1) * nq] * kmax) * (-1.0 - 2.0 ** -7)
        tile = jnp.where(lax.broadcasted_iota(jnp.int32, (32, nq), 0) == 0, jnp.broadcast_to(m, (32, nq)), 0.0)
        return tile.astype(bf16)
    def score(u):
        h, q, k = u
        if k == 0:
            rhs[h, q] = jnp.concatenate([q_ref[rows(h), q * nq:(q + 1) * nq], shift_rows(h, q)], axis=0)
        st[u] = dot(k_ref[h, k * kb:(k + 1) * kb, :], rhs[h, q])
    def mix(u):
        h, q, k = u
        p = jnp.exp2(st.pop(u) * C)
        ls = jnp.sum(p.reshape(kb // 8, 8, nq), axis=0)
        pv = dot(v_ref[rows(h), k * kb:(k + 1) * kb], p.astype(bf16))
        if k:
            a, b = acc[h, q]
            ls, pv = a + ls, b + pv
        acc[h, q] = (ls, pv)
        if k == nk - 1:
            a, b = acc.pop((h, q))
            l = jnp.sum(a, axis=0, keepdims=True)
            lows.append(l)
            o_ref[rows(h), q * nq:(q + 1) * nq] = (b * (1.0 / l)).astype(bf16)
    n = len(units)
    for i in range(n + lag):
        if i < n:
            score(units[i])
        if i >= lag:
            mix(units[i - lag])
    low = lows[0]
    for l in lows[1:]:
        low = jnp.minimum(low, l)
    low = jnp.min(low)

    @pl.when(jnp.logical_not(low >= LOW))
    def _():
        qb = 256
        def body(j, c):
            h = lax.div(j, S // qb)
            qs = pl.ds(pl.multiple_of(lax.rem(j, S // qb) * qb, qb), qb)
            r = pl.ds(pl.multiple_of(h * HD, 32), HD)
            s = dot(k_ref[h, :, :HD], q_ref[r, qs])
            m = jnp.max(s, axis=0, keepdims=True)
            p = jnp.exp2((s - m) * C)
            l = jnp.sum(p, axis=0, keepdims=True)
            o_ref[r, qs] = (dot(v_ref[r, :], p.astype(bf16)) / l).astype(bf16)
            return c
        lax.fori_loop(0, hp * (S // qb), body, 0)

def attn(q, k, v, nq2, nk2, hp=8, nq=512, kb=256, lag=3, flags=None):
    T = q.shape[1]
    S = SEQ
    nh = HEADS // hp
    blk = pl.BlockSpec((hp * HD, S), lambda i, j: (j, i))
    nrm = pl.BlockSpec((hp, S), lambda i, j: (j, i))
    return pl.pallas_call(
        functools.partial(attn_kernel, hp=hp, nq=nq, kb=kb, lag=lag),
        out_shape=jax.ShapeDtypeStruct((D, T), bf16),
        grid=(T // S, nh),
        in_specs=[blk, pl.BlockSpec((hp, S, 128), lambda i, j: (j, i, 0)), blk, nrm, nrm],
        out_specs=blk,
        compiler_params=pltpu.CompilerParams(vmem_limit_bytes=VMEM_MAX, dimension_semantics=("arbitrary", "arbitrary"), **({"flags": flags} if flags else {})),
        cost_estimate=pl.CostEstimate(flops=4 * T * S * D, bytes_accessed=T * D * 9, transcendentals=T * S * HEADS),
        name="attn",
    )(q, k, v, nq2, nk2)

def gelu(u):
    c = 0.7978845608028654
    return (0.5 * u) * (1.0 + jnp.tanh(u * (c + (c * 0.044715) * (u * u))))

def mlp_kernel(x_hbm, o_hbm, wo_hbm, bo_ref, g_ref, s_ref, wu_hbm, bu_ref, wd_hbm, bd_ref, out_ref,
               xb, ob, wo, wu, wd, m_s, n_s, act, acc, xsem, osem, wsem, *, layer, tm, fc, nc):
    i = pl.program_id(0)
    nblk = pl.num_programs(0)
    nj = F // fc
    def x_copy(b, slot):
        return pltpu.make_async_copy(x_hbm.at[pl.ds(b * tm, tm)], xb.at[slot], xsem.at[slot])
    def o_copy(b, slot):
        return pltpu.make_async_copy(o_hbm.at[:, pl.ds(b * tm, tm)], ob.at[slot], osem.at[slot])
    wo_copy = pltpu.make_async_copy(wo_hbm.at[layer], wo, wsem.at[0])
    def wu_copy(j):
        return pltpu.make_async_copy(wu_hbm.at[layer, :, pl.ds(j * fc, fc)], wu.at[:, pl.ds(j * fc, fc)], wsem.at[1 + j])
    def wd_copy(j):
        return pltpu.make_async_copy(wd_hbm.at[layer, pl.ds(j * fc, fc)], wd.at[pl.ds(j * fc, fc)], wsem.at[1 + nj + j])
    gain, shift = g_ref[...], s_ref[...]
    bo = bo_ref[...]

    def project(slot, c):
        cs = slice(c * nc, (c + 1) * nc)
        y = dot_tn(ob[slot], wo[:, cs])
        m_s[:, cs] = (xb[slot, :, cs].astype(f32) + (y + bo[:, cs])).astype(bf16)

    def norm():
        def st(r, n, v):
            n_s[r:r + n, :] = v
        ln_rows(lambda r, n: m_s[r:r + n, :].astype(f32), st, gain, shift, tm)

    @pl.when(i == 0)
    def _():
        x_copy(0, 0).start()
        o_copy(0, 0).start()
        wo_copy.start()
        wu_copy(0).start()
        for j in range(nj):
            if j + 1 < nj:
                wu_copy(j + 1).start()
            wd_copy(j).start()
        x_copy(1, 1).start()
        o_copy(1, 1).start()
        x_copy(0, 0).wait()
        o_copy(0, 0).wait()
        wo_copy.wait()
        for c in range(D // nc):
            project(0, c)
        norm()
        wu_copy(0).wait()

    def up(j, c):
        f0 = j * fc + c * nc
        u = dot(n_s[...], wu[:, f0:f0 + nc]) + bu_ref[:, f0:f0 + nc]
        act[j % 2, :, c * nc:(c + 1) * nc] = gelu(u).astype(bf16)

    def down(j, c):
        cs = slice(c * nc, (c + 1) * nc)
        y = dot(act[j % 2], wd[j * fc:(j + 1) * fc, cs])
        if j == 0:
            acc[:, cs] = (m_s[:, cs].astype(f32) + bd_ref[:, cs]) + y
        elif j < nj - 1:
            acc[:, cs] = acc[:, cs] + y
        else:
            out_ref[:, cs] = (acc[:, cs] + y).astype(bf16)

    for c in range(fc // nc):
        up(0, c)
    for j in range(1, nj):
        if j <= 2:
            @pl.when(i == 0)
            def _():
                if j == 1:
                    wu_copy(1).wait()
                    wd_copy(0).wait()
                else:
                    for jj in range(2, nj):
                        wu_copy(jj).wait()
                    for jj in range(1, nj):
                        wd_copy(jj).wait()
        for c in range(max(fc, D) // nc):
            if c < fc // nc:
                up(j, c)
            if c < D // nc:
                down(j - 1, c)
    slot = lax.rem(i + 1, 2)

    @pl.when(i + 1 < nblk)
    def _():
        x_copy(i + 1, slot).wait()
        o_copy(i + 1, slot).wait()

    @pl.when(i + 2 < nblk)
    def _():
        x_copy(i + 2, 1 - slot).start()
        o_copy(i + 2, 1 - slot).start()

    for c in range(D // nc):
        project(slot, c)
    for c in range(D // nc):
        down(nj - 1, c)
    norm()

def mlp(x, o, wo, bo, g, s, wu, bu, wd, bd, layer, tm=512, fc=1024, nc=256, flags=None):
    T = x.shape[0]
    row = lambda n: pl.BlockSpec((1, n), lambda i: (0, 0))
    hbm = pl.BlockSpec(memory_space=pltpu.HBM)
    nj = F // fc
    dma = pltpu.SemaphoreType.DMA
    return pl.pallas_call(
        functools.partial(mlp_kernel, layer=layer, tm=tm, fc=fc, nc=nc),
        out_shape=jax.ShapeDtypeStruct((T, D), bf16),
        grid=(T // tm,),
        in_specs=[hbm, hbm, hbm, row(D), row(D), row(D), hbm, row(F), hbm, row(D)],
        out_specs=pl.BlockSpec((tm, D), lambda i: (i, 0)),
        scratch_shapes=[pltpu.VMEM((2, tm, D), bf16), pltpu.VMEM((2, D, tm), bf16), pltpu.VMEM((D, D), bf16),
                        pltpu.VMEM((D, F), bf16), pltpu.VMEM((F, D), bf16), pltpu.VMEM((tm, D), bf16), pltpu.VMEM((tm, D), bf16),
                        pltpu.VMEM((2, tm, fc), bf16), pltpu.VMEM((tm, D), f32), dma((2,)), dma((2,)), dma((1 + 2 * nj,))],
        compiler_params=pltpu.CompilerParams(vmem_limit_bytes=VMEM_MAX, dimension_semantics=("arbitrary",), **({"flags": flags} if flags else {})),
        cost_estimate=pl.CostEstimate(flops=2 * T * D * (2 * F + D), bytes_accessed=(2 * F + D) * D * 2 + T * D * 6, transcendentals=T * F),
        name="mlp",
    )(x, o, wo, bo, g, s, wu, bu, wd, bd)


def solution(mesh):
    token_spec = P('dp', 'sp', None)

    def device_step(image_tokens, ln1_gain, ln1_shift, w_qkv, b_qkv, w_out, b_out, ln2_gain, ln2_shift, w_up, b_up, w_down, b_down):
        layers = w_qkv.shape[0]
        w_t = w_qkv.transpose(0, 2, 3, 4, 1).reshape(layers, 3 * D, D)
        b_t = jnp.broadcast_to(b_qkv.reshape(layers, 3 * D, 1), (layers, 3 * D, 128))
        w_o = w_out.reshape(layers, D, D)
        hidden = lax.all_to_all(image_tokens, 'sp', 0, 1, tiled=True)
        shape = hidden.shape
        h = hidden.reshape(-1, D)
        for l in range(layers):
            row = lambda a: a[l].reshape(1, -1)
            q, k, v, nq2, nk2 = qkv(h, row(ln1_gain), row(ln1_shift), w_t, b_t[l], l)
            o = attn(q, k, v, nq2, nk2)
            h = mlp(h, o, w_o, row(b_out), row(ln2_gain), row(ln2_shift), w_up, row(b_up), w_down, row(b_down), l)
        return lax.all_to_all(h.reshape(shape), 'sp', 1, 0, tiled=True)

    return jax.shard_map(device_step, mesh=mesh, in_specs=(token_spec,) + (P(),) * 12, out_specs=token_spec, check_vma=False)
```

time: 1500 us -> 1070 us (0.71)
  matrix products: 958 us -> 0 us
  Pallas kernels: 0 us -> 732 us
  other arithmetic: 208 us -> 0 us
    dot_general x12 -> x0, matrix products: 958 us -> none  [the longest x2 212 us: mlp_block(): jnp.einsum('bsd,df->bsf', normed, w_up, preferred_element_type=jnp.float32)]
    pallas_call x0 -> x6, Pallas kernels: none -> 732 us  [the longest x2 461 us: mlp(): pl.pallas_call(functools.partial(mlp_kernel, layer=layer, tm=tm, fc=fc, n...]
    reduce_sum x7 -> x0, other arithmetic: 192 us -> none  [the longest x2 161 us: attend(): row_total = jnp.sum(prob_vals, axis=-1, keepdims=True)]
    convert_element_type x2 -> x0, local copies, waits for them, and re-layouts: 29.5 us -> none  [the longest x1 14.9 us: device_step(): mid_state = (hidden.astype(jnp.float32) + attn_proj).astype(jnp.bfloat16)]
    convert_element_type x2 -> x0, other arithmetic: 16.1 us -> none  [the longest x1 8.56 us: layer_norm(): (centred * lax.rsqrt(var_val + LN_EPS) * ln_gain + ln_shift).astype(jnp.b...]
where the time goes in v2:
time: 1070 us; the launch traced here: 1060 us
  Pallas kernels  732 us (68%)
  blocking collectives  141 us (13%)
  waiting for transfers between devices  135 us (13%)
  local copies, waits for them, and re-layouts  40.8 us (4%)
    pallas_call x2, Pallas kernels, mlp(): pl.pallas_call(functools.partial(mlp_kernel, layer=layer, tm=tm, fc=fc, n...  461 us
    pallas_call x2, Pallas kernels, qkv(): pl.pallas_call(functools.partial(qkv_kernel, layer=layer, tm=tm), out_sha...  153 us
    all_to_all x1, blocking collectives, device_step(): return lax.all_to_all(h.reshape(shape), 'sp', 1, 0, tiled=True)  141 us
    all_to_all x1, waiting for transfers between devices, device_step(): hidden = lax.all_to_all(image_tokens, 'sp', 0, 1, tiled=True)  135 us
    pallas_call x2, Pallas kernels, attn(): pl.pallas_call(functools.partial(attn_kernel, hp=hp, nq=nq, kb=kb, lag=la...  119 us
  transfers between devices with their start and end apart: 1, of which 1 were waited for; matrix products, arithmetic and copies ran while one was open for 0% of the time, Pallas kernels for 0%

profile of v2, /device:TPU:0, one launch (start us, length us, event | category | flops | bytes accessed | tf_op | source)
XLA Modules:
  0.0 1056.5 jit_solution(12483616306974552916)
XLA Ops:
  0.0 0.0 copy-start
  0.0 0.0 copy-start.3
  0.0 0.0 copy-start.2
  0.0 0.0 copy-start.5
  0.0 0.0 copy-start.4
  0.0 0.0 copy-start.7
  0.0 0.0 copy-start.6
  0.0 0.0 copy-start.1
  0.0 6.5 all-to-all-start
  6.5 0.0 copy-done
  6.5 0.1 broadcast_in_dim.11
  6.6 0.7 broadcast_in_dim.13
  7.3 0.0 copy-done.3
  7.3 0.0 copy-done.2
  7.3 0.6 fusion.6
  7.9 0.0 copy-done.5
  7.9 0.0 copy-done.4
  7.9 0.6 fusion.2
  8.6 0.0 copy-done.7
  8.6 0.0 copy-done.6
  8.6 0.6 fusion.4
  9.2 0.0 copy-done.1
  9.2 0.7 fusion
  9.9 135.5 %all-to-all-done = bf16[16,256,1536]{2,1,0:T(8,128)(2,1)} async-done(((bf16[16,256,1536]{2,1,0:T(8,128)(2,1)}), bf16[16,256,1536]{2,1,0:T(8,128)(2,1)}, u32[]{:S(2)}, u32[]{:S(2)}) %all-to-all-start) | async-done | bytes 12582944 | tf_op jit(solution)/shard_map/all_to_all | solution.py:322
  145.3 10.6 copy.16
  155.9 3.0 broadcast_in_dim.12.b_ref
  158.9 76.5 %qkv.2 = (bf16[1536,4096]{1,0:T(8,128)(2,1)}, bf16[16,4096,128]{2,1,0:T(8,128)(2,1)}, bf16[1536,4096]{1,0:T(8,128)(2,1)}, f32[16,4096]{1,0:T(8,128)}, f32[16,4096]{1,0:T(8,128)}) custom-call(bf16[4096,1536]{1,0:T(8,128)(2,1)} %bitcast.18, bf16[4096,1536]{1,0:T(8,128)(2,1)} %bitcast.19, f32[1,1536]{1,0:T(1,128)} %get-tuple-element.41.g_ref, ...), custom_call_target="tpu_custom_call" | custom-call | flops 57982058496 | bytes 77070336 | tf_op jit(solution)/shard_map/qkv/pallas_call | solution.py:101
  235.4 59.4 %attn.2.o_hbm = bf16[1536,4096]{1,0:T(8,128)(2,1)} custom-call(bf16[1536,4096]{1,0:T(8,128)(2,1)} %get-tuple-element.15.q_ref, bf16[16,4096,128]{2,1,0:T(8,128)(2,1)} %get-tuple-element.16.k_ref, bf16[1536,4096]{1,0:T(8,128)(2,1)} %get-tuple-element.17.v_ref, f32[16,4096]{1,0:T(8,128)} %get-tuple-element.18.nq_ref, f32[16,4096]{1,0:T(8,128)} %get-tuple-element.19.nk_ref), custom_call_target="tpu_custom_call" | custom-call | flops 25769803776 | bytes 56623104 | tf_op jit(solution)/shard_map/attn/pallas_call | solution.py:179
  294.7 243.1 %mlp.2.x_ref.xn_ref.x_hbm = bf16[4096,1536]{1,0:T(8,128)(2,1)} custom-call(bf16[4096,1536]{1,0:T(8,128)(2,1)} %bitcast.20, bf16[1536,4096]{1,0:T(8,128)(2,1)} %attn.2.o_hbm, bf16[2,1536,1536]{2,1,0:T(8,128)(2,1)} %bitcast.24, f32[1,1536]{1,0:T(1,128)} %get-tuple-element.45.bo_ref, f32[1,1536]{1,0:T(1,128)} %get-tuple-element.34.g_ref, ...), custom_call_target="tpu_custom_call" | custom-call | flops 173946175488 | bytes 80216064 | tf_op jit(solution)/shard_map/mlp/pallas_call | solution.py:299
  537.8 3.4 broadcast_in_dim.14.b_ref
  541.2 76.6 %qkv.3 = (bf16[1536,4096]{1,0:T(8,128)(2,1)}, bf16[16,4096,128]{2,1,0:T(8,128)(2,1)}, bf16[1536,4096]{1,0:T(8,128)(2,1)}, f32[16,4096]{1,0:T(8,128)}, f32[16,4096]{1,0:T(8,128)}) custom-call(bf16[4096,1536]{1,0:T(8,128)(2,1)} %mlp.2.x_ref.xn_ref.x_hbm, bf16[4096,1536]{1,0:T(8,128)(2,1)} %mlp.2.x_ref.xn_ref.x_hbm, f32[1,1536]{1,0:T(1,128)} %get-tuple-element.42.g_ref, ...), custom_call_target="tpu_custom_call" | custom-call | flops 57982058496 | bytes 77070336 | tf_op jit(solution)/shard_map/qkv/pallas_call | solution.py:101
  617.8 59.4 %attn.3.o_hbm = bf16[1536,4096]{1,0:T(8,128)(2,1)} custom-call(bf16[1536,4096]{1,0:T(8,128)(2,1)} %get-tuple-element.20.q_ref, bf16[16,4096,128]{2,1,0:T(8,128)(2,1)} %get-tuple-element.21.k_ref, bf16[1536,4096]{1,0:T(8,128)(2,1)} %get-tuple-element.22.v_ref, f32[16,4096]{1,0:T(8,128)} %get-tuple-element.23.nq_ref, f32[16,4096]{1,0:T(8,128)} %get-tuple-element.24.nk_ref), custom_call_target="tpu_custom_call" | custom-call | flops 25769803776 | bytes 56623104 | tf_op jit(solution)/shard_map/attn/pallas_call | solution.py:179
  677.2 217.5 %mlp.3 = bf16[4096,1536]{1,0:T(8,128)(2,1)} custom-call(bf16[4096,1536]{1,0:T(8,128)(2,1)} %mlp.2.x_ref.xn_ref.x_hbm, bf16[1536,4096]{1,0:T(8,128)(2,1)} %attn.3.o_hbm, bf16[2,1536,1536]{2,1,0:T(8,128)(2,1)} %bitcast.25, f32[1,1536]{1,0:T(1,128)} %get-tuple-element.46.bo_ref, f32[1,1536]{1,0:T(1,128)} %get-tuple-element.33.g_ref, ...), custom_call_target="tpu_custom_call" | custom-call | flops 173946175488 | bytes 80216064 | tf_op jit(solution)/shard_map/mlp/pallas_call | solution.py:299
  894.7 14.6 %copy.17 = bf16[4,1024,1536]{2,0,1:T(4,128)(2,1)S(1)} copy(bf16[4,1024,1536]{2,1,0:T(8,128)(2,1)} %bitcast.21) | data formatting | bytes 25165824 | tf_op jit(solution)/shard_map/reshape | solution.py:330
  909.3 141.0 %all_to_all.33 = bf16[4,1024,1536]{2,0,1:T(4,128)(2,1)S(1)} all-to-all(bf16[4,1024,1536]{2,0,1:T(4,128)(2,1)S(1)} %copy.17), channel_id=1, replica_groups=mesh['dp'=2,'sp'=4] {'sp'}, dimensions={1} | all-to-all | bytes 25165824 | tf_op jit(solution)/shard_map/all_to_all | solution.py:330
  1050.3 5.9 copy.18
  (1 shorter events, 0.0 us)
Async XLA Ops:
  0.0 6.5 copy-start
  0.0 7.3 copy-start.3
  0.0 7.3 copy-start.2
  0.0 7.9 copy-start.5
  0.0 7.9 copy-start.4
  0.0 8.5 copy-start.7
  0.0 8.5 copy-start.6
  0.0 9.2 copy-start.1
  0.0 145.3 %all-to-all-start = ((bf16[16,256,1536]{2,1,0:T(8,128)(2,1)}), bf16[16,256,1536]{2,1,0:T(8,128)(2,1)}, u32[]{:S(2)}, u32[]{:S(2)}) async-start(bf16[16,256,1536]{2,1,0:T(8,128)(2,1)} %param.13), calls=%async_computation | async-start | bytes 25165824 | tf_op jit(solution)/shard_map/all_to_all | solution.py:322

commit v3 on v1

v3 whole, which is shorter than its diff:
```python
import functools

import jax
import jax.numpy as jnp
from jax import lax
from jax.experimental import pallas as pl
from jax.experimental.pallas import tpu as pltpu
from jax.sharding import PartitionSpec as P

LN_EPS = 1e-6
HD = 96
HEADS = 16
D = HD * HEADS
F = 4 * D
IMAGES = 4
BLK = 256
SEQ = 4 * BLK
T = IMAGES * SEQ
CH = 4 * HD
C = HD ** -0.5 * 1.4426950408889634
LOW = 2.0 ** -80
VMEM_MAX = 67043328
f32, bf16 = jnp.float32, jnp.bfloat16
MESH = pl.DeviceIdType.MESH
HBM = pl.BlockSpec(memory_space=pltpu.HBM)


def dot(a, b):
    return jnp.dot(a, b, preferred_element_type=f32)


def dot_nt(a, b):
    return lax.dot_general(a, b, (((1,), (1,)), ((), ())), preferred_element_type=f32)


def dot_tn(a, b):
    return lax.dot_general(a, b, (((0,), (0,)), ((), ())), preferred_element_type=f32)


def row(n):
    return pl.BlockSpec((1, n), lambda *_: (0, 0))


def ln_rows(load, store, gain, shift, start, rows, step=16):
    for r in range(start, start + rows, step):
        v = load(r, step).astype(f32)
        mu = jnp.sum(v, axis=-1, keepdims=True) * (1.0 / D)
        c = v - mu
        var = jnp.sum(c * c, axis=-1, keepdims=True) * (1.0 / D)
        store(r, step, (c * lax.rsqrt(var + LN_EPS) * gain + shift).astype(bf16))


def qkv_kernel(*refs, layer, n, copy_h, alias):
    (_, xa, xb, xan, xbn, g_ref, s_ref, w_hbm, b_ref), refs = refs[:9], refs[9:]
    refs = refs[alias:]
    (q_ref, k_ref, v_ref, nq_ref, nk_ref), refs = refs[:5], refs[5:]
    if copy_h:
        h_ref, refs = refs[0], refs[1:]
    w, n_s, n_next, sem = refs
    i = pl.program_id(0)
    tm = 2 * BLK
    per = D // CH
    order = (1, 0, 2)
    gain, shift = g_ref[...], s_ref[...]

    def w_rows(o, c):
        return order[o] * D + c * CH

    def w_copy(o, c):
        r = pl.ds(w_rows(o, c), CH)
        return pltpu.make_async_copy(w_hbm.at[layer, r], w.at[r], sem.at[o * per + c])

    def norm(a, b, dst, start, rows):
        def load(r, m):
            return a[0, r:r + m, :] if r < BLK else b[0, r - BLK:r - BLK + m, :]
        def store(r, m, v):
            dst[r:r + m, :] = v
        ln_rows(load, store, gain, shift, start, rows)

    def project(o, c):
        t = order[o]
        if isinstance(c, int):
            r0, rw = c * CH, t * D + c * CH
        else:
            r0, rw = pl.multiple_of(c * CH, CH), pl.multiple_of(t * D + c * CH, CH)
        y = dot_nt(w[pl.ds(rw, CH), :], n_s[...])
        bias = jnp.concatenate([b_ref[pl.ds(rw, CH), :]] * (tm // 128), axis=1)
        yb = (y + bias).astype(bf16)
        if t == 2:
            v_ref[pl.ds(r0, CH), :] = yb
            return
        if t == 0:
            q_ref[pl.ds(r0, CH), :] = yb
        for h in range(CH // HD):
            hh = c * (CH // HD) + h
            yh = yb[h * HD:(h + 1) * HD, :]
            yf = yh.astype(f32)
            nn = jnp.sum(yf * yf, axis=0, keepdims=True)
            if t == 0:
                nq_ref[pl.ds(hh, 1), :] = nn
            else:
                nk_ref[pl.ds(hh, 1), :] = nn
                one = (lax.broadcasted_iota(jnp.int32, (128 - HD, tm), 0) == 0).astype(f32).astype(bf16)
                k_ref[hh] = jnp.concatenate([yh, one], axis=0).T

    def keep():
        if copy_h:
            h_ref[:BLK, :] = xa[0]
            h_ref[BLK:, :] = xb[0]

    @pl.when(i == 0)
    def _():
        for o in range(3):
            for c in range(per):
                w_copy(o, c).start()
        norm(xa, xb, n_s, 0, tm)
        for o in range(3):
            def step(c, carry):
                w_copy(o, c).wait()
                project(o, c)
                return carry
            lax.fori_loop(0, per, step, 0)
        keep()
        if n > 1:
            norm(xan, xbn, n_next, 0, tm)

    if n > 1:
        @pl.when(i > 0)
        def _():
            n_s[...] = n_next[...]
            for o in range(3):
                for c in range(per):
                    project(o, c)
                    m = o * per + c - 2
                    if 0 <= m < 8:
                        norm(xan, xbn, n_next, m * (tm // 8), tm // 8)
            keep()


def qkv(me, xa, xa_map, xb, xb_map, g, s, wt, b, layer, n, out_block, copy_h, into=None, after=None):
    tm = 2 * BLK
    last = n - 1
    piece = lambda f, d: pl.BlockSpec((1, BLK, D), lambda i, m: (f(jnp.minimum(i + d, last), m), 0, 0))
    col = lambda r: pl.BlockSpec((r, tm), lambda i, m: (0, out_block(i)))
    sd = jax.ShapeDtypeStruct
    shapes = [sd((D, T), bf16), sd((HEADS, T, 128), bf16), sd((D, T), bf16), sd((HEADS, T), f32), sd((HEADS, T), f32)]
    specs = [col(D), pl.BlockSpec((HEADS, tm, 128), lambda i, m: (0, out_block(i), 0)), col(D), col(HEADS), col(HEADS)]
    if copy_h:
        shapes.append(sd((T, D), bf16))
        specs.append(pl.BlockSpec((tm, D), lambda i, m: (out_block(i), 0)))
    extra = list(into or ()) + ([after] if after is not None else [])
    return pl.pallas_call(
        functools.partial(qkv_kernel, layer=layer, n=n, copy_h=copy_h, alias=len(extra)),
        out_shape=tuple(shapes),
        grid_spec=pltpu.PrefetchScalarGridSpec(
            num_scalar_prefetch=1, grid=(n,),
            in_specs=[piece(xa_map, 0), piece(xb_map, 0), piece(xa_map, 1), piece(xb_map, 1), row(D), row(D), HBM,
                      pl.BlockSpec((3 * D, 128), lambda *_: (0, 0))] + [HBM] * len(extra),
            out_specs=tuple(specs),
            scratch_shapes=[pltpu.VMEM((3 * D, D), bf16), pltpu.VMEM((tm, D), bf16), pltpu.VMEM((tm, D), bf16),
                            pltpu.SemaphoreType.DMA((12,))]),
        input_output_aliases={9 + a: a for a in range(len(into or ()))},
        compiler_params=pltpu.CompilerParams(vmem_limit_bytes=VMEM_MAX, dimension_semantics=("arbitrary",)),
        cost_estimate=pl.CostEstimate(flops=2 * n * tm * D * 3 * D, bytes_accessed=3 * D * D * 2 + n * tm * D * 10, transcendentals=0),
        name="qkv",
    )(me, xa, xb, xa, xb, g, s, wt, b, *extra)


def attn_kernel(q_ref, k_ref, v_ref, nq_ref, nk_ref, o_ref, *, hp, nq, kb, lag):
    nk = SEQ // kb
    units = [(h, q, k) for h in range(hp) for q in range(SEQ // nq) for k in range(nk)]
    st, lows, acc, rhs = {}, [], {}, {}

    def rows(h):
        return slice(h * HD, (h + 1) * HD)

    def shift_rows(h, q):
        kmax = jnp.max(nk_ref[0, h:h + 1, :], axis=1, keepdims=True)
        m = jnp.sqrt(nq_ref[0, h:h + 1, q * nq:(q + 1) * nq] * kmax) * (-1.0 - 2.0 ** -7)
        first = lax.broadcasted_iota(jnp.int32, (128 - HD, nq), 0) == 0
        return jnp.where(first, jnp.broadcast_to(m, (128 - HD, nq)), 0.0).astype(bf16)

    def score(u):
        h, q, k = u
        if k == 0:
            rhs[h, q] = jnp.concatenate([q_ref[rows(h), q * nq:(q + 1) * nq], shift_rows(h, q)], axis=0)
        st[u] = dot(k_ref[h, k * kb:(k + 1) * kb, :], rhs[h, q])

    def mix(u):
        h, q, k = u
        p = jnp.exp2(st.pop(u) * C)
        ls = jnp.sum(p.reshape(kb // 8, 8, nq), axis=0)
        pv = dot(v_ref[rows(h), k * kb:(k + 1) * kb], p.astype(bf16))
        if k:
            a, b = acc[h, q]
            ls, pv = a + ls, b + pv
        acc[h, q] = (ls, pv)
        if k == nk - 1:
            a, b = acc.pop((h, q))
            l = jnp.sum(a, axis=0, keepdims=True)
            lows.append(l)
            o_ref[rows(h), q * nq:(q + 1) * nq] = (b * (1.0 / l)).astype(bf16)

    for i in range(len(units) + lag):
        if i < len(units):
            score(units[i])
        if i >= lag:
            mix(units[i - lag])
    low = lows[0]
    for l in lows[1:]:
        low = jnp.minimum(low, l)
    low = jnp.min(low)

    @pl.when(jnp.logical_not(low >= LOW))
    def _():
        qb = 256
        def body(j, c):
            h = lax.div(j, SEQ // qb)
            qs = pl.ds(pl.multiple_of(lax.rem(j, SEQ // qb) * qb, qb), qb)
            r = pl.ds(pl.multiple_of(h * HD, 32), HD)
            s = dot(k_ref[h, :, :HD], q_ref[r, qs])
            m = jnp.max(s, axis=0, keepdims=True)
            p = jnp.exp2((s - m) * C)
            l = jnp.sum(p, axis=0, keepdims=True)
            o_ref[r, qs] = (dot(v_ref[r, :], p.astype(bf16)) / l).astype(bf16)
            return c
        lax.fori_loop(0, hp * (SEQ // qb), body, 0)


def attn(q, k, v, nq2, nk2, first, count, hp=8, nq=512, kb=256, lag=3):
    blk = pl.BlockSpec((hp * HD, SEQ), lambda i, j: (j, first + i))
    nrm = pl.BlockSpec((1, hp, SEQ), lambda i, j: (j, 0, first + i))
    split = lambda a: a.reshape(HEADS // hp, hp, T)
    return pl.pallas_call(
        functools.partial(attn_kernel, hp=hp, nq=nq, kb=kb, lag=lag),
        out_shape=jax.ShapeDtypeStruct((D, count * SEQ), bf16),
        grid=(count, HEADS // hp),
        in_specs=[blk, pl.BlockSpec((hp, SEQ, 128), lambda i, j: (j, first + i, 0)), blk, nrm, nrm],
        out_specs=pl.BlockSpec((hp * HD, SEQ), lambda i, j: (j, i)),
        compiler_params=pltpu.CompilerParams(vmem_limit_bytes=VMEM_MAX, dimension_semantics=("arbitrary", "arbitrary")),
        cost_estimate=pl.CostEstimate(flops=4 * count * SEQ * SEQ * D, bytes_accessed=count * SEQ * D * 9, transcendentals=count * SEQ * SEQ * HEADS),
        name="attn",
    )(q, k, v, split(nq2), split(nk2))


def gelu(u):
    c = 0.7978845608028654
    return (0.5 * u) * (1.0 + jnp.tanh(u * (c + (c * 0.044715) * (u * u))))


def mlp_kernel(*refs, layer, base, n, fc, nc, alias, send):
    (x_hbm, o_hbm, wo_hbm, bo_ref, g_ref, s_ref, wu_hbm, bu_ref, wd_hbm, bd_ref), refs = refs[:10], refs[10:]
    refs = refs[alias:]
    out_ref, refs = refs[0], refs[1:]
    (xb, ob, wo, wu, wd, m_s, n_s, act, acc, xsem, osem, wsem), refs = refs[:12], refs[12:]
    i = pl.program_id(0)
    tm = BLK
    nj = F // fc
    gain, shift, bo = g_ref[...], s_ref[...], bo_ref[...]

    def block(g):
        if not send:
            return g
        p, m = g // IMAGES, g % IMAGES
        return m * 4 + jnp.where(p < 2, p + 2, 3 - p)

    def x_copy(g):
        slot = g % 2
        return pltpu.make_async_copy(x_hbm.at[pl.ds((base + block(g)) * tm, tm)], xb.at[slot], xsem.at[slot])

    def o_copy(g):
        slot = g % 2
        return pltpu.make_async_copy(o_hbm.at[:, pl.ds(pl.multiple_of(block(g) * tm, tm), tm)], ob.at[slot], osem.at[slot])

    wo_copy = pltpu.make_async_copy(wo_hbm.at[layer], wo, wsem.at[0])

    def wu_copy(j):
        cols = pl.ds(pl.multiple_of(j * fc, fc), fc)
        return pltpu.make_async_copy(wu_hbm.at[layer, :, cols], wu.at[:, cols], wsem.at[1 + j])

    def wd_copy(j):
        r = pl.ds(pl.multiple_of(j * fc, fc), fc)
        return pltpu.make_async_copy(wd_hbm.at[layer, r], wd.at[r], wsem.at[1 + nj + j])

    if send:
        out_v, ssem, rsem = refs
        dp, me = lax.axis_index("dp"), lax.axis_index("sp")
        slots = out_v.shape[0]

        def peer(k):
            return jnp.where(k == 1, me + 1 - 2 * (me % 2), jnp.where(k == 2, lax.rem(me + 2, 4), 3 - me))

        def remote(g):
            p, m = g // IMAGES, g % IMAGES
            k = jnp.where(p < 2, p + 2, 3 - p)
            return pltpu.make_async_remote_copy(
                src_ref=out_v.at[g % slots], dst_ref=out_ref.at[me * IMAGES + m], send_sem=ssem.at[g], recv_sem=rsem.at[g],
                device_id=(dp, peer(k)), device_id_type=MESH)

        def local(g):
            m = g % IMAGES
            return pltpu.make_async_copy(out_v.at[g % slots], out_ref.at[me * IMAGES + m], ssem.at[g])

    def put(cs, v):
        if send:
            out_v[i % slots, :, cs] = v
        else:
            out_ref[:, cs] = v

    def cols(c):
        return slice(c * nc, (c + 1) * nc)

    def project(slot):
        for c in range(D // nc):
            y = dot_tn(ob[slot], wo[:, cols(c)])
            m_s[:, cols(c)] = (xb[slot, :, cols(c)].astype(f32) + (y + bo[:, cols(c)])).astype(bf16)

    def norm():
        def store(r, m, v):
            n_s[r:r + m, :] = v
        ln_rows(lambda r, m: m_s[r:r + m, :], store, gain, shift, 0, tm)

    @pl.when(i == 0)
    def _():
        if send:
            barrier = pltpu.get_barrier_semaphore()
            for k in range(1, 4):
                pl.semaphore_signal(barrier, inc=1, device_id=(dp, peer(k)), device_id_type=MESH)
            pl.semaphore_wait(barrier, 3)
        x_copy(0).start()
        o_copy(0).start()
        wo_copy.start()
        for j in range(nj):
            wu_copy(j).start()
            wd_copy(j).start()
            if j == 0 and n > 1:
                x_copy(1).start()
                o_copy(1).start()
        x_copy(0).wait()
        o_copy(0).wait()
        wo_copy.wait()
        project(0)
        if n > 2:
            x_copy(2).start()
            o_copy(2).start()
        norm()
        acc[...] = m_s[...].astype(f32) + bd_ref[...]

        def chunk(j, carry):
            wu_copy(j).wait()
            for c in range(fc // nc):
                f0 = pl.ds(pl.multiple_of(j * fc + c * nc, nc), nc)
                act[0, :, cols(c)] = gelu(dot(n_s[...], wu[:, f0]) + bu_ref[:, f0]).astype(bf16)
            wd_copy(j).wait()
            for c in range(D // nc):
                acc[:, cols(c)] = acc[:, cols(c)] + dot(act[0], wd[pl.ds(pl.multiple_of(j * fc, fc), fc), cols(c)])
            return carry
        lax.fori_loop(0, nj, chunk, 0)
        for c in range(D // nc):
            put(cols(c), acc[:, cols(c)].astype(bf16))
        if n > 1:
            x_copy(1).wait()
            o_copy(1).wait()
            project(1)
            norm()

    def up(j, c):
        f0 = j * fc + c * nc
        act[j % 2, :, cols(c)] = gelu(dot(n_s[...], wu[:, f0:f0 + nc]) + bu_ref[:, f0:f0 + nc]).astype(bf16)

    def down(j, c):
        y = dot(act[j % 2], wd[j * fc:(j + 1) * fc, cols(c)])
        if j == 0:
            acc[:, cols(c)] = (m_s[:, cols(c)].astype(f32) + bd_ref[:, cols(c)]) + y
        elif j < nj - 1:
            acc[:, cols(c)] = acc[:, cols(c)] + y
        else:
            put(cols(c), (acc[:, cols(c)] + y).astype(bf16))

    if n > 1:
        @pl.when(i > 0)
        def _():
            @pl.when(i + 1 < n)
            def _():
                x_copy(i + 1).wait()
                o_copy(i + 1).wait()

            @pl.when(i + 2 < n)
            def _():
                x_copy(i + 2).start()
                o_copy(i + 2).start()

            if send:
                @pl.when(i - 1 < 3 * IMAGES)
                def _():
                    remote(i - 1).start()

                @pl.when(i - 1 >= 3 * IMAGES)
                def _():
                    local(i - 1).start()

                @pl.when(i >= slots)
                def _():
                    remote(i - slots).wait_send()

            for c in range(fc // nc):
                up(0, c)
            for j in range(1, nj):
                for c in range(max(fc, D) // nc):
                    if c < fc // nc:
                        up(j, c)
                    if c < D // nc:
                        down(j - 1, c)
            project((i + 1) % 2)
            for c in range(D // nc):
                down(nj - 1, c)
            norm()

            if send:
                @pl.when(i == n - 1)
                def _():
                    local(n - 1).start()
                    for g in range(n - slots, 3 * IMAGES):
                        remote(g).wait_send()
                    for g in range(3 * IMAGES, n):
                        local(g).wait()
                    for g in range(3 * IMAGES):
                        remote(g).wait_recv()


def mlp(x, o, wo, bo, g, s, wu, bu, wd, bd, layer, first, count, into=None, send=False, fc=1536, nc=512):
    n = count * SEQ // BLK
    base = first * SEQ // BLK
    nj = F // fc
    dma = pltpu.SemaphoreType.DMA
    vm = pltpu.VMEM
    scratch = [vm((2, BLK, D), bf16), vm((2, D, BLK), bf16), vm((D, D), bf16), vm((D, F), bf16), vm((F, D), bf16), vm((BLK, D), bf16),
               vm((BLK, D), bf16), vm((2, BLK, fc), bf16), vm((BLK, D), f32), dma((2,)), dma((2,)), dma((1 + 2 * nj,))]
    params = dict(vmem_limit_bytes=VMEM_MAX, dimension_semantics=("arbitrary",))
    if send:
        scratch += [vm((8, BLK, D), bf16), dma((n,)), dma((3 * IMAGES,))]
        out_shape, out_spec = jax.ShapeDtypeStruct((4 * IMAGES, BLK, D), bf16), HBM
        params.update(collective_id=0, has_side_effects=True)
    else:
        out_shape, out_spec = jax.ShapeDtypeStruct((T, D), bf16), pl.BlockSpec((BLK, D), lambda i: (base + i, 0))
    extra = [] if into is None else [into]
    tok = n * BLK
    return pl.pallas_call(
        functools.partial(mlp_kernel, layer=layer, base=base, n=n, fc=fc, nc=nc, alias=len(extra), send=send),
        out_shape=out_shape,
        grid=(n,),
        in_specs=[HBM, HBM, HBM, row(D), row(D), row(D), HBM, row(F), HBM, row(D)] + [HBM] * len(extra),
        out_specs=out_spec,
        scratch_shapes=scratch,
        input_output_aliases={10: 0} if extra else {},
        compiler_params=pltpu.CompilerParams(**params),
        cost_estimate=pl.CostEstimate(flops=2 * tok * D * (2 * F + D), bytes_accessed=(2 * F + D) * D * 2 + tok * D * 6, transcendentals=tok * F),
        name="mlp",
    )(x, o, wo, bo, g, s, wu, bu, wd, bd, *extra)

def solution(mesh):
    token_spec = P('dp', 'sp', None)

    def device_step(image_tokens, ln1_gain, ln1_shift, w_qkv, b_qkv, w_out, b_out, ln2_gain, ln2_shift, w_up, b_up, w_down, b_down):
        layers = w_qkv.shape[0]
        w_t = w_qkv.transpose(0, 2, 3, 4, 1).reshape(layers, 3 * D, D)
        b_t = jnp.broadcast_to(b_qkv.reshape(layers, 3 * D, 1), (layers, 3 * D, 128))
        w_o = w_out.reshape(layers, D, D)
        me = lax.axis_index('sp')
        me1 = me.reshape(1).astype(jnp.int32)

        def exchange(k, first, count):
            part = lax.dynamic_slice_in_dim(image_tokens, (me ^ k) * IMAGES + first, count)
            return lax.ppermute(part, 'sp', [(s, s ^ k) for s in range(4)])

        near = exchange(1, 0, IMAGES)
        far_a, far_b = exchange(2, 0, 1), exchange(3, 0, 1)
        rest_a, rest_b = exchange(2, 1, IMAGES - 1), exchange(3, 1, IMAGES - 1)

        def args(l):
            r = lambda a: a[l].reshape(1, -1)
            pre = (r(ln1_gain), r(ln1_shift), w_t, b_t[l], l)
            post = (w_o, r(b_out), r(ln2_gain), r(ln2_shift), w_up, r(b_up), w_down, r(b_down), l)
            return pre, post

        pre, post = args(0)
        here = lambda i, m: i
        bufs = qkv(me1, image_tokens, lambda i, m: m[0] * IMAGES + i, near, here, *pre, IMAGES, lambda i: 2 * i, True)
        bufs = qkv(me1, far_a, here, far_b, here, *pre, 1, lambda i: 1, True, into=bufs)
        o = attn(*bufs[:5], 0, 1)
        h = mlp(bufs[5], o, *post, 0, 1)
        bufs = qkv(me1, rest_a, here, rest_b, here, *pre, IMAGES - 1, lambda i: 2 * i + 3, True, into=bufs, after=h)
        o = attn(*bufs[:5], 1, IMAGES - 1)
        h = mlp(bufs[5], o, *post, 1, IMAGES - 1, into=h)
        for l in range(1, layers):
            pre, post = args(l)
            x = h.reshape(4 * IMAGES, BLK, D)
            bufs = qkv(me1, x, lambda i, m: 2 * i, x, lambda i, m: 2 * i + 1, *pre, 2 * IMAGES, lambda i: i, False)
            o = attn(*bufs[:5], 0, IMAGES)
            h = mlp(h, o, *post, 0, IMAGES, send=l == layers - 1)
        return h

    return jax.shard_map(device_step, mesh=mesh, in_specs=(token_spec,) + (P(),) * 12, out_specs=token_spec, check_vma=False)
```

time: 1500 us -> 787 us (0.52)
  matrix products: 958 us -> 0 us
  Pallas kernels: 0 us -> 737 us
  other arithmetic: 208 us -> 0 us
  blocking collectives: 141 us -> 0 us
  waiting for transfers between devices: 135 us -> 0.01 us
    dot_general x12 -> x0, matrix products: 958 us -> none  [the longest x2 212 us: mlp_block(): jnp.einsum('bsd,df->bsf', normed, w_up, preferred_element_type=jnp.float32)]
    pallas_call x0 -> x10, Pallas kernels: none -> 737 us  [the longest x3 438 us: mlp(): pl.pallas_call(functools.partial(mlp_kernel, layer=layer, base=base, n=n,...]
    reduce_sum x7 -> x0, other arithmetic: 192 us -> none  [the longest x2 161 us: attend(): row_total = jnp.sum(prob_vals, axis=-1, keepdims=True)]
    all_to_all x1 -> x0, blocking collectives: 141 us -> none  [device_step(): return lax.all_to_all(hidden, 'sp', 1, 0, tiled=True)]
    all_to_all x1 -> x0, waiting for transfers between devices: 135 us -> none  [device_step(): hidden = lax.all_to_all(image_tokens, 'sp', 0, 1, tiled=True)]
    convert_element_type x2 -> x0, local copies, waits for them, and re-layouts: 29.5 us -> none  [the longest x1 14.9 us: device_step(): mid_state = (hidden.astype(jnp.float32) + attn_proj).astype(jnp.bfloat16)]
    convert_element_type x2 -> x0, other arithmetic: 16.1 us -> none  [the longest x1 8.56 us: layer_norm(): (centred * lax.rsqrt(var_val + LN_EPS) * ln_gain + ln_shift).astype(jnp.b...]
  transfers between devices with their start and end apart: 1 -> 5, of which waited for: 1 -> 0; matrix products, arithmetic and copies ran while one was open for 0% -> 2% of each run, Pallas kernels for 0% -> 19%
where the time goes in v3:
time: 787 us; the launch traced here: 773 us
  Pallas kernels  737 us (94%)
  local copies, waits for them, and re-layouts  30 us (4%)
    pallas_call x3, Pallas kernels, mlp(): pl.pallas_call(functools.partial(mlp_kernel, layer=layer, base=base, n=n,...  438 us
    pallas_call x4, Pallas kernels, qkv(): pl.pallas_call(functools.partial(qkv_kernel, layer=layer, n=n, copy_h=cop...  177 us
    pallas_call x3, Pallas kernels, attn(): pl.pallas_call(functools.partial(attn_kernel, hp=hp, nq=nq, kb=kb, lag=la...  122 us
  transfers between devices with their start and end apart: 5, of which 0 were waited for; matrix products, arithmetic and copies ran while one was open for 2% of the time, Pallas kernels for 19%

profile of v3, /device:TPU:0, one launch (start us, length us, event | category | flops | bytes accessed | tf_op | source)
XLA Modules:
  0.0 772.8 jit_solution(15928168549496766081)
XLA Ops:
  0.0 0.0 copy-start
  0.0 0.0 copy-start.3
  0.0 0.0 copy-start.2
  0.0 0.0 copy-start.5
  0.0 0.0 copy-start.4
  0.0 0.0 copy-start.7
  0.0 0.0 copy-start.6
  0.0 0.0 copy-start.1
  0.1 2.7 constant_dynamic-slice_fusion.1
  2.8 3.3 collective-permute-start.2
  6.1 0.0 collective-permute-start.3
  6.1 2.1 constant_dynamic-slice_fusion
  8.2 0.1 collective-permute-start.4
  8.3 5.1 constant_dynamic-slice_fusion.3
  13.4 2.0 collective-permute-start
  15.4 0.0 collective-permute-start.1
  15.4 0.0 copy-done
  15.4 0.1 broadcast_in_dim.11
  15.5 0.7 broadcast_in_dim.13
  16.2 0.0 copy-done.3
  16.2 0.0 copy-done.2
  16.2 0.6 fusion.6
  16.8 0.0 copy-done.5
  16.8 0.0 copy-done.4
  16.8 0.6 fusion.2
  17.4 0.0 copy-done.7
  17.4 0.0 copy-done.6
  17.4 0.6 fusion.4
  18.1 0.0 copy-done.1
  18.1 0.7 fusion
  18.7 0.0 collective-permute-done.4.refs_2_.refs_4_
  18.7 3.0 broadcast_in_dim.12.refs_8_
  21.7 45.0 %qkv.4 = (bf16[1536,4096]{1,0:T(8,128)(2,1)}, bf16[16,4096,128]{2,1,0:T(8,128)(2,1)}, bf16[1536,4096]{1,0:T(8,128)(2,1)}, f32[16,4096]{1,0:T(8,128)}, f32[16,4096]{1,0:T(8,128)}, /*index=5*/bf16[4096,1536]{1,0:T(8,128)(2,1)}) custom-call(s32[1]{0:T(128)} %bitcast.refs_0_, bf16[16,256,1536]{2,1,0:T(8,128)(2,1)} %refs_3_.1, ...), custom_call_target="tpu_custom_call" | custom-call | flops 28991029248 | bytes 45613056 | tf_op jit(solution)/shard_map/qkv/pallas_call | solution.py:152
  66.7 0.0 collective-permute-done.2.refs_1_.refs_3_
  66.7 0.0 collective-permute-done.3.refs_2_.refs_4_
  66.7 16.8 %qkv.5 = (bf16[1536,4096]{1,0:T(8,128)(2,1)}, bf16[16,4096,128]{2,1,0:T(8,128)(2,1)}, bf16[1536,4096]{1,0:T(8,128)(2,1)}, f32[16,4096]{1,0:T(8,128)}, f32[16,4096]{1,0:T(8,128)}, /*index=5*/bf16[4096,1536]{1,0:T(8,128)(2,1)}) custom-call(s32[1]{0:T(128)} %bitcast.refs_0_, ...), custom_call_target="tpu_custom_call", output_to_operand_aliasing={{0}: (9, {}), {1}: (10, {}), {2}: (11, {}), {3}: (12, {}), ... | custom-call | flops 7247757312 | bytes 22020096 | tf_op jit(solution)/shard_map/qkv/pallas_call | solution.py:152
  83.5 17.5 %attn.3.refs_1_ = bf16[1536,1024]{1,0:T(8,128)(2,1)} custom-call(bf16[1536,4096]{1,0:T(8,128)(2,1)} %get-tuple-element.34.q_ref.refs_9_, bf16[16,4096,128]{2,1,0:T(8,128)(2,1)} %get-tuple-element.35.k_ref.refs_10_, bf16[1536,4096]{1,0:T(8,128)(2,1)} %get-tuple-element.36.v_ref.refs_11_, f32[2,8,4096]{2,1,0:T(8,128)} %bitcast.24, f32[2,8,4096]{2,1,0:T(8,128)} %bitcast.26), custom_call_target="tpu_custom_call" | custom-call | flops 6442450944 | bytes 14155776 | tf_op jit(solution)/shard_map/attn/pallas_call | solution.py:234
  101.0 65.3 %mlp.3.refs_15_.refs_10_ = bf16[4096,1536]{1,0:T(8,128)(2,1)} custom-call(bf16[4096,1536]{1,0:T(8,128)(2,1)} %get-tuple-element.39.refs_0_.refs_14_, bf16[1536,1024]{1,0:T(8,128)(2,1)} %attn.3.refs_1_, bf16[2,1536,1536]{2,1,0:T(8,128)(2,1)} %bitcast.28, f32[1,1536]{1,0:T(1,128)} %get-tuple-element.75.refs_3_, f32[1,1536]{1,0:T(1,128)} %get-tuple-element.64.refs_4_, ...), custom_call_target="tpu_custom_call" | custom-call | flops 43486543872 | bytes 51904512 | tf_op jit(solution)/shard_map/mlp/pallas_call | solution.py:448
  166.4 0.0 collective-permute-done.refs_1_.refs_3_
  166.4 0.0 collective-permute-done.1.refs_2_.refs_4_
  166.4 36.3 %qkv.6 = (bf16[1536,4096]{1,0:T(8,128)(2,1)}, bf16[16,4096,128]{2,1,0:T(8,128)(2,1)}, bf16[1536,4096]{1,0:T(8,128)(2,1)}, f32[16,4096]{1,0:T(8,128)}, f32[16,4096]{1,0:T(8,128)}, /*index=5*/bf16[4096,1536]{1,0:T(8,128)(2,1)}) custom-call(s32[1]{0:T(128)} %bitcast.refs_0_, ...), custom_call_target="tpu_custom_call", output_to_operand_aliasing={{0}: (9, {}), {1}: (10, {}), {2}: (11, {}), {3}: (12, {}), ... | custom-call | flops 21743271936 | bytes 37748736 | tf_op jit(solution)/shard_map/qkv/pallas_call | solution.py:152
  202.7 45.5 %attn.4.refs_1_ = bf16[1536,3072]{1,0:T(8,128)(2,1)} custom-call(bf16[1536,4096]{1,0:T(8,128)(2,1)} %get-tuple-element.41.q_ref, bf16[16,4096,128]{2,1,0:T(8,128)(2,1)} %get-tuple-element.42.k_ref, bf16[1536,4096]{1,0:T(8,128)(2,1)} %get-tuple-element.43.v_ref, f32[2,8,4096]{2,1,0:T(8,128)} %bitcast.25, f32[2,8,4096]{2,1,0:T(8,128)} %bitcast.27), custom_call_target="tpu_custom_call" | custom-call | flops 19327352832 | bytes 42467328 | tf_op jit(solution)/shard_map/attn/pallas_call | solution.py:234
  248.2 161.1 %mlp.4.refs_0_ = bf16[4096,1536]{1,0:T(8,128)(2,1)} custom-call(bf16[4096,1536]{1,0:T(8,128)(2,1)} %get-tuple-element.40.refs_0_, bf16[1536,3072]{1,0:T(8,128)(2,1)} %attn.4.refs_1_, bf16[2,1536,1536]{2,1,0:T(8,128)(2,1)} %bitcast.29, f32[1,1536]{1,0:T(1,128)} %get-tuple-element.75.refs_3_, ...), custom_call_target="tpu_custom_call", output_to_operand_aliasing={{}: (10, {})} | custom-call | flops 130459631616 | bytes 70778880 | tf_op jit(solution)/shard_map/mlp/pallas_call | solution.py:448
  409.3 3.4 broadcast_in_dim.14.refs_8_
  412.7 78.6 %qkv.7 = (bf16[1536,4096]{1,0:T(8,128)(2,1)}, bf16[16,4096,128]{2,1,0:T(8,128)(2,1)}, bf16[1536,4096]{1,0:T(8,128)(2,1)}, f32[16,4096]{1,0:T(8,128)}, f32[16,4096]{1,0:T(8,128)}) custom-call(s32[1]{0:T(128)} %bitcast.refs_0_, bf16[16,256,1536]{2,1,0:T(8,128)(2,1)} %bitcast.20, bf16[16,256,1536]{2,1,0:T(8,128)(2,1)} %bitcast.21, ...), custom_call_target="tpu_custom_call" | custom-call | flops 57982058496 | bytes 77070336 | tf_op jit(solution)/shard_map/qkv/pallas_call | solution.py:152
  491.2 59.3 %attn.5.refs_1_ = bf16[1536,4096]{1,0:T(8,128)(2,1)} custom-call(bf16[1536,4096]{1,0:T(8,128)(2,1)} %get-tuple-element.46.q_ref, bf16[16,4096,128]{2,1,0:T(8,128)(2,1)} %get-tuple-element.47.k_ref, bf16[1536,4096]{1,0:T(8,128)(2,1)} %get-tuple-element.48.v_ref, f32[2,8,4096]{2,1,0:T(8,128)} %bitcast.31, f32[2,8,4096]{2,1,0:T(8,128)} %bitcast.32), custom_call_target="tpu_custom_call" | custom-call | flops 25769803776 | bytes 56623104 | tf_op jit(solution)/shard_map/attn/pallas_call | solution.py:234
  550.6 211.4 %mlp.5 = bf16[16,256,1536]{2,1,0:T(8,128)(2,1)} custom-call(bf16[4096,1536]{1,0:T(8,128)(2,1)} %mlp.4.refs_0_, bf16[1536,4096]{1,0:T(8,128)(2,1)} %attn.5.refs_1_, bf16[2,1536,1536]{2,1,0:T(8,128)(2,1)} %bitcast.30, f32[1,1536]{1,0:T(1,128)} %get-tuple-element.76.refs_3_, f32[1,1536]{1,0:T(1,128)} %get-tuple-element.63.refs_4_, ...), custom_call_target="tpu_custom_call" | custom-call | flops 173946175488 | bytes 80216064 | tf_op jit(solution)/shard_map/mlp/pallas_call | solution.py:448
  761.9 10.5 %copy.41 = bf16[16,256,1536]{2,1,0:T(8,128)(2,1)} copy(bf16[16,256,1536]{2,1,0:T(8,128)(2,1)} %mlp.5) | data formatting | bytes 25165824
  (1 shorter events, 0.0 us)
Async XLA Ops:
  0.0 15.4 %copy-start = (f32[2,3,16,96]{3,2,1,0:T(8,128)S(1)}, f32[2,3,16,96]{3,2,1,0:T(8,128)}, u32[]{:S(2)}) copy-start(f32[2,3,16,96]{3,2,1,0:T(8,128)} %param.17) | copy-start | bytes 110596
  0.0 16.2 %copy-start.3 = (f32[2,1536]{1,0:T(2,128)S(1)}, f32[2,1536]{1,0:T(2,128)}, u32[]{:S(2)}) copy-start(f32[2,1536]{1,0:T(2,128)} %param.14) | copy-start | bytes 36868
  0.0 16.2 %copy-start.2 = (f32[2,1536]{1,0:T(2,128)S(1)}, f32[2,1536]{1,0:T(2,128)}, u32[]{:S(2)}) copy-start(f32[2,1536]{1,0:T(2,128)} %param.15) | copy-start | bytes 36868
  0.0 16.8 %copy-start.5 = (f32[2,1536]{1,0:T(2,128)S(1)}, f32[2,1536]{1,0:T(2,128)}, u32[]{:S(2)}) copy-start(f32[2,1536]{1,0:T(2,128)} %param.21) | copy-start | bytes 36868
  0.0 16.8 %copy-start.4 = (f32[2,1536]{1,0:T(2,128)S(1)}, f32[2,1536]{1,0:T(2,128)}, u32[]{:S(2)}) copy-start(f32[2,1536]{1,0:T(2,128)} %param.25) | copy-start | bytes 36868
  0.0 17.4 %copy-start.7 = (f32[2,1536]{1,0:T(2,128)S(1)}, f32[2,1536]{1,0:T(2,128)}, u32[]{:S(2)}) copy-start(f32[2,1536]{1,0:T(2,128)} %param.19) | copy-start | bytes 36868
  0.0 17.4 %copy-start.6 = (f32[2,1536]{1,0:T(2,128)S(1)}, f32[2,1536]{1,0:T(2,128)}, u32[]{:S(2)}) copy-start(f32[2,1536]{1,0:T(2,128)} %param.20) | copy-start | bytes 36868
  0.0 18.0 %copy-start.1 = (f32[2,6144]{1,0:T(2,128)S(1)}, f32[2,6144]{1,0:T(2,128)}, u32[]{:S(2)}) copy-start(f32[2,6144]{1,0:T(2,128)} %param.23) | copy-start | bytes 147460
  2.8 63.9 %collective-permute-start.2 = (bf16[1,256,1536]{2,1,0:T(8,128)(2,1)}, bf16[1,256,1536]{2,1,0:T(8,128)(2,1)}, u32[]{:S(2)}, u32[]{:S(2)}) collective-permute-start(bf16[1,256,1536]{2,1,0:T(8,128)(2,1)} %get-tuple-element.52), channel_id=1, source_target_pairs={{0,2},{1,3},{2,0},{3,1},{4,6},{5,7},{6,4},{7,5}} | collective-permute-start | bytes 2359304 | tf_op jit(solution)/shard_map/ppermute | solution.py:474
  6.1 60.6 %collective-permute-start.3 = (bf16[1,256,1536]{2,1,0:T(8,128)(2,1)}, bf16[1,256,1536]{2,1,0:T(8,128)(2,1)}, u32[]{:S(2)}, u32[]{:S(2)}) collective-permute-start(bf16[1,256,1536]{2,1,0:T(8,128)(2,1)} %get-tuple-element.51), channel_id=1, source_target_pairs={{0,3},{1,2},{2,1},{3,0},{4,7},{5,6},{6,5},{7,4}} | collective-permute-start | bytes 2359304 | tf_op jit(solution)/shard_map/ppermute | solution.py:474
  8.2 10.5 %collective-permute-start.4 = (bf16[4,256,1536]{2,1,0:T(8,128)(2,1)S(1)}, bf16[4,256,1536]{2,1,0:T(8,128)(2,1)}, u32[]{:S(2)}, u32[]{:S(2)}) collective-permute-start(bf16[4,256,1536]{2,1,0:T(8,128)(2,1)S(1)} %constant_dynamic-slice_fusion), channel_id=1, source_target_pairs={{0,1},{1,0},{2,3},{3,2},{4,5},{5,4},{6,7},{7,6}} | collective-permute-start | bytes 9437192 | tf_op jit(solution)/shard_map/ppermute | solution.py:474
  13.4 153.0 %collective-permute-start = (bf16[3,256,1536]{2,1,0:T(8,128)(2,1)}, bf16[3,256,1536]{2,1,0:T(8,128)(2,1)}, u32[]{:S(2)}, u32[]{:S(2)}) collective-permute-start(bf16[3,256,1536]{2,1,0:T(8,128)(2,1)} %get-tuple-element.54), channel_id=1, source_target_pairs={{0,2},{1,3},{2,0},{3,1},{4,6},{5,7},{6,4},{7,5}} | collective-permute-start | bytes 7077896 | tf_op jit(solution)/shard_map/ppermute | solution.py:474
  15.4 151.0 %collective-permute-start.1 = (bf16[3,256,1536]{2,1,0:T(8,128)(2,1)}, bf16[3,256,1536]{2,1,0:T(8,128)(2,1)}, u32[]{:S(2)}, u32[]{:S(2)}) collective-permute-start(bf16[3,256,1536]{2,1,0:T(8,128)(2,1)} %get-tuple-element.53), channel_id=1, source_target_pairs={{0,3},{1,2},{2,1},{3,0},{4,7},{5,6},{6,5},{7,4}} | collective-permute-start | bytes 7077896 | tf_op jit(solution)/shard_map/ppermute | solution.py:474

commit v4 on v3

v4 whole, which is shorter than its diff:
```python
import functools

import jax
import jax.numpy as jnp
from jax import lax
from jax.experimental import pallas as pl
from jax.experimental.pallas import tpu as pltpu
from jax.sharding import PartitionSpec as P

LN_EPS = 1e-6
HD = 96
HEADS = 16
D = HD * HEADS
F = 4 * D
IMAGES = 4
BLK = 256
SEQ = 4 * BLK
T = IMAGES * SEQ
CH = 4 * HD
C = HD ** -0.5 * 1.4426950408889634
LOW = 2.0 ** -80
f32, bf16 = jnp.float32, jnp.bfloat16
MESH = pl.DeviceIdType.MESH
HBM = pl.BlockSpec(memory_space=pltpu.HBM)


def dot(a, b):
    return jnp.dot(a, b, preferred_element_type=f32)


def dot_nt(a, b):
    return lax.dot_general(a, b, (((1,), (1,)), ((), ())), preferred_element_type=f32)


def dot_tn(a, b):
    return lax.dot_general(a, b, (((0,), (0,)), ((), ())), preferred_element_type=f32)


VMEM = pl.BlockSpec(memory_space=pltpu.VMEM)
ATTN_LIMIT = 17 << 20
MLP_LIMIT = 15 << 20


def at_hbm(*arrays):
    return tuple(pltpu.with_memory_space_constraint(a, pltpu.HBM) for a in arrays)


def at_vmem(*arrays):
    return tuple(pltpu.with_memory_space_constraint(a, pltpu.VMEM) for a in arrays)


def whole(shape):
    return pl.BlockSpec(shape, lambda *_: (0,) * len(shape))


def ln_rows(load, store, gain, shift, start, rows, step=16):
    for r in range(start, start + rows, step):
        v = load(r, step).astype(f32)
        mu = jnp.sum(v, axis=-1, keepdims=True) * (1.0 / D)
        c = v - mu
        var = jnp.sum(c * c, axis=-1, keepdims=True) * (1.0 / D)
        store(r, step, (c * lax.rsqrt(var + LN_EPS) * gain + shift).astype(bf16))


def start_kernel(par, a_ref, b_ref, bias_ref, w_hbm, sa_ref, sb_ref, w_out, b0_out, b1_out, sem):
    i = pl.program_id(0)
    w_copy = pltpu.make_async_copy(w_hbm.at[0], w_out, sem)

    @pl.when(i == 0)
    def _():
        w_copy.start()
        for l, out in ((0, b0_out), (1, b1_out)):
            for t in range(3):
                cols = bias_ref[l, t].T
                for h in range(HEADS):
                    r = (t * HEADS + h) * HD
                    out[r:r + HD, :] = jnp.broadcast_to(cols[:, h:h + 1], (HD, 128))

    sa_ref[...] = a_ref[...]
    sb_ref[...] = b_ref[...]

    @pl.when(i == pl.num_programs(0) - 1)
    def _():
        w_copy.wait()


def start(par, tokens, w_t, b_qkv):
    sd = jax.ShapeDtypeStruct
    piece = lambda k: pl.BlockSpec((1, BLK, D), lambda i, p: ((p[0] ^ k) * IMAGES + 1 + i, 0, 0))
    out = pl.BlockSpec((1, BLK, D), lambda i, p: (i, 0, 0))
    part = sd((IMAGES - 1, BLK, D), bf16)
    bias = sd((3 * D, 128), f32)
    return pl.pallas_call(
        start_kernel,
        out_shape=(part, part, pltpu.VMEM((3 * D, D), bf16), bias, bias),
        grid_spec=pltpu.PrefetchScalarGridSpec(
            num_scalar_prefetch=1, grid=(IMAGES - 1,),
            in_specs=[piece(2), piece(3), whole(b_qkv.shape), HBM],
            out_specs=(out, out, VMEM, whole((3 * D, 128)), whole((3 * D, 128))),
            scratch_shapes=[pltpu.SemaphoreType.DMA(())]),
        compiler_params=pltpu.CompilerParams(vmem_limit_bytes=40 << 20, dimension_semantics=("arbitrary",)),
        cost_estimate=pl.CostEstimate(flops=1 << 30, bytes_accessed=30 << 20, transcendentals=0),
        name="start",
    )(par, *at_hbm(tokens, tokens), b_qkv, w_t)


def qkv_kernel(*refs, layer, n, copy_h, alias, fetch):
    (_, xa, xb, xan, xbn, g_ref, s_ref, w, b_ref), refs = refs[:9], refs[9:]
    refs = refs[alias:]
    (q_ref, k_ref, v_ref, nq_ref, nk_ref), refs = refs[:5], refs[5:]
    if copy_h:
        h_ref, refs = refs[0], refs[1:]
    n_s, n_next = refs[:2]
    if fetch:
        w_hbm, w, w_sem = w, refs[2], refs[3]
        w_copy = pltpu.make_async_copy(w_hbm.at[layer], w, w_sem)
    i = pl.program_id(0)
    tm = 2 * BLK
    per = D // CH
    order = (1, 0, 2)
    gain, shift = g_ref[layer:layer + 1, :], s_ref[layer:layer + 1, :]

    def norm(a, b, start, rows):
        def load(r, m):
            return a[0, r:r + m, :] if r < BLK else b[0, r - BLK:r - BLK + m, :]
        def store(r, m, v):
            n_next[r:r + m, :] = v
        ln_rows(load, store, gain, shift, start, rows)

    def project(o, c):
        t = order[o]
        r0, rw = c * CH, t * D + c * CH
        y = dot_nt(w[rw:rw + CH, :], n_s[...])
        bias = jnp.concatenate([b_ref[rw:rw + CH, :]] * (tm // 128), axis=1)
        yb = (y + bias).astype(bf16)
        if t == 2:
            v_ref[r0:r0 + CH, :] = yb
            return
        if t == 0:
            q_ref[r0:r0 + CH, :] = yb
        for h in range(CH // HD):
            hh = c * (CH // HD) + h
            yh = yb[h * HD:(h + 1) * HD, :]
            yf = yh.astype(f32)
            nn = jnp.sum(yf * yf, axis=0, keepdims=True)
            if t == 0:
                nq_ref[hh:hh + 1, :] = nn
            else:
                nk_ref[hh:hh + 1, :] = nn
                one = (lax.broadcasted_iota(jnp.int32, (128 - HD, tm), 0) == 0).astype(f32).astype(bf16)
                k_ref[hh] = jnp.concatenate([yh, one], axis=0).T

    @pl.when(i == 0)
    def _():
        if fetch:
            w_copy.start()
        norm(xa, xb, 0, tm)
        if fetch:
            w_copy.wait()

    n_s[...] = n_next[...]
    for o in range(3):
        for c in range(per):
            project(o, c)
            m = o * per + c - 2
            if n > 1 and 0 <= m < 8:
                norm(xan, xbn, m * (tm // 8), tm // 8)
    if copy_h:
        h_ref[:BLK, :] = xa[0]
        h_ref[BLK:, :] = xb[0]


def qkv(par, xa, xa_map, xb, xb_map, g, s, w, b, layer, n, out_block, copy_h, into=None, after=None):
    tm = 2 * BLK
    last = n - 1
    piece = lambda f, d: pl.BlockSpec((1, BLK, D), lambda i, m: (f(jnp.minimum(i + d, last), m), 0, 0))
    col = lambda r: pl.BlockSpec((r, tm), lambda i, m: (0, out_block(i)))
    shapes = [pltpu.HBM((D, T), bf16), pltpu.HBM((HEADS, T, 128), bf16), pltpu.HBM((D, T), bf16), pltpu.HBM((HEADS, T), f32), pltpu.HBM((HEADS, T), f32)]
    specs = [col(D), pl.BlockSpec((HEADS, tm, 128), lambda i, m: (0, out_block(i), 0)), col(D), col(HEADS), col(HEADS)]
    if copy_h:
        shapes.append(pltpu.HBM((T, D), bf16))
        specs.append(pl.BlockSpec((tm, D), lambda i, m: (out_block(i), 0)))
    extra = list(into or ()) + ([after] if after is not None else [])
    fetch = w.ndim == 3
    return pl.pallas_call(
        functools.partial(qkv_kernel, layer=layer, n=n, copy_h=copy_h, alias=len(extra), fetch=fetch),
        out_shape=tuple(shapes),
        grid_spec=pltpu.PrefetchScalarGridSpec(
            num_scalar_prefetch=1, grid=(n,),
            in_specs=[piece(xa_map, 0), piece(xb_map, 0), piece(xa_map, 1), piece(xb_map, 1), whole((2, D)), whole((2, D)), HBM if fetch else VMEM,
                      whole((3 * D, 128))] + [HBM] * len(extra),
            out_specs=tuple(specs),
            scratch_shapes=[pltpu.VMEM((tm, D), bf16), pltpu.VMEM((tm, D), bf16)]
            + ([pltpu.VMEM((3 * D, D), bf16), pltpu.SemaphoreType.DMA(())] if fetch else [])),
        input_output_aliases={9 + a: a for a in range(len(into or ()))},
        compiler_params=pltpu.CompilerParams(vmem_limit_bytes=48 << 20, dimension_semantics=("arbitrary",)),
        cost_estimate=pl.CostEstimate(flops=2 * n * tm * D * 3 * D, bytes_accessed=n * tm * D * 10, transcendentals=0),
        name="qkv",
    )(par, *at_hbm(xa, xb, xa, xb), *at_hbm(g, s), *(at_hbm(w) if fetch else at_vmem(w)), *at_hbm(b), *extra)


def attn_kernel(q_ref, k_ref, v_ref, nq_ref, nk_ref, wo_hbm, wu_hbm, wd_hbm, o_ref, wb, sem, *, layer, hp, nq, kb, lag):
    step = pl.program_id(0) * pl.num_programs(1) + pl.program_id(1)
    parts = [wo_hbm.at[layer]] + [wu_hbm.at[layer, :, c * D:(c + 1) * D] for c in range(F // D)] + [wd_hbm.at[layer]]
    copies = [pltpu.make_async_copy(p, wb.at[c * D:(c + 1) * D] if c <= F // D else wb.at[(1 + F // D) * D:], sem.at[c]) for c, p in enumerate(parts)]

    @pl.when(step == 0)
    def _():
        for c in copies:
            c.start()

    @pl.when(step == pl.num_programs(0) * pl.num_programs(1) - 1)
    def _():
        for c in copies:
            c.wait()

    nk = SEQ // kb
    units = [(h, q, k) for h in range(hp) for q in range(SEQ // nq) for k in range(nk)]
    st, lows, acc, rhs = {}, [], {}, {}

    def rows(h):
        return slice(h * HD, (h + 1) * HD)

    def shift_rows(h, q):
        kmax = jnp.max(nk_ref[0, h:h + 1, :], axis=1, keepdims=True)
        m = jnp.sqrt(nq_ref[0, h:h + 1, q * nq:(q + 1) * nq] * kmax) * (-1.0 - 2.0 ** -7)
        first = lax.broadcasted_iota(jnp.int32, (128 - HD, nq), 0) == 0
        return jnp.where(first, jnp.broadcast_to(m, (128 - HD, nq)), 0.0).astype(bf16)

    def score(u):
        h, q, k = u
        if k == 0:
            rhs[h, q] = jnp.concatenate([q_ref[rows(h), q * nq:(q + 1) * nq], shift_rows(h, q)], axis=0)
        st[u] = dot(k_ref[h, k * kb:(k + 1) * kb, :], rhs[h, q])

    def mix(u):
        h, q, k = u
        p = jnp.exp2(st.pop(u) * C)
        ls = jnp.sum(p.reshape(kb // 8, 8, nq), axis=0)
        pv = dot(v_ref[rows(h), k * kb:(k + 1) * kb], p.astype(bf16))
        if k:
            a, b = acc[h, q]
            ls, pv = a + ls, b + pv
        acc[h, q] = (ls, pv)
        if k == nk - 1:
            a, b = acc.pop((h, q))
            l = jnp.sum(a, axis=0, keepdims=True)
            lows.append(l)
            o_ref[rows(h), q * nq:(q + 1) * nq] = (b * (1.0 / l)).astype(bf16)

    for i in range(len(units) + lag):
        if i < len(units):
            score(units[i])
        if i >= lag:
            mix(units[i - lag])
    low = lows[0]
    for l in lows[1:]:
        low = jnp.minimum(low, l)
    low = jnp.min(low)

    @pl.when(jnp.logical_not(low >= LOW))
    def _():
        qb = 256
        def body(j, c):
            h = lax.div(j, SEQ // qb)
            qs = pl.ds(pl.multiple_of(lax.rem(j, SEQ // qb) * qb, qb), qb)
            r = pl.ds(pl.multiple_of(h * HD, 32), HD)
            s = dot(k_ref[h, :, :HD], q_ref[r, qs])
            m = jnp.max(s, axis=0, keepdims=True)
            p = jnp.exp2((s - m) * C)
            l = jnp.sum(p, axis=0, keepdims=True)
            o_ref[r, qs] = (dot(v_ref[r, :], p.astype(bf16)) / l).astype(bf16)
            return c
        lax.fori_loop(0, hp * (SEQ // qb), body, 0)


def attn(q, k, v, nq2, nk2, w_o, w_up, w_down, layer, first, count, hp=4, nq=512, kb=256, lag=3):
    blk = pl.BlockSpec((hp * HD, SEQ), lambda i, j: (j, first + i))
    nrm = pl.BlockSpec((1, hp, SEQ), lambda i, j: (j, 0, first + i))
    split = lambda a: a.reshape(HEADS // hp, hp, T)
    return pl.pallas_call(
        functools.partial(attn_kernel, layer=layer, hp=hp, nq=nq, kb=kb, lag=lag),
        out_shape=(pltpu.HBM((D, count * SEQ), bf16), pltpu.VMEM((D + 2 * F, D), bf16)),
        grid=(count, HEADS // hp),
        in_specs=[blk, pl.BlockSpec((hp, SEQ, 128), lambda i, j: (j, first + i, 0)), blk, nrm, nrm, HBM, HBM, HBM],
        out_specs=(pl.BlockSpec((hp * HD, SEQ), lambda i, j: (j, i)), VMEM),
        scratch_shapes=[pltpu.SemaphoreType.DMA((2 + F // D,))],
        compiler_params=pltpu.CompilerParams(vmem_limit_bytes=(ATTN_LIMIT), dimension_semantics=("arbitrary", "arbitrary")),
        cost_estimate=pl.CostEstimate(flops=4 * count * SEQ * SEQ * D, bytes_accessed=count * SEQ * D * 9, transcendentals=count * SEQ * SEQ * HEADS),
        name="attn",
    )(*at_hbm(q, k, v, split(nq2), split(nk2)), w_o, w_up, w_down)


def gelu(u):
    c = 0.7978845608028654
    return (0.5 * u) * (1.0 + jnp.tanh(u * (c + (c * 0.044715) * (u * u))))


def mlp_kernel(*refs, layer, base, n, fc, nc, alias, send, fetch):
    (x_hbm, o_hbm, wb, bo_ref, g_ref, s_ref, bu_ref, bd_ref), refs = refs[:8], refs[8:]
    if fetch is not None:
        wq_hbm, refs = refs[0], refs[1:]
    refs = refs[alias:]
    out_ref, refs = refs[0], refs[1:]
    if fetch is not None:
        wq, refs = refs[0], refs[1:]
    (xb, ob, m_s, n_s, act, acc, xsem, osem, wsem), refs = refs[:9], refs[9:]
    i = pl.program_id(0)
    tm = BLK
    assert fc == D
    nj = F // fc
    one = slice(layer, layer + 1)
    gain, shift, bo = g_ref[one, :], s_ref[one, :], bo_ref[one, :]

    def block(g):
        if not send:
            return g
        p, m = g // IMAGES, g % IMAGES
        return m * 4 + jnp.where(p < 2, p + 2, 3 - p)

    def x_copy(g):
        slot = g % 2
        return pltpu.make_async_copy(x_hbm.at[pl.ds((base + block(g)) * tm, tm)], xb.at[slot], xsem.at[slot])

    def o_copy(g):
        slot = g % 2
        return pltpu.make_async_copy(o_hbm.at[:, pl.ds(pl.multiple_of(block(g) * tm, tm), tm)], ob.at[slot], osem.at[slot])

    if fetch is not None:
        wq_copy = pltpu.make_async_copy(wq_hbm.at[fetch], wq, wsem)

    if send:
        out_v, ssem, rsem = refs
        dp, me = lax.axis_index("dp"), lax.axis_index("sp")
        slots = out_v.shape[0]

        def peer(k):
            return jnp.where(k == 1, me + 1 - 2 * (me % 2), jnp.where(k == 2, lax.rem(me + 2, 4), 3 - me))

        def remote(g):
            p, m = g // IMAGES, g % IMAGES
            k = jnp.where(p < 2, p + 2, 3 - p)
            return pltpu.make_async_remote_copy(
                src_ref=out_v.at[g % slots], dst_ref=out_ref.at[me * IMAGES + m], send_sem=ssem.at[g], recv_sem=rsem.at[g],
                device_id=(dp, peer(k)), device_id_type=MESH)

        def local(g):
            m = g % IMAGES
            return pltpu.make_async_copy(out_v.at[g % slots], out_ref.at[me * IMAGES + m], ssem.at[g])

    def put(cs, v):
        if send:
            out_v[i % slots, :, cs] = v
        else:
            out_ref[:, cs] = v

    def cols(c):
        return slice(c * nc, (c + 1) * nc)

    def project(slot):
        for c in range(D // nc):
            y = dot_tn(ob[slot], wb[:D, cols(c)])
            m_s[:, cols(c)] = (xb[slot, :, cols(c)].astype(f32) + (y + bo[:, cols(c)])).astype(bf16)

    def norm():
        def store(r, m, v):
            n_s[r:r + m, :] = v
        ln_rows(lambda r, m: m_s[r:r + m, :], store, gain, shift, 0, tm)

    @pl.when(i == 0)
    def _():
        x_copy(0).start()
        o_copy(0).start()
        x_copy(1).start()
        o_copy(1).start()
        if fetch is not None:
            wq_copy.start()
        if send:
            barrier = pltpu.get_barrier_semaphore()
            for k in range(1, 4):
                pl.semaphore_signal(barrier, inc=1, device_id=(dp, peer(k)), device_id_type=MESH)
            pl.semaphore_wait(barrier, 3)
        x_copy(0).wait()
        o_copy(0).wait()
        project(0)
        norm()

    @pl.when(i + 1 < n)
    def _():
        x_copy(i + 1).wait()
        o_copy(i + 1).wait()

    @pl.when(i + 2 < n)
    def _():
        x_copy(i + 2).start()
        o_copy(i + 2).start()

    if send:
        @pl.when(jnp.logical_and(i >= 1, i - 1 < 3 * IMAGES))
        def _():
            remote(i - 1).start()

        @pl.when(i - 1 >= 3 * IMAGES)
        def _():
            local(i - 1).start()

        @pl.when(i >= slots)
        def _():
            remote(i - slots).wait_send()

    def up(j, c):
        f0 = j * fc + c * nc
        act[j % 2, :, cols(c)] = gelu(dot(n_s[...], wb[D * (1 + j):D * (2 + j), cols(c)]) + bu_ref[one, f0:f0 + nc]).astype(bf16)

    def down(j, c):
        y = dot(act[j % 2], wb[D + F + j * fc:D + F + (j + 1) * fc, cols(c)])
        if j == 0:
            acc[:, cols(c)] = (m_s[:, cols(c)].astype(f32) + bd_ref[one, cols(c)]) + y
        elif j < nj - 1:
            acc[:, cols(c)] = acc[:, cols(c)] + y
        else:
            put(cols(c), (acc[:, cols(c)] + y).astype(bf16))

    for c in range(fc // nc):
        up(0, c)
    for j in range(1, nj):
        for c in range(max(fc, D) // nc):
            if c < fc // nc:
                up(j, c)
            if c < D // nc:
                down(j - 1, c)
    project((i + 1) % 2)
    for c in range(D // nc):
        down(nj - 1, c)
    norm()

    @pl.when(i == n - 1)
    def _():
        if fetch is not None:
            wq_copy.wait()
        if send:
            local(n - 1).start()
            for g in range(n - slots, 3 * IMAGES):
                remote(g).wait_send()
            for g in range(3 * IMAGES, n):
                local(g).wait()
            for g in range(3 * IMAGES):
                remote(g).wait_recv()


def mlp(x, o, w, bo, g, s, bu, bd, layer, first, count, into=None, send=False, fetch=None, w_t=None, fc=1536, nc=512):
    n = count * SEQ // BLK
    base = first * SEQ // BLK
    dma = pltpu.SemaphoreType.DMA
    vm = pltpu.VMEM
    sd = jax.ShapeDtypeStruct
    scratch = [vm((2, BLK, D), bf16), vm((2, D, BLK), bf16), vm((BLK, D), bf16), vm((BLK, D), bf16), vm((2, BLK, fc), bf16), vm((BLK, D), f32),
               dma((2,)), dma((2,)), dma(())]
    limit = MLP_LIMIT
    params = dict(dimension_semantics=("arbitrary",))
    if send:
        scratch += [vm((8, BLK, D), bf16), dma((n,)), dma((3 * IMAGES,))]
        out_shape, out_spec = [sd((4 * IMAGES, BLK, D), bf16)], [HBM]
        params.update(collective_id=0, has_side_effects=True)
        limit += 6 << 20
    else:
        out_shape, out_spec = [pltpu.HBM((T, D), bf16)], [pl.BlockSpec((BLK, D), lambda i: (base + i, 0))]
    extra = []
    if fetch is not None:
        extra.append(w_t)
        out_shape.append(pltpu.VMEM((3 * D, D), bf16))
        out_spec.append(VMEM)
    if into is not None:
        extra.append(into)
    tok = n * BLK
    return pl.pallas_call(
        functools.partial(mlp_kernel, layer=layer, base=base, n=n, fc=fc, nc=nc, alias=into is not None, send=send, fetch=fetch),
        out_shape=out_shape,
        grid=(n,),
        in_specs=[HBM, HBM, VMEM, whole((2, D)), whole((2, D)), whole((2, D)), whole((2, F)), whole((2, D))] + [HBM] * len(extra),
        out_specs=out_spec,
        scratch_shapes=scratch,
        input_output_aliases={7 + len(extra): 0} if into is not None else {},
        compiler_params=pltpu.CompilerParams(vmem_limit_bytes=limit, **params),
        cost_estimate=pl.CostEstimate(flops=2 * tok * D * (2 * F + D), bytes_accessed=tok * D * 6, transcendentals=tok * F),
        name="mlp",
    )(*at_hbm(x, o), *at_vmem(w), *at_hbm(bo, g, s, bu, bd), *extra)


def solution(mesh):
    token_spec = P('dp', 'sp', None)

    def device_step(image_tokens, ln1_gain, ln1_shift, w_qkv, b_qkv, w_out, b_out, ln2_gain, ln2_shift, w_up, b_up, w_down, b_down):
        layers = w_qkv.shape[0]
        w_t = w_qkv.transpose(0, 2, 3, 4, 1).reshape(layers, 3 * D, D)
        w_o = w_out.reshape(layers, D, D)
        me = lax.axis_index('sp')
        par = me.reshape(1).astype(jnp.int32)

        def exchange(k, part):
            return lax.ppermute(part, 'sp', [(s, s ^ k) for s in range(4)])

        def images(k, first, count):
            return lax.dynamic_slice_in_dim(image_tokens, (me ^ k) * IMAGES + first, count)

        far_a, far_b = exchange(2, images(2, 0, 1)), exchange(3, images(3, 0, 1))
        near = exchange(1, images(1, 0, IMAGES))
        rest_a, rest_b, wq, *bias = start(par, image_tokens, w_t, b_qkv)
        rest_a, rest_b = exchange(2, rest_a), exchange(3, rest_b)

        here = lambda i, m: i
        pre = (ln1_gain, ln1_shift)
        fold = (w_o, w_up, w_down)

        def post(l, o, w, *place, **kw):
            return mlp(x, o, w, b_out, ln2_gain, ln2_shift, b_up, b_down, l, *place, **kw)

        bufs = qkv(par, image_tokens, lambda i, m: m[0] * IMAGES + i, near, here, *pre, wq, bias[0], 0, IMAGES, lambda i: 2 * i, True)
        bufs = qkv(par, far_a, here, far_b, here, *pre, wq, bias[0], 0, 1, lambda i: 1, True, into=bufs)
        x = bufs[5]
        h, = post(0, *attn(*bufs[:5], *fold, 0, 0, 1), 0, 1)
        bufs = qkv(par, rest_a, here, rest_b, here, *pre, w_t, bias[0], 0, IMAGES - 1, lambda i: 2 * i + 3, True, into=bufs, after=h)
        x = bufs[5]
        h, = post(0, *attn(*bufs[:5], *fold, 0, 1, IMAGES - 1), 1, IMAGES - 1, into=h)
        x = h.reshape(4 * IMAGES, BLK, D)
        bufs = qkv(par, x, lambda i, m: 2 * i, x, lambda i, m: 2 * i + 1, *pre, w_t, bias[1], 1, 2 * IMAGES, lambda i: i, False)
        x = h
        return post(1, *attn(*bufs[:5], *fold, 1, 0, IMAGES), 0, IMAGES, send=True)[0]

    return jax.shard_map(device_step, mesh=mesh, in_specs=(token_spec,) + (P(),) * 12, out_specs=token_spec, check_vma=False)
```

time: 787 us -> 760 us (0.966)
  Pallas kernels: 737 us -> 717 us
    pallas_call x3, Pallas kernels: 438 us -> 388 us  [mlp(): pl.pallas_call(functools.partial(mlp_kernel, layer=layer, base=base, n=n,...]
    pallas_call x3 -> x4, Pallas kernels: 122 us -> 157 us  [the longest x3 146 us: attn(): pl.pallas_call(functools.partial(attn_kernel, layer=layer, hp=hp, nq=nq,...]
    reshape x0 -> x6, local copies, waits for them, and re-layouts: none -> 10.4 us  [attn(): split = lambda a: a.reshape(HEADS // hp, hp, T)]
  transfers between devices with their start and end apart: 5 -> 5, of which waited for: 0 -> 0; matrix products, arithmetic and copies ran while one was open for 2% -> 1% of each run, Pallas kernels for 19% -> 19%
where the time goes in v4:
time: 760 us; the launch traced here: 752 us
  Pallas kernels  717 us (94%)
  local copies, waits for them, and re-layouts  29.4 us (4%)
    pallas_call x3, Pallas kernels, mlp(): pl.pallas_call(functools.partial(mlp_kernel, layer=layer, base=base, n=n,...  388 us
    pallas_call x4, Pallas kernels, qkv(): pl.pallas_call(functools.partial(qkv_kernel, layer=layer, n=n, copy_h=cop...  171 us
    pallas_call x3, Pallas kernels, attn(): pl.pallas_call(functools.partial(attn_kernel, layer=layer, hp=hp, nq=nq,...  146 us
  transfers between devices with their start and end apart: 5, of which 0 were waited for; matrix products, arithmetic and copies ran while one was open for 1% of the time, Pallas kernels for 19%

profile of v4, /device:TPU:0, one launch (start us, length us, event | category | flops | bytes accessed | tf_op | source)
XLA Modules:
  0.0 752.2 jit_solution(7495738366534346271)
XLA Ops:
  0.0 3.8 constant_dynamic-slice_fusion
  3.8 0.9 collective-permute-start.4
  4.6 2.6 constant_dynamic-slice_fusion.1
  7.3 2.6 collective-permute-start.3
  9.9 0.0 collective-permute-start.2
  9.9 0.0 copy-start
  9.9 0.8 copy-done
  10.7 10.9 %start.1 = (bf16[3,256,1536]{2,1,0:T(8,128)(2,1)}, bf16[3,256,1536]{2,1,0:T(8,128)(2,1)}, bf16[4608,1536]{1,0:T(8,128)(2,1)S(1)}, f32[4608,128]{1,0:T(8,128)}, f32[4608,128]{1,0:T(8,128)}) custom-call(s32[1]{0:T(128)} %bitcast.par.refs_0_, bf16[16,256,1536]{2,1,0:T(8,128)(2,1)} %refs_3_.4, bf16[16,256,1536]{2,1,0:T(8,128)(2,1)} %refs_3_.4, ...), custom_call_target="tpu_custom_call" | custom-call | flops 1073741824 | bytes 31457280 | tf_op jit(solution)/shard_map/start/pallas_call | solution.py:93
  21.6 2.0 collective-permute-start
  23.6 0.0 collective-permute-start.1
  23.6 0.0 collective-permute-done.4.refs_2_.refs_4_
  23.6 41.6 %qkv.4 = (bf16[1536,4096]{1,0:T(8,128)(2,1)}, bf16[16,4096,128]{2,1,0:T(8,128)(2,1)}, bf16[1536,4096]{1,0:T(8,128)(2,1)}, f32[16,4096]{1,0:T(8,128)}, f32[16,4096]{1,0:T(8,128)}, /*index=5*/bf16[4096,1536]{1,0:T(8,128)(2,1)}) custom-call(s32[1]{0:T(128)} %bitcast.par.refs_0_, bf16[16,256,1536]{2,1,0:T(8,128)(2,1)} %refs_3_.4, ...), custom_call_target="tpu_custom_call" | custom-call | flops 28991029248 | bytes 31457280 | tf_op jit(solution)/shard_map/qkv/pallas_call | solution.py:185
  65.2 0.0 collective-permute-done.3.refs_2_.refs_4_
  65.2 0.0 collective-permute-done.2.refs_1_.refs_3_
  65.2 13.5 %qkv.5 = (bf16[1536,4096]{1,0:T(8,128)(2,1)}, bf16[16,4096,128]{2,1,0:T(8,128)(2,1)}, bf16[1536,4096]{1,0:T(8,128)(2,1)}, f32[16,4096]{1,0:T(8,128)}, f32[16,4096]{1,0:T(8,128)}, /*index=5*/bf16[4096,1536]{1,0:T(8,128)(2,1)}) custom-call(s32[1]{0:T(128)} %bitcast.par.refs_0_, ...), custom_call_target="tpu_custom_call", output_to_operand_aliasing={{0}: (9, {}), {1}: (10, {}), {2}: (11, {}), {3}: (12, {}), ... | custom-call | flops 7247757312 | bytes 7864320 | tf_op jit(solution)/shard_map/qkv/pallas_call | solution.py:185
  78.7 1.7 reshape.32.nq_ref
  80.4 1.8 reshape.33.nk_ref
  82.1 24.4 %attn.3 = (bf16[1536,1024]{1,0:T(8,128)(2,1)}, bf16[13824,1536]{1,0:T(8,128)(2,1)S(1)}) custom-call(bf16[1536,4096]{1,0:T(8,128)(2,1)} %get-tuple-element.49.q_ref.refs_9_, bf16[16,4096,128]{2,1,0:T(8,128)(2,1)} %get-tuple-element.50.k_ref.refs_10_, bf16[1536,4096]{1,0:T(8,128)(2,1)} %get-tuple-element.51.v_ref.refs_11_, f32[4,4,4096]{2,1,0:T(4,128)} %reshape.32.nq_ref, ...), custom_call_target="tpu_custom_call" | custom-call | flops 6442450944 | bytes 14155776 | tf_op jit(solution)/shard_map/attn/pallas_call | solution.py:281
  106.5 51.6 %mlp.3.refs_15_.refs_8_ = bf16[4096,1536]{1,0:T(8,128)(2,1)} custom-call(bf16[4096,1536]{1,0:T(8,128)(2,1)} %get-tuple-element.54.refs_0_.refs_14_, bf16[1536,1024]{1,0:T(8,128)(2,1)} %get-tuple-element.55.refs_1_, bf16[13824,1536]{1,0:T(8,128)(2,1)S(1)} %get-tuple-element.56.refs_2_, f32[2,1536]{1,0:T(2,128)} %refs_3_.7, f32[2,1536]{1,0:T(2,128)} %refs_4_.5, ...), custom_call_target="tpu_custom_call" | custom-call | flops 43486543872 | bytes 9437184 | tf_op jit(solution)/shard_map/mlp/pallas_call | solution.py:476
  158.2 0.0 collective-permute-done.refs_1_.refs_3_
  158.2 0.0 copy-start.1
  158.2 0.0 collective-permute-done.1.refs_2_.refs_4_
  158.2 1.4 copy-done.1
  159.6 37.2 %qkv.6 = (bf16[1536,4096]{1,0:T(8,128)(2,1)}, bf16[16,4096,128]{2,1,0:T(8,128)(2,1)}, bf16[1536,4096]{1,0:T(8,128)(2,1)}, f32[16,4096]{1,0:T(8,128)}, f32[16,4096]{1,0:T(8,128)}, /*index=5*/bf16[4096,1536]{1,0:T(8,128)(2,1)}) custom-call(s32[1]{0:T(128)} %bitcast.par.refs_0_, ...), custom_call_target="tpu_custom_call", output_to_operand_aliasing={{0}: (9, {}), {1}: (10, {}), {2}: (11, {}), {3}: (12, {}), ... | custom-call | flops 21743271936 | bytes 23592960 | tf_op jit(solution)/shard_map/qkv/pallas_call | solution.py:185
  196.8 1.8 reshape.35.nq_ref
  198.5 1.7 reshape.36.nk_ref
  200.2 53.7 %attn.4 = (bf16[1536,3072]{1,0:T(8,128)(2,1)}, bf16[13824,1536]{1,0:T(8,128)(2,1)S(1)}) custom-call(bf16[1536,4096]{1,0:T(8,128)(2,1)} %get-tuple-element.58.q_ref, bf16[16,4096,128]{2,1,0:T(8,128)(2,1)} %get-tuple-element.59.k_ref, bf16[1536,4096]{1,0:T(8,128)(2,1)} %get-tuple-element.60.v_ref, f32[4,4,4096]{2,1,0:T(4,128)} %reshape.35.nq_ref, ...), custom_call_target="tpu_custom_call" | custom-call | flops 19327352832 | bytes 42467328 | tf_op jit(solution)/shard_map/attn/pallas_call | solution.py:281
  253.9 144.3 %mlp.4.refs_0_ = bf16[4096,1536]{1,0:T(8,128)(2,1)} custom-call(bf16[4096,1536]{1,0:T(8,128)(2,1)} %get-tuple-element.57.refs_0_, bf16[1536,3072]{1,0:T(8,128)(2,1)} %get-tuple-element.63.refs_1_, bf16[13824,1536]{1,0:T(8,128)(2,1)S(1)} %get-tuple-element.64.refs_2_, f32[2,1536]{1,0:T(2,128)} %refs_3_.7, ...), custom_call_target="tpu_custom_call", output_to_operand_aliasing={{}: (8, {})} | custom-call | flops 130459631616 | bytes 28311552 | tf_op jit(solution)/shard_map/mlp/pallas_call | solution.py:476
  398.3 78.9 %qkv.7 = (bf16[1536,4096]{1,0:T(8,128)(2,1)}, bf16[16,4096,128]{2,1,0:T(8,128)(2,1)}, bf16[1536,4096]{1,0:T(8,128)(2,1)}, f32[16,4096]{1,0:T(8,128)}, f32[16,4096]{1,0:T(8,128)}) custom-call(s32[1]{0:T(128)} %bitcast.par.refs_0_, bf16[16,256,1536]{2,1,0:T(8,128)(2,1)} %bitcast.12, bf16[16,256,1536]{2,1,0:T(8,128)(2,1)} %bitcast.13, ...), custom_call_target="tpu_custom_call" | custom-call | flops 57982058496 | bytes 62914560 | tf_op jit(solution)/shard_map/qkv/pallas_call | solution.py:185
  477.2 1.7 reshape.38.nq_ref
  478.9 1.7 reshape.39.nk_ref
  480.7 68.3 %attn.5 = (bf16[1536,4096]{1,0:T(8,128)(2,1)}, bf16[13824,1536]{1,0:T(8,128)(2,1)S(1)}) custom-call(bf16[1536,4096]{1,0:T(8,128)(2,1)} %get-tuple-element.66.q_ref, bf16[16,4096,128]{2,1,0:T(8,128)(2,1)} %get-tuple-element.67.k_ref, bf16[1536,4096]{1,0:T(8,128)(2,1)} %get-tuple-element.68.v_ref, f32[4,4,4096]{2,1,0:T(4,128)} %reshape.38.nq_ref, ...), custom_call_target="tpu_custom_call" | custom-call | flops 25769803776 | bytes 56623104 | tf_op jit(solution)/shard_map/attn/pallas_call | solution.py:281
  549.0 192.3 %mlp.5 = bf16[16,256,1536]{2,1,0:T(8,128)(2,1)} custom-call(bf16[4096,1536]{1,0:T(8,128)(2,1)} %mlp.4.refs_0_, bf16[1536,4096]{1,0:T(8,128)(2,1)} %get-tuple-element.71.refs_1_, bf16[13824,1536]{1,0:T(8,128)(2,1)S(1)} %get-tuple-element.72.refs_2_, f32[2,1536]{1,0:T(2,128)} %refs_3_.7, f32[2,1536]{1,0:T(2,128)} %refs_4_.5, f32[2,1536]{1,0:T(2,128)} %refs_5_.13, ...), custom_call_target="tpu_custom_call" | custom-call | flops 173946175488 | bytes 37748736 | tf_op jit(solution)/shard_map/mlp/pallas_call | solution.py:476
  741.3 10.5 %copy.41 = bf16[16,256,1536]{2,1,0:T(8,128)(2,1)} copy(bf16[16,256,1536]{2,1,0:T(8,128)(2,1)} %mlp.5) | data formatting | bytes 25165824
Async XLA Ops:
  3.8 19.8 %collective-permute-start.4 = (bf16[4,256,1536]{2,1,0:T(8,128)(2,1)}, bf16[4,256,1536]{2,1,0:T(8,128)(2,1)}, u32[]{:S(2)}, u32[]{:S(2)}) collective-permute-start(bf16[4,256,1536]{2,1,0:T(8,128)(2,1)} %constant_dynamic-slice_fusion), channel_id=1, source_target_pairs={{0,1},{1,0},{2,3},{3,2},{4,5},{5,4},{6,7},{7,6}} | collective-permute-start | bytes 9437192 | tf_op jit(solution)/shard_map/ppermute | solution.py:501
  7.3 57.9 %collective-permute-start.3 = (bf16[1,256,1536]{2,1,0:T(8,128)(2,1)}, bf16[1,256,1536]{2,1,0:T(8,128)(2,1)}, u32[]{:S(2)}, u32[]{:S(2)}) collective-permute-start(bf16[1,256,1536]{2,1,0:T(8,128)(2,1)} %get-tuple-element.73), channel_id=1, source_target_pairs={{0,3},{1,2},{2,1},{3,0},{4,7},{5,6},{6,5},{7,4}} | collective-permute-start | bytes 2359304 | tf_op jit(solution)/shard_map/ppermute | solution.py:501
  9.9 55.3 %collective-permute-start.2 = (bf16[1,256,1536]{2,1,0:T(8,128)(2,1)}, bf16[1,256,1536]{2,1,0:T(8,128)(2,1)}, u32[]{:S(2)}, u32[]{:S(2)}) collective-permute-start(bf16[1,256,1536]{2,1,0:T(8,128)(2,1)} %get-tuple-element.74), channel_id=1, source_target_pairs={{0,2},{1,3},{2,0},{3,1},{4,6},{5,7},{6,4},{7,5}} | collective-permute-start | bytes 2359304 | tf_op jit(solution)/shard_map/ppermute | solution.py:501
  9.9 0.8 copy-start
  21.6 136.6 %collective-permute-start = (bf16[3,256,1536]{2,1,0:T(8,128)(2,1)}, bf16[3,256,1536]{2,1,0:T(8,128)(2,1)S(1)}, u32[]{:S(2)}, u32[]{:S(2)}) collective-permute-start(bf16[3,256,1536]{2,1,0:T(8,128)(2,1)} %get-tuple-element.39), channel_id=1, source_target_pairs={{0,2},{1,3},{2,0},{3,1},{4,6},{5,7},{6,4},{7,5}} | collective-permute-start | bytes 7077896 | tf_op jit(solution)/shard_map/ppermute | solution.py:501
  23.6 134.6 %collective-permute-start.1 = (bf16[3,256,1536]{2,1,0:T(8,128)(2,1)}, bf16[3,256,1536]{2,1,0:T(8,128)(2,1)}, u32[]{:S(2)}, u32[]{:S(2)}) collective-permute-start(bf16[3,256,1536]{2,1,0:T(8,128)(2,1)} %get-tuple-element.40), channel_id=1, source_target_pairs={{0,3},{1,2},{2,1},{3,0},{4,7},{5,6},{6,5},{7,4}} | collective-permute-start | bytes 7077896 | tf_op jit(solution)/shard_map/ppermute | solution.py:501
  158.2 1.4 copy-start.1

commit v5 on v4

--- a/solution.py
+++ b/solution.py
@@ -37,8 +37,8 @@
 
 
 VMEM = pl.BlockSpec(memory_space=pltpu.VMEM)
-ATTN_LIMIT = 17 << 20
-MLP_LIMIT = 15 << 20
+QKV_LIMIT = 50 << 20
+LAYER_LIMIT = 23 << 20
 
 
 def at_hbm(*arrays):
@@ -62,46 +62,44 @@
         store(r, step, (c * lax.rsqrt(var + LN_EPS) * gain + shift).astype(bf16))
 
 
-def start_kernel(par, a_ref, b_ref, bias_ref, w_hbm, sa_ref, sb_ref, w_out, b0_out, b1_out, sem):
-    i = pl.program_id(0)
-    w_copy = pltpu.make_async_copy(w_hbm.at[0], w_out, sem)
-
-    @pl.when(i == 0)
-    def _():
-        w_copy.start()
-        for l, out in ((0, b0_out), (1, b1_out)):
-            for t in range(3):
-                cols = bias_ref[l, t].T
-                for h in range(HEADS):
-                    r = (t * HEADS + h) * HD
-                    out[r:r + HD, :] = jnp.broadcast_to(cols[:, h:h + 1], (HD, 128))
-
-    sa_ref[...] = a_ref[...]
-    sb_ref[...] = b_ref[...]
-
-    @pl.when(i == pl.num_programs(0) - 1)
-    def _():
-        w_copy.wait()
-
-
-def start(par, tokens, w_t, b_qkv):
-    sd = jax.ShapeDtypeStruct
-    piece = lambda k: pl.BlockSpec((1, BLK, D), lambda i, p: ((p[0] ^ k) * IMAGES + 1 + i, 0, 0))
-    out = pl.BlockSpec((1, BLK, D), lambda i, p: (i, 0, 0))
-    part = sd((IMAGES - 1, BLK, D), bf16)
-    bias = sd((3 * D, 128), f32)
+def start_kernel(tokens, w_hbm, sa, sb, near, w_out, buf, w_sem, in_sem, out_sem, s_sem, r_sem):
+    dp, me = lax.axis_index("dp"), lax.axis_index("sp")
+    peer = me + 1 - 2 * (me % 2)
+    w_copy = pltpu.make_async_copy(w_hbm.at[0], w_out, w_sem)
+    swap = pltpu.make_async_remote_copy(
+        src_ref=tokens.at[pl.ds(peer * IMAGES, IMAGES)], dst_ref=near, send_sem=s_sem, recv_sem=r_sem, device_id=(dp, peer), device_id_type=MESH)
+    far = (lax.rem(me + 2, 4), 3 - me)
+    ins = [pltpu.make_async_copy(tokens.at[pl.ds(f * IMAGES + 1, IMAGES - 1)], buf.at[n], in_sem.at[n]) for n, f in enumerate(far)]
+    outs = [pltpu.make_async_copy(buf.at[n], out, out_sem.at[n]) for n, out in enumerate((sa, sb))]
+    for c in ins:
+        c.start()
+    w_copy.start()
+    barrier = pltpu.get_barrier_semaphore()
+    pl.semaphore_signal(barrier, inc=1, device_id=(dp, peer), device_id_type=MESH)
+    pl.semaphore_wait(barrier, 1)
+    swap.start()
+    for i, o in zip(ins, outs):
+        i.wait()
+        o.start()
+    for o in outs:
+        o.wait()
+    swap.wait()
+    w_copy.wait()
+
+
+def start(tokens, w_t):
+    part = pltpu.HBM((IMAGES - 1, BLK, D), bf16)
+    dma = pltpu.SemaphoreType.DMA
     return pl.pallas_call(
         start_kernel,
-        out_shape=(part, part, pltpu.VMEM((3 * D, D), bf16), bias, bias),
-        grid_spec=pltpu.PrefetchScalarGridSpec(
-            num_scalar_prefetch=1, grid=(IMAGES - 1,),
-            in_specs=[piece(2), piece(3), whole(b_qkv.shape), HBM],
-            out_specs=(out, out, VMEM, whole((3 * D, 128)), whole((3 * D, 128))),
-            scratch_shapes=[pltpu.SemaphoreType.DMA(())]),
-        compiler_params=pltpu.CompilerParams(vmem_limit_bytes=40 << 20, dimension_semantics=("arbitrary",)),
+        out_shape=(part, part, pltpu.HBM((IMAGES, BLK, D), bf16), pltpu.VMEM((3 * D, D), bf16)),
+        in_specs=[HBM, HBM],
+        out_specs=(HBM, HBM, HBM, VMEM),
+        scratch_shapes=[pltpu.VMEM((2, IMAGES - 1, BLK, D), bf16), dma(()), dma((2,)), dma((2,)), dma(()), dma(())],
+        compiler_params=pltpu.CompilerParams(vmem_limit_bytes=QKV_LIMIT, collective_id=1, has_side_effects=True),
         cost_estimate=pl.CostEstimate(flops=1 << 30, bytes_accessed=30 << 20, transcendentals=0),
         name="start",
-    )(par, *at_hbm(tokens, tokens), b_qkv, w_t)
+    )(*at_hbm(tokens), w_t)
 
 
 def qkv_kernel(*refs, layer, n, copy_h, alias, fetch):
@@ -131,15 +129,16 @@
         t = order[o]
         r0, rw = c * CH, t * D + c * CH
         y = dot_nt(w[rw:rw + CH, :], n_s[...])
-        bias = jnp.concatenate([b_ref[rw:rw + CH, :]] * (tm // 128), axis=1)
+        heads = range(c * (CH // HD), (c + 1) * (CH // HD))
+        bias = b_ref[layer, t].T
+        bias = jnp.concatenate([jnp.broadcast_to(bias[:, h:h + 1], (HD, tm)) for h in heads], axis=0)
         yb = (y + bias).astype(bf16)
         if t == 2:
             v_ref[r0:r0 + CH, :] = yb
             return
         if t == 0:
             q_ref[r0:r0 + CH, :] = yb
-        for h in range(CH // HD):
-            hh = c * (CH // HD) + h
+        for h, hh in enumerate(heads):
             yh = yb[h * HD:(h + 1) * HD, :]
             yf = yh.astype(f32)
             nn = jnp.sum(yf * yf, axis=0, keepdims=True)
@@ -188,12 +187,12 @@
         grid_spec=pltpu.PrefetchScalarGridSpec(
             num_scalar_prefetch=1, grid=(n,),
             in_specs=[piece(xa_map, 0), piece(xb_map, 0), piece(xa_map, 1), piece(xb_map, 1), whole((2, D)), whole((2, D)), HBM if fetch else VMEM,
-                      whole((3 * D, 128))] + [HBM] * len(extra),
+                      whole(b.shape)] + [HBM] * len(extra),
             out_specs=tuple(specs),
             scratch_shapes=[pltpu.VMEM((tm, D), bf16), pltpu.VMEM((tm, D), bf16)]
             + ([pltpu.VMEM((3 * D, D), bf16), pltpu.SemaphoreType.DMA(())] if fetch else [])),
         input_output_aliases={9 + a: a for a in range(len(into or ()))},
-        compiler_params=pltpu.CompilerParams(vmem_limit_bytes=48 << 20, dimension_semantics=("arbitrary",)),
+        compiler_params=pltpu.CompilerParams(vmem_limit_bytes=63 << 20 if fetch else QKV_LIMIT, dimension_semantics=("arbitrary",)),
         cost_estimate=pl.CostEstimate(flops=2 * n * tm * D * 3 * D, bytes_accessed=n * tm * D * 10, transcendentals=0),
         name="qkv",
     )(par, *at_hbm(xa, xb, xa, xb), *at_hbm(g, s), *(at_hbm(w) if fetch else at_vmem(w)), *at_hbm(b), *extra)
@@ -207,7 +206,7 @@
     @pl.when(step == 0)
     def _():
         for c in copies:
-            c.start()
+            c.start(priority=1)
 
     @pl.when(step == pl.num_programs(0) * pl.num_programs(1) - 1)
     def _():
@@ -222,8 +221,8 @@
         return slice(h * HD, (h + 1) * HD)
 
     def shift_rows(h, q):
-        kmax = jnp.max(nk_ref[0, h:h + 1, :], axis=1, keepdims=True)
-        m = jnp.sqrt(nq_ref[0, h:h + 1, q * nq:(q + 1) * nq] * kmax) * (-1.0 - 2.0 ** -7)
+        kmax = jnp.max(nk_ref[h:h + 1, :], axis=1, keepdims=True)
+        m = jnp.sqrt(nq_ref[h:h + 1, q * nq:(q + 1) * nq] * kmax) * (-1.0 - 2.0 ** -7)
         first = lax.broadcasted_iota(jnp.int32, (128 - HD, nq), 0) == 0
         return jnp.where(first, jnp.broadcast_to(m, (128 - HD, nq)), 0.0).astype(bf16)
 
@@ -274,10 +273,9 @@
         lax.fori_loop(0, hp * (SEQ // qb), body, 0)
 
 
-def attn(q, k, v, nq2, nk2, w_o, w_up, w_down, layer, first, count, hp=4, nq=512, kb=256, lag=3):
+def attn(q, k, v, nq2, nk2, w_o, w_up, w_down, layer, first, count, hp=8, nq=512, kb=256, lag=3):
     blk = pl.BlockSpec((hp * HD, SEQ), lambda i, j: (j, first + i))
-    nrm = pl.BlockSpec((1, hp, SEQ), lambda i, j: (j, 0, first + i))
-    split = lambda a: a.reshape(HEADS // hp, hp, T)
+    nrm = pl.BlockSpec((hp, SEQ), lambda i, j: (j, first + i))
     return pl.pallas_call(
         functools.partial(attn_kernel, layer=layer, hp=hp, nq=nq, kb=kb, lag=lag),
         out_shape=(pltpu.HBM((D, count * SEQ), bf16), pltpu.VMEM((D + 2 * F, D), bf16)),
@@ -285,10 +283,10 @@
         in_specs=[blk, pl.BlockSpec((hp, SEQ, 128), lambda i, j: (j, first + i, 0)), blk, nrm, nrm, HBM, HBM, HBM],
         out_specs=(pl.BlockSpec((hp * HD, SEQ), lambda i, j: (j, i)), VMEM),
         scratch_shapes=[pltpu.SemaphoreType.DMA((2 + F // D,))],
-        compiler_params=pltpu.CompilerParams(vmem_limit_bytes=(ATTN_LIMIT), dimension_semantics=("arbitrary", "arbitrary")),
+        compiler_params=pltpu.CompilerParams(vmem_limit_bytes=LAYER_LIMIT, dimension_semantics=("arbitrary", "arbitrary")),
         cost_estimate=pl.CostEstimate(flops=4 * count * SEQ * SEQ * D, bytes_accessed=count * SEQ * D * 9, transcendentals=count * SEQ * SEQ * HEADS),
         name="attn",
-    )(*at_hbm(q, k, v, split(nq2), split(nk2)), w_o, w_up, w_down)
+    )(*at_hbm(q, k, v, nq2, nk2), w_o, w_up, w_down)
 
 
 def gelu(u):
@@ -456,13 +454,11 @@
     sd = jax.ShapeDtypeStruct
     scratch = [vm((2, BLK, D), bf16), vm((2, D, BLK), bf16), vm((BLK, D), bf16), vm((BLK, D), bf16), vm((2, BLK, fc), bf16), vm((BLK, D), f32),
                dma((2,)), dma((2,)), dma(())]
-    limit = MLP_LIMIT
     params = dict(dimension_semantics=("arbitrary",))
     if send:
         scratch += [vm((8, BLK, D), bf16), dma((n,)), dma((3 * IMAGES,))]
         out_shape, out_spec = [sd((4 * IMAGES, BLK, D), bf16)], [HBM]
         params.update(collective_id=0, has_side_effects=True)
-        limit += 6 << 20
     else:
         out_shape, out_spec = [pltpu.HBM((T, D), bf16)], [pl.BlockSpec((BLK, D), lambda i: (base + i, 0))]
     extra = []
@@ -481,7 +477,7 @@
         out_specs=out_spec,
         scratch_shapes=scratch,
         input_output_aliases={7 + len(extra): 0} if into is not None else {},
-        compiler_params=pltpu.CompilerParams(vmem_limit_bytes=limit, **params),
+        compiler_params=pltpu.CompilerParams(vmem_limit_bytes=LAYER_LIMIT, **params),
         cost_estimate=pl.CostEstimate(flops=2 * tok * D * (2 * F + D), bytes_accessed=tok * D * 6, transcendentals=tok * F),
         name="mlp",
     )(*at_hbm(x, o), *at_vmem(w), *at_hbm(bo, g, s, bu, bd), *extra)
@@ -504,8 +500,7 @@
             return lax.dynamic_slice_in_dim(image_tokens, (me ^ k) * IMAGES + first, count)
 
         far_a, far_b = exchange(2, images(2, 0, 1)), exchange(3, images(3, 0, 1))
-        near = exchange(1, images(1, 0, IMAGES))
-        rest_a, rest_b, wq, *bias = start(par, image_tokens, w_t, b_qkv)
+        rest_a, rest_b, near, wq = start(image_tokens, w_t)
         rest_a, rest_b = exchange(2, rest_a), exchange(3, rest_b)
 
         here = lambda i, m: i
@@ -515,15 +510,15 @@
         def post(l, o, w, *place, **kw):
             return mlp(x, o, w, b_out, ln2_gain, ln2_shift, b_up, b_down, l, *place, **kw)
 
-        bufs = qkv(par, image_tokens, lambda i, m: m[0] * IMAGES + i, near, here, *pre, wq, bias[0], 0, IMAGES, lambda i: 2 * i, True)
-        bufs = qkv(par, far_a, here, far_b, here, *pre, wq, bias[0], 0, 1, lambda i: 1, True, into=bufs)
+        bufs = qkv(par, image_tokens, lambda i, m: m[0] * IMAGES + i, near, here, *pre, wq, b_qkv, 0, IMAGES, lambda i: 2 * i, True)
+        bufs = qkv(par, far_a, here, far_b, here, *pre, wq, b_qkv, 0, 1, lambda i: 1, True, into=bufs)
         x = bufs[5]
         h, = post(0, *attn(*bufs[:5], *fold, 0, 0, 1), 0, 1)
-        bufs = qkv(par, rest_a, here, rest_b, here, *pre, w_t, bias[0], 0, IMAGES - 1, lambda i: 2 * i + 3, True, into=bufs, after=h)
+        bufs = qkv(par, rest_a, here, rest_b, here, *pre, w_t, b_qkv, 0, IMAGES - 1, lambda i: 2 * i + 3, True, into=bufs, after=h)
         x = bufs[5]
         h, = post(0, *attn(*bufs[:5], *fold, 0, 1, IMAGES - 1), 1, IMAGES - 1, into=h)
         x = h.reshape(4 * IMAGES, BLK, D)
-        bufs = qkv(par, x, lambda i, m: 2 * i, x, lambda i, m: 2 * i + 1, *pre, w_t, bias[1], 1, 2 * IMAGES, lambda i: i, False)
+        bufs = qkv(par, x, lambda i, m: 2 * i, x, lambda i, m: 2 * i + 1, *pre, w_t, b_qkv, 1, 2 * IMAGES, lambda i: i, False)
         x = h
         return post(1, *attn(*bufs[:5], *fold, 1, 0, IMAGES), 0, IMAGES, send=True)[0]
 

time: 760 us -> 716 us (0.942)
  Pallas kernels: 717 us -> 691 us
  local copies, waits for them, and re-layouts: 29.4 us -> 13.1 us
    pallas_call x3, Pallas kernels: 146 us -> 132 us  [attn(): pl.pallas_call(functools.partial(attn_kernel, layer=layer, hp=hp, nq=nq,...]
    reshape x6 -> x0, local copies, waits for them, and re-layouts: 10.4 us -> none  [attn(): split = lambda a: a.reshape(HEADS // hp, hp, T)]
  transfers between devices with their start and end apart: 5 -> 4, of which waited for: 0 -> 0; matrix products, arithmetic and copies ran while one was open for 1% -> 0% of each run, Pallas kernels for 19% -> 19%
where the time goes in v5:
time: 716 us; the launch traced here: 710 us
  Pallas kernels  691 us (97%)
  local copies, waits for them, and re-layouts  13.1 us (2%)
    pallas_call x3, Pallas kernels, mlp(): pl.pallas_call(functools.partial(mlp_kernel, layer=layer, base=base, n=n,...  388 us
    pallas_call x4, Pallas kernels, qkv(): pl.pallas_call(functools.partial(qkv_kernel, layer=layer, n=n, copy_h=cop...  164 us
    pallas_call x3, Pallas kernels, attn(): pl.pallas_call(functools.partial(attn_kernel, layer=layer, hp=hp, nq=nq,...  132 us
  transfers between devices with their start and end apart: 4, of which 0 were waited for; matrix products, arithmetic and copies ran while one was open for 0% of the time, Pallas kernels for 19%

profile of v5, /device:TPU:0, one launch (start us, length us, event | category | flops | bytes accessed | tf_op | source)
XLA Modules:
  0.0 709.7 jit_solution(3985379291674271715)
XLA Ops:
  0.0 2.6 constant_dynamic-slice_fusion
  2.6 2.8 collective-permute-start.3
  5.4 0.6 collective-permute-start.2
  6.0 8.2 %start.1 = (bf16[3,256,1536]{2,1,0:T(8,128)(2,1)}, bf16[3,256,1536]{2,1,0:T(8,128)(2,1)}, bf16[4,256,1536]{2,1,0:T(8,128)(2,1)}, bf16[4608,1536]{1,0:T(8,128)(2,1)S(1)}) custom-call(bf16[16,256,1536]{2,1,0:T(8,128)(2,1)} %refs_3_.4, bf16[2,4608,1536]{2,1,0:T(8,128)(2,1)} %bitcast.6), custom_call_target="tpu_custom_call" | custom-call | flops 1073741824 | bytes 31457280 | tf_op jit(solution)/shard_map/start/pallas_call | solution.py:93
  14.2 1.5 collective-permute-start
  15.7 0.0 collective-permute-start.1
  15.7 39.8 %qkv.4 = (bf16[1536,4096]{1,0:T(8,128)(2,1)}, bf16[16,4096,128]{2,1,0:T(8,128)(2,1)}, bf16[1536,4096]{1,0:T(8,128)(2,1)}, f32[16,4096]{1,0:T(8,128)}, f32[16,4096]{1,0:T(8,128)}, /*index=5*/bf16[4096,1536]{1,0:T(8,128)(2,1)}) custom-call(s32[1]{0:T(128)} %bitcast.refs_0_, bf16[16,256,1536]{2,1,0:T(8,128)(2,1)} %refs_3_.4, ...), custom_call_target="tpu_custom_call" | custom-call | flops 28991029248 | bytes 31457280 | tf_op jit(solution)/shard_map/qkv/pallas_call | solution.py:184
  55.5 0.0 collective-permute-done.3.refs_2_.refs_4_
  55.5 0.0 collective-permute-done.2.refs_1_.refs_3_
  55.5 12.9 %qkv.5 = (bf16[1536,4096]{1,0:T(8,128)(2,1)}, bf16[16,4096,128]{2,1,0:T(8,128)(2,1)}, bf16[1536,4096]{1,0:T(8,128)(2,1)}, f32[16,4096]{1,0:T(8,128)}, f32[16,4096]{1,0:T(8,128)}, /*index=5*/bf16[4096,1536]{1,0:T(8,128)(2,1)}) custom-call(s32[1]{0:T(128)} %bitcast.refs_0_, ...), custom_call_target="tpu_custom_call", output_to_operand_aliasing={{0}: (9, {}), {1}: (10, {}), {2}: (11, {}), {3}: (12, {}), ... | custom-call | flops 7247757312 | bytes 7864320 | tf_op jit(solution)/shard_map/qkv/pallas_call | solution.py:184
  68.4 25.6 %attn.3 = (bf16[1536,1024]{1,0:T(8,128)(2,1)}, bf16[13824,1536]{1,0:T(8,128)(2,1)S(1)}) custom-call(bf16[1536,4096]{1,0:T(8,128)(2,1)} %get-tuple-element.48.q_ref.refs_9_, bf16[16,4096,128]{2,1,0:T(8,128)(2,1)} %get-tuple-element.49.k_ref.refs_10_, bf16[1536,4096]{1,0:T(8,128)(2,1)} %get-tuple-element.50.v_ref.refs_11_, ...), custom_call_target="tpu_custom_call" | custom-call | flops 6442450944 | bytes 14155776 | tf_op jit(solution)/shard_map/attn/pallas_call | solution.py:279
  94.1 51.5 %mlp.3.refs_15_.refs_8_ = bf16[4096,1536]{1,0:T(8,128)(2,1)} custom-call(bf16[4096,1536]{1,0:T(8,128)(2,1)} %get-tuple-element.53.refs_0_.refs_14_, bf16[1536,1024]{1,0:T(8,128)(2,1)} %get-tuple-element.54.refs_1_, bf16[13824,1536]{1,0:T(8,128)(2,1)S(1)} %get-tuple-element.55.refs_2_, f32[2,1536]{1,0:T(2,128)} %refs_3_.7, f32[2,1536]{1,0:T(2,128)} %refs_4_.5, ...), custom_call_target="tpu_custom_call" | custom-call | flops 43486543872 | bytes 9437184 | tf_op jit(solution)/shard_map/mlp/pallas_call | solution.py:472
  145.6 0.0 collective-permute-done.refs_1_.refs_3_
  145.6 0.0 collective-permute-done.1.refs_2_.refs_4_
  145.6 35.5 %qkv.6 = (bf16[1536,4096]{1,0:T(8,128)(2,1)}, bf16[16,4096,128]{2,1,0:T(8,128)(2,1)}, bf16[1536,4096]{1,0:T(8,128)(2,1)}, f32[16,4096]{1,0:T(8,128)}, f32[16,4096]{1,0:T(8,128)}, /*index=5*/bf16[4096,1536]{1,0:T(8,128)(2,1)}) custom-call(s32[1]{0:T(128)} %bitcast.refs_0_, ...), custom_call_target="tpu_custom_call", output_to_operand_aliasing={{0}: (9, {}), {1}: (10, {}), {2}: (11, {}), {3}: (12, {}), ... | custom-call | flops 21743271936 | bytes 23592960 | tf_op jit(solution)/shard_map/qkv/pallas_call | solution.py:184
  181.1 46.0 %attn.4 = (bf16[1536,3072]{1,0:T(8,128)(2,1)}, bf16[13824,1536]{1,0:T(8,128)(2,1)S(1)}) custom-call(bf16[1536,4096]{1,0:T(8,128)(2,1)} %get-tuple-element.57.q_ref, bf16[16,4096,128]{2,1,0:T(8,128)(2,1)} %get-tuple-element.58.k_ref, bf16[1536,4096]{1,0:T(8,128)(2,1)} %get-tuple-element.59.v_ref, f32[16,4096]{1,0:T(8,128)} %get-tuple-element.60.nq_ref, ...), custom_call_target="tpu_custom_call" | custom-call | flops 19327352832 | bytes 42467328 | tf_op jit(solution)/shard_map/attn/pallas_call | solution.py:279
  227.2 144.3 %mlp.4.refs_0_ = bf16[4096,1536]{1,0:T(8,128)(2,1)} custom-call(bf16[4096,1536]{1,0:T(8,128)(2,1)} %get-tuple-element.56.refs_0_, bf16[1536,3072]{1,0:T(8,128)(2,1)} %get-tuple-element.62.refs_1_, bf16[13824,1536]{1,0:T(8,128)(2,1)S(1)} %get-tuple-element.63.refs_2_, f32[2,1536]{1,0:T(2,128)} %refs_3_.7, ...), custom_call_target="tpu_custom_call", output_to_operand_aliasing={{}: (8, {})} | custom-call | flops 130459631616 | bytes 28311552 | tf_op jit(solution)/shard_map/mlp/pallas_call | solution.py:472
  371.5 75.4 %qkv.7 = (bf16[1536,4096]{1,0:T(8,128)(2,1)}, bf16[16,4096,128]{2,1,0:T(8,128)(2,1)}, bf16[1536,4096]{1,0:T(8,128)(2,1)}, f32[16,4096]{1,0:T(8,128)}, f32[16,4096]{1,0:T(8,128)}) custom-call(s32[1]{0:T(128)} %bitcast.refs_0_, bf16[16,256,1536]{2,1,0:T(8,128)(2,1)} %bitcast.12, bf16[16,256,1536]{2,1,0:T(8,128)(2,1)} %bitcast.13, ...), custom_call_target="tpu_custom_call" | custom-call | flops 57982058496 | bytes 62914560 | tf_op jit(solution)/shard_map/qkv/pallas_call | solution.py:184
  446.9 60.0 %attn.5 = (bf16[1536,4096]{1,0:T(8,128)(2,1)}, bf16[13824,1536]{1,0:T(8,128)(2,1)S(1)}) custom-call(bf16[1536,4096]{1,0:T(8,128)(2,1)} %get-tuple-element.64.q_ref, bf16[16,4096,128]{2,1,0:T(8,128)(2,1)} %get-tuple-element.65.k_ref, bf16[1536,4096]{1,0:T(8,128)(2,1)} %get-tuple-element.66.v_ref, f32[16,4096]{1,0:T(8,128)} %get-tuple-element.67.nq_ref, ...), custom_call_target="tpu_custom_call" | custom-call | flops 25769803776 | bytes 56623104 | tf_op jit(solution)/shard_map/attn/pallas_call | solution.py:279
  506.9 192.1 %mlp.5 = bf16[16,256,1536]{2,1,0:T(8,128)(2,1)} custom-call(bf16[4096,1536]{1,0:T(8,128)(2,1)} %mlp.4.refs_0_, bf16[1536,4096]{1,0:T(8,128)(2,1)} %get-tuple-element.69.refs_1_, bf16[13824,1536]{1,0:T(8,128)(2,1)S(1)} %get-tuple-element.70.refs_2_, f32[2,1536]{1,0:T(2,128)} %refs_3_.7, f32[2,1536]{1,0:T(2,128)} %refs_4_.5, f32[2,1536]{1,0:T(2,128)} %refs_5_.13, ...), custom_call_target="tpu_custom_call" | custom-call | flops 173946175488 | bytes 37748736 | tf_op jit(solution)/shard_map/mlp/pallas_call | solution.py:472
  699.1 10.5 %copy.41 = bf16[16,256,1536]{2,1,0:T(8,128)(2,1)} copy(bf16[16,256,1536]{2,1,0:T(8,128)(2,1)} %mlp.5) | data formatting | bytes 25165824
Async XLA Ops:
  2.6 52.9 %collective-permute-start.3 = (bf16[1,256,1536]{2,1,0:T(8,128)(2,1)}, bf16[1,256,1536]{2,1,0:T(8,128)(2,1)}, u32[]{:S(2)}, u32[]{:S(2)}) collective-permute-start(bf16[1,256,1536]{2,1,0:T(8,128)(2,1)} %get-tuple-element.71), channel_id=1, source_target_pairs={{0,3},{1,2},{2,1},{3,0},{4,7},{5,6},{6,5},{7,4}} | collective-permute-start | bytes 2359304 | tf_op jit(solution)/shard_map/ppermute | solution.py:497
  5.4 50.1 %collective-permute-start.2 = (bf16[1,256,1536]{2,1,0:T(8,128)(2,1)}, bf16[1,256,1536]{2,1,0:T(8,128)(2,1)}, u32[]{:S(2)}, u32[]{:S(2)}) collective-permute-start(bf16[1,256,1536]{2,1,0:T(8,128)(2,1)} %get-tuple-element.72), channel_id=1, source_target_pairs={{0,2},{1,3},{2,0},{3,1},{4,6},{5,7},{6,4},{7,5}} | collective-permute-start | bytes 2359304 | tf_op jit(solution)/shard_map/ppermute | solution.py:497
  14.2 131.4 %collective-permute-start = (bf16[3,256,1536]{2,1,0:T(8,128)(2,1)}, bf16[3,256,1536]{2,1,0:T(8,128)(2,1)}, u32[]{:S(2)}, u32[]{:S(2)}) collective-permute-start(bf16[3,256,1536]{2,1,0:T(8,128)(2,1)} %get-tuple-element.38), channel_id=1, source_target_pairs={{0,2},{1,3},{2,0},{3,1},{4,6},{5,7},{6,4},{7,5}} | collective-permute-start | bytes 7077896 | tf_op jit(solution)/shard_map/ppermute | solution.py:497
  15.7 129.9 %collective-permute-start.1 = (bf16[3,256,1536]{2,1,0:T(8,128)(2,1)}, bf16[3,256,1536]{2,1,0:T(8,128)(2,1)}, u32[]{:S(2)}, u32[]{:S(2)}) collective-permute-start(bf16[3,256,1536]{2,1,0:T(8,128)(2,1)} %get-tuple-element.39), channel_id=1, source_target_pairs={{0,3},{1,2},{2,1},{3,0},{4,7},{5,6},{6,5},{7,4}} | collective-permute-start | bytes 7077896 | tf_op jit(solution)/shard_map/ppermute | solution.py:497

commit v6 on v5

--- a/solution.py
+++ b/solution.py
@@ -62,10 +62,9 @@
         store(r, step, (c * lax.rsqrt(var + LN_EPS) * gain + shift).astype(bf16))
 
 
-def start_kernel(tokens, w_hbm, sa, sb, near, w_out, buf, w_sem, in_sem, out_sem, s_sem, r_sem):
+def start_kernel(tokens, sa, sb, near, buf, in_sem, out_sem, s_sem, r_sem):
     dp, me = lax.axis_index("dp"), lax.axis_index("sp")
     peer = me + 1 - 2 * (me % 2)
-    w_copy = pltpu.make_async_copy(w_hbm.at[0], w_out, w_sem)
     swap = pltpu.make_async_remote_copy(
         src_ref=tokens.at[pl.ds(peer * IMAGES, IMAGES)], dst_ref=near, send_sem=s_sem, recv_sem=r_sem, device_id=(dp, peer), device_id_type=MESH)
     far = (lax.rem(me + 2, 4), 3 - me)
@@ -73,7 +72,6 @@
     outs = [pltpu.make_async_copy(buf.at[n], out, out_sem.at[n]) for n, out in enumerate((sa, sb))]
     for c in ins:
         c.start()
-    w_copy.start()
     barrier = pltpu.get_barrier_semaphore()
     pl.semaphore_signal(barrier, inc=1, device_id=(dp, peer), device_id_type=MESH)
     pl.semaphore_wait(barrier, 1)
@@ -84,45 +82,48 @@
     for o in outs:
         o.wait()
     swap.wait()
-    w_copy.wait()
-
-
-def start(tokens, w_t):
+
+
+def start(tokens):
     part = pltpu.HBM((IMAGES - 1, BLK, D), bf16)
     dma = pltpu.SemaphoreType.DMA
     return pl.pallas_call(
         start_kernel,
-        out_shape=(part, part, pltpu.HBM((IMAGES, BLK, D), bf16), pltpu.VMEM((3 * D, D), bf16)),
-        in_specs=[HBM, HBM],
-        out_specs=(HBM, HBM, HBM, VMEM),
-        scratch_shapes=[pltpu.VMEM((2, IMAGES - 1, BLK, D), bf16), dma(()), dma((2,)), dma((2,)), dma(()), dma(())],
-        compiler_params=pltpu.CompilerParams(vmem_limit_bytes=QKV_LIMIT, collective_id=1, has_side_effects=True),
+        out_shape=(part, part, pltpu.HBM((IMAGES, BLK, D), bf16)),
+        in_specs=[HBM],
+        out_specs=(HBM, HBM, HBM),
+        scratch_shapes=[pltpu.VMEM((2, IMAGES - 1, BLK, D), bf16), dma((2,)), dma((2,)), dma(()), dma(())],
+        compiler_params=pltpu.CompilerParams(vmem_limit_bytes=60 << 20, collective_id=1, has_side_effects=True),
         cost_estimate=pl.CostEstimate(flops=1 << 30, bytes_accessed=30 << 20, transcendentals=0),
         name="start",
-    )(*at_hbm(tokens), w_t)
-
-
-def qkv_kernel(*refs, layer, n, copy_h, alias, fetch):
+    )(*at_hbm(tokens))
+
+
+def qkv_kernel(*refs, layer, n, copy_h, alias, given, hand):
     (_, xa, xb, xan, xbn, g_ref, s_ref, w, b_ref), refs = refs[:9], refs[9:]
     refs = refs[alias:]
     (q_ref, k_ref, v_ref, nq_ref, nk_ref), refs = refs[:5], refs[5:]
     if copy_h:
         h_ref, refs = refs[0], refs[1:]
-    n_s, n_next = refs[:2]
-    if fetch:
-        w_hbm, w, w_sem = w, refs[2], refs[3]
-        w_copy = pltpu.make_async_copy(w_hbm.at[layer], w, w_sem)
+    if hand:
+        w_hbm, w, refs = w, refs[0], refs[1:]
+    n_s, n_next, sem = refs[:3]
+    if not given and not hand:
+        w_hbm, w = w, refs[3]
     i = pl.program_id(0)
     tm = 2 * BLK
     per = D // CH
     order = (1, 0, 2)
     gain, shift = g_ref[layer:layer + 1, :], s_ref[layer:layer + 1, :]
-
-    def norm(a, b, start, rows):
+    copies = []
+    if not given:
+        parts = ((order[0] * D, CH), (order[0] * D + CH, D - CH), (order[1] * D, D), (order[2] * D, D))
+        copies = [pltpu.make_async_copy(w_hbm.at[layer, r:r + m], w.at[r:r + m], sem.at[p]) for p, (r, m) in enumerate(parts)]
+    def norm(a, b, dst, start, rows):
         def load(r, m):
             return a[0, r:r + m, :] if r < BLK else b[0, r - BLK:r - BLK + m, :]
         def store(r, m, v):
-            n_next[r:r + m, :] = v
+            dst[r:r + m, :] = v
         ln_rows(load, store, gain, shift, start, rows)
 
     def project(o, c):
@@ -149,27 +150,32 @@
                 one = (lax.broadcasted_iota(jnp.int32, (128 - HD, tm), 0) == 0).astype(f32).astype(bf16)
                 k_ref[hh] = jnp.concatenate([yh, one], axis=0).T
 
+    def body(first):
+        for p in range(3 * per):
+            if first and not given and p in (0, 1, per, 2 * per):
+                copies[(0, 1, per, 2 * per).index(p)].wait()
+            project(p // per, p % per)
+            if n > 1 and 0 <= p - 2 < 8:
+                norm(xan, xbn, n_next, (p - 2) * (tm // 8), tm // 8)
+        if copy_h:
+            h_ref[:BLK, :] = xa[0]
+            h_ref[BLK:, :] = xb[0]
+
     @pl.when(i == 0)
     def _():
-        if fetch:
-            w_copy.start()
-        norm(xa, xb, 0, tm)
-        if fetch:
-            w_copy.wait()
-
-    n_s[...] = n_next[...]
-    for o in range(3):
-        for c in range(per):
-            project(o, c)
-            m = o * per + c - 2
-            if n > 1 and 0 <= m < 8:
-                norm(xan, xbn, m * (tm // 8), tm // 8)
-    if copy_h:
-        h_ref[:BLK, :] = xa[0]
-        h_ref[BLK:, :] = xb[0]
-
-
-def qkv(par, xa, xa_map, xb, xb_map, g, s, w, b, layer, n, out_block, copy_h, into=None, after=None):
+        for c in copies:
+            c.start()
+        norm(xa, xb, n_s, 0, tm)
+        body(True)
+
+    if n > 1:
+        @pl.when(i > 0)
+        def _():
+            n_s[...] = n_next[...]
+            body(False)
+
+
+def qkv(par, xa, xa_map, xb, xb_map, g, s, w, b, layer, n, out_block, copy_h, into=None, after=None, given=False, hand=False):
     tm = 2 * BLK
     last = n - 1
     piece = lambda f, d: pl.BlockSpec((1, BLK, D), lambda i, m: (f(jnp.minimum(i + d, last), m), 0, 0))
@@ -179,29 +185,34 @@
     if copy_h:
         shapes.append(pltpu.HBM((T, D), bf16))
         specs.append(pl.BlockSpec((tm, D), lambda i, m: (out_block(i), 0)))
-    extra = list(into or ()) + ([after] if after is not None else [])
-    fetch = w.ndim == 3
+    scratch = [pltpu.VMEM((tm, D), bf16), pltpu.VMEM((tm, D), bf16), pltpu.SemaphoreType.DMA((4,))]
+    if hand:
+        shapes.append(pltpu.VMEM((3 * D, D), bf16))
+        specs.append(VMEM)
+    elif not given:
+        scratch.append(pltpu.VMEM((3 * D, D), bf16))
+    into = list(into or ())
+    extra = into + ([after] if after is not None else [])
     return pl.pallas_call(
-        functools.partial(qkv_kernel, layer=layer, n=n, copy_h=copy_h, alias=len(extra), fetch=fetch),
+        functools.partial(qkv_kernel, layer=layer, n=n, copy_h=copy_h, alias=len(extra), given=given, hand=hand),
         out_shape=tuple(shapes),
         grid_spec=pltpu.PrefetchScalarGridSpec(
             num_scalar_prefetch=1, grid=(n,),
-            in_specs=[piece(xa_map, 0), piece(xb_map, 0), piece(xa_map, 1), piece(xb_map, 1), whole((2, D)), whole((2, D)), HBM if fetch else VMEM,
+            in_specs=[piece(xa_map, 0), piece(xb_map, 0), piece(xa_map, 1), piece(xb_map, 1), whole((2, D)), whole((2, D)), VMEM if given else HBM,
                       whole(b.shape)] + [HBM] * len(extra),
             out_specs=tuple(specs),
-            scratch_shapes=[pltpu.VMEM((tm, D), bf16), pltpu.VMEM((tm, D), bf16)]
-            + ([pltpu.VMEM((3 * D, D), bf16), pltpu.SemaphoreType.DMA(())] if fetch else [])),
-        input_output_aliases={9 + a: a for a in range(len(into or ()))},
-        compiler_params=pltpu.CompilerParams(vmem_limit_bytes=63 << 20 if fetch else QKV_LIMIT, dimension_semantics=("arbitrary",)),
+            scratch_shapes=scratch),
+        input_output_aliases={9 + a: a for a in range(len(into))},
+        compiler_params=pltpu.CompilerParams(vmem_limit_bytes=QKV_LIMIT if given or hand else 63 << 20, dimension_semantics=("arbitrary",)),
         cost_estimate=pl.CostEstimate(flops=2 * n * tm * D * 3 * D, bytes_accessed=n * tm * D * 10, transcendentals=0),
         name="qkv",
-    )(par, *at_hbm(xa, xb, xa, xb), *at_hbm(g, s), *(at_hbm(w) if fetch else at_vmem(w)), *at_hbm(b), *extra)
+    )(par, *at_hbm(xa, xb, xa, xb, g, s), *(at_vmem(w) if given else at_hbm(w)), *at_hbm(b), *extra)
 
 
 def attn_kernel(q_ref, k_ref, v_ref, nq_ref, nk_ref, wo_hbm, wu_hbm, wd_hbm, o_ref, wb, sem, *, layer, hp, nq, kb, lag):
     step = pl.program_id(0) * pl.num_programs(1) + pl.program_id(1)
     parts = [wo_hbm.at[layer]] + [wu_hbm.at[layer, :, c * D:(c + 1) * D] for c in range(F // D)] + [wd_hbm.at[layer]]
-    copies = [pltpu.make_async_copy(p, wb.at[c * D:(c + 1) * D] if c <= F // D else wb.at[(1 + F // D) * D:], sem.at[c]) for c, p in enumerate(parts)]
+    copies = [pltpu.make_async_copy(p, wb.at[c * D:(c + 1) * D] if c < len(parts) - 1 else wb.at[c * D:], sem.at[c]) for c, p in enumerate(parts)]
 
     @pl.when(step == 0)
     def _():
@@ -294,15 +305,15 @@
     return (0.5 * u) * (1.0 + jnp.tanh(u * (c + (c * 0.044715) * (u * u))))
 
 
-def mlp_kernel(*refs, layer, base, n, fc, nc, alias, send, fetch):
-    (x_hbm, o_hbm, wb, bo_ref, g_ref, s_ref, bu_ref, bd_ref), refs = refs[:8], refs[8:]
-    if fetch is not None:
-        wq_hbm, refs = refs[0], refs[1:]
-    refs = refs[alias:]
+def mlp_kernel(*refs, layer, base, n, fc, nc, alias, send):
+    (x_hbm, o_hbm, bo_ref, g_ref, s_ref, bu_ref, bd_ref), refs = refs[:7], refs[7:]
+    wb, refs = refs[0], refs[1 + alias:]
     out_ref, refs = refs[0], refs[1:]
-    if fetch is not None:
-        wq, refs = refs[0], refs[1:]
-    (xb, ob, m_s, n_s, act, acc, xsem, osem, wsem), refs = refs[:9], refs[9:]
+    (xb, ob, m_s, n_s, act, acc, xsem, osem), refs = refs[:8], refs[8:]
+
+    def w(b, cs):
+        return wb[b * D:(b + 1) * D, cs]
+
     i = pl.program_id(0)
     tm = BLK
     assert fc == D
@@ -324,9 +335,6 @@
         slot = g % 2
         return pltpu.make_async_copy(o_hbm.at[:, pl.ds(pl.multiple_of(block(g) * tm, tm), tm)], ob.at[slot], osem.at[slot])
 
-    if fetch is not None:
-        wq_copy = pltpu.make_async_copy(wq_hbm.at[fetch], wq, wsem)
-
     if send:
         out_v, ssem, rsem = refs
         dp, me = lax.axis_index("dp"), lax.axis_index("sp")
@@ -357,7 +365,7 @@
 
     def project(slot):
         for c in range(D // nc):
-            y = dot_tn(ob[slot], wb[:D, cols(c)])
+            y = dot_tn(ob[slot], w(0, cols(c)))
             m_s[:, cols(c)] = (xb[slot, :, cols(c)].astype(f32) + (y + bo[:, cols(c)])).astype(bf16)
 
     def norm():
@@ -371,8 +379,6 @@
         o_copy(0).start()
         x_copy(1).start()
         o_copy(1).start()
-        if fetch is not None:
-            wq_copy.start()
         if send:
             barrier = pltpu.get_barrier_semaphore()
             for k in range(1, 4):
@@ -408,10 +414,10 @@
 
     def up(j, c):
         f0 = j * fc + c * nc
-        act[j % 2, :, cols(c)] = gelu(dot(n_s[...], wb[D * (1 + j):D * (2 + j), cols(c)]) + bu_ref[one, f0:f0 + nc]).astype(bf16)
+        act[j % 2, :, cols(c)] = gelu(dot(n_s[...], w(1 + j, cols(c))) + bu_ref[one, f0:f0 + nc]).astype(bf16)
 
     def down(j, c):
-        y = dot(act[j % 2], wb[D + F + j * fc:D + F + (j + 1) * fc, cols(c)])
+        y = dot(act[j % 2], w(1 + nj + j, cols(c)))
         if j == 0:
             acc[:, cols(c)] = (m_s[:, cols(c)].astype(f32) + bd_ref[one, cols(c)]) + y
         elif j < nj - 1:
@@ -432,11 +438,9 @@
         down(nj - 1, c)
     norm()
 
-    @pl.when(i == n - 1)
-    def _():
-        if fetch is not None:
-            wq_copy.wait()
-        if send:
+    if send:
+        @pl.when(i == n - 1)
+        def _():
             local(n - 1).start()
             for g in range(n - slots, 3 * IMAGES):
                 remote(g).wait_send()
@@ -446,41 +450,34 @@
                 remote(g).wait_recv()
 
 
-def mlp(x, o, w, bo, g, s, bu, bd, layer, first, count, into=None, send=False, fetch=None, w_t=None, fc=1536, nc=512):
+def mlp(x, o, w, bo, g, s, bu, bd, layer, first, count, into=None, send=False, fc=1536, nc=512):
     n = count * SEQ // BLK
     base = first * SEQ // BLK
     dma = pltpu.SemaphoreType.DMA
     vm = pltpu.VMEM
-    sd = jax.ShapeDtypeStruct
     scratch = [vm((2, BLK, D), bf16), vm((2, D, BLK), bf16), vm((BLK, D), bf16), vm((BLK, D), bf16), vm((2, BLK, fc), bf16), vm((BLK, D), f32),
-               dma((2,)), dma((2,)), dma(())]
+               dma((2,)), dma((2,))]
     params = dict(dimension_semantics=("arbitrary",))
     if send:
         scratch += [vm((8, BLK, D), bf16), dma((n,)), dma((3 * IMAGES,))]
-        out_shape, out_spec = [sd((4 * IMAGES, BLK, D), bf16)], [HBM]
+        out_shape, out_spec = jax.ShapeDtypeStruct((4 * IMAGES, BLK, D), bf16), HBM
         params.update(collective_id=0, has_side_effects=True)
     else:
-        out_shape, out_spec = [pltpu.HBM((T, D), bf16)], [pl.BlockSpec((BLK, D), lambda i: (base + i, 0))]
-    extra = []
-    if fetch is not None:
-        extra.append(w_t)
-        out_shape.append(pltpu.VMEM((3 * D, D), bf16))
-        out_spec.append(VMEM)
-    if into is not None:
-        extra.append(into)
+        out_shape, out_spec = pltpu.HBM((T, D), bf16), pl.BlockSpec((BLK, D), lambda i: (base + i, 0))
+    extra = [] if into is None else [into]
     tok = n * BLK
     return pl.pallas_call(
-        functools.partial(mlp_kernel, layer=layer, base=base, n=n, fc=fc, nc=nc, alias=into is not None, send=send, fetch=fetch),
+        functools.partial(mlp_kernel, layer=layer, base=base, n=n, fc=fc, nc=nc, alias=len(extra), send=send),
         out_shape=out_shape,
         grid=(n,),
-        in_specs=[HBM, HBM, VMEM, whole((2, D)), whole((2, D)), whole((2, D)), whole((2, F)), whole((2, D))] + [HBM] * len(extra),
+        in_specs=[HBM, HBM, whole((2, D)), whole((2, D)), whole((2, D)), whole((2, F)), whole((2, D))] + [VMEM] + [HBM] * len(extra),
         out_specs=out_spec,
         scratch_shapes=scratch,
-        input_output_aliases={7 + len(extra): 0} if into is not None else {},
+        input_output_aliases={8: 0} if extra else {},
         compiler_params=pltpu.CompilerParams(vmem_limit_bytes=LAYER_LIMIT, **params),
         cost_estimate=pl.CostEstimate(flops=2 * tok * D * (2 * F + D), bytes_accessed=tok * D * 6, transcendentals=tok * F),
         name="mlp",
-    )(*at_hbm(x, o), *at_vmem(w), *at_hbm(bo, g, s, bu, bd), *extra)
+    )(*at_hbm(x, o, bo, g, s, bu, bd), *at_vmem(w), *extra)
 
 
 def solution(mesh):
@@ -500,26 +497,26 @@
             return lax.dynamic_slice_in_dim(image_tokens, (me ^ k) * IMAGES + first, count)
 
         far_a, far_b = exchange(2, images(2, 0, 1)), exchange(3, images(3, 0, 1))
-        rest_a, rest_b, near, wq = start(image_tokens, w_t)
+        rest_a, rest_b, near = start(image_tokens)
         rest_a, rest_b = exchange(2, rest_a), exchange(3, rest_b)
 
         here = lambda i, m: i
         pre = (ln1_gain, ln1_shift)
-        fold = (w_o, w_up, w_down)
-
-        def post(l, o, w, *place, **kw):
+        others = (w_o, w_up, w_down)
+
+        def post(x, l, o, w, *place, **kw):
             return mlp(x, o, w, b_out, ln2_gain, ln2_shift, b_up, b_down, l, *place, **kw)
 
-        bufs = qkv(par, image_tokens, lambda i, m: m[0] * IMAGES + i, near, here, *pre, wq, b_qkv, 0, IMAGES, lambda i: 2 * i, True)
-        bufs = qkv(par, far_a, here, far_b, here, *pre, wq, b_qkv, 0, 1, lambda i: 1, True, into=bufs)
-        x = bufs[5]
-        h, = post(0, *attn(*bufs[:5], *fold, 0, 0, 1), 0, 1)
+        *bufs, wq = qkv(par, image_tokens, lambda i, m: m[0] * IMAGES + i, near, here, *pre, w_t, b_qkv, 0, IMAGES, lambda i: 2 * i, True, hand=True)
+        bufs = qkv(par, far_a, here, far_b, here, *pre, wq, b_qkv, 0, 1, lambda i: 1, True, into=bufs, given=True)
+        o, wb = attn(*bufs[:5], *others, 0, 0, 1)
+        h = post(bufs[5], 0, o, wb, 0, 1)
         bufs = qkv(par, rest_a, here, rest_b, here, *pre, w_t, b_qkv, 0, IMAGES - 1, lambda i: 2 * i + 3, True, into=bufs, after=h)
-        x = bufs[5]
-        h, = post(0, *attn(*bufs[:5], *fold, 0, 1, IMAGES - 1), 1, IMAGES - 1, into=h)
+        o, wb = attn(*bufs[:5], *others, 0, 1, IMAGES - 1)
+        h = post(bufs[5], 0, o, wb, 1, IMAGES - 1, into=h)
         x = h.reshape(4 * IMAGES, BLK, D)
         bufs = qkv(par, x, lambda i, m: 2 * i, x, lambda i, m: 2 * i + 1, *pre, w_t, b_qkv, 1, 2 * IMAGES, lambda i: i, False)
-        x = h
-        return post(1, *attn(*bufs[:5], *fold, 1, 0, IMAGES), 0, IMAGES, send=True)[0]
+        o, wb = attn(*bufs[:5], *others, 1, 0, IMAGES)
+        return post(h, 1, o, wb, 0, IMAGES, send=True)
 
     return jax.shard_map(device_step, mesh=mesh, in_specs=(token_spec,) + (P(),) * 12, out_specs=token_spec, check_vma=False)

time: 716 us -> 714 us (level)
  no operation moved by 1% of the time
where the time goes in v6:
time: 714 us; the launch traced here: 703 us
  Pallas kernels  685 us (96%)
  local copies, waits for them, and re-layouts  13.1 us (2%)
    pallas_call x3, Pallas kernels, mlp(): pl.pallas_call(functools.partial(mlp_kernel, layer=layer, base=base, n=n,...  388 us
    pallas_call x4, Pallas kernels, qkv(): pl.pallas_call(functools.partial(qkv_kernel, layer=layer, n=n, copy_h=cop...  161 us
    pallas_call x3, Pallas kernels, attn(): pl.pallas_call(functools.partial(attn_kernel, layer=layer, hp=hp, nq=nq,...  130 us
  transfers between devices with their start and end apart: 4, of which 0 were waited for; matrix products, arithmetic and copies ran while one was open for 0% of the time, Pallas kernels for 19%

profile of v6, /device:TPU:0, one launch (start us, length us, event | category | flops | bytes accessed | tf_op | source)
XLA Modules:
  0.0 703.5 jit_solution(10937911864956917617)
XLA Ops:
  0.0 2.6 constant_dynamic-slice_fusion
  2.6 2.8 collective-permute-start.3
  5.4 0.6 collective-permute-start.2
  6.0 5.7 start.1
  11.7 1.6 collective-permute-start
  13.2 0.0 collective-permute-start.1
  13.2 41.2 %qkv.4 = (bf16[1536,4096]{1,0:T(8,128)(2,1)}, bf16[16,4096,128]{2,1,0:T(8,128)(2,1)}, bf16[1536,4096]{1,0:T(8,128)(2,1)}, f32[16,4096]{1,0:T(8,128)}, f32[16,409...) custom-call(s32[1]{0:T(128)} %bitcast.refs_0_, bf16[16,256,1536]{2,1,0:T(8,128)(2,1)} %refs_3_.4, ...), custom_call_target="tpu_custom_call" | custom-call | flops 28991029248 | bytes 31457280 | tf_op jit(solution)/shard_map/qkv/pallas_call | solution.py:196
  54.4 0.0 collective-permute-done.3.refs_2_.refs_4_
  54.4 0.0 collective-permute-done.2.refs_1_.refs_3_
  54.4 13.0 %qkv.5 = (bf16[1536,4096]{1,0:T(8,128)(2,1)}, bf16[16,4096,128]{2,1,0:T(8,128)(2,1)}, bf16[1536,4096]{1,0:T(8,128)(2,1)}, f32[16,4096]{1,0:T(8,128)}, f32[16,4096]{1,0:T(8,128)}, /*index=5*/bf16[4096,1536]{1,0:T(8,128)(2,1)}) custom-call(s32[1]{0:T(128)} %bitcast.refs_0_, ...), custom_call_target="tpu_custom_call", output_to_operand_aliasing={{0}: (9, {}), {1}: (10, {}), {2}: (11, {}), {3}: (12, {}), ... | custom-call | flops 7247757312 | bytes 7864320 | tf_op jit(solution)/shard_map/qkv/pallas_call | solution.py:196
  67.4 25.1 %attn.3 = (bf16[1536,1024]{1,0:T(8,128)(2,1)}, bf16[13824,1536]{1,0:T(8,128)(2,1)S(1)}) custom-call(bf16[1536,4096]{1,0:T(8,128)(2,1)} %get-tuple-element.48.q_ref.refs_9_, bf16[16,4096,128]{2,1,0:T(8,128)(2,1)} %get-tuple-element.49.k_ref.refs_10_, bf16[1536,4096]{1,0:T(8,128)(2,1)} %get-tuple-element.50.v_ref.refs_11_, ...), custom_call_target="tpu_custom_call" | custom-call | flops 6442450944 | bytes 14155776 | tf_op jit(solution)/shard_map/attn/pallas_call | solution.py:290
  92.5 51.8 %mlp.3.refs_15_.refs_8_ = bf16[4096,1536]{1,0:T(8,128)(2,1)} custom-call(bf16[4096,1536]{1,0:T(8,128)(2,1)} %get-tuple-element.53.refs_0_.refs_14_, bf16[1536,1024]{1,0:T(8,128)(2,1)} %get-tuple-element.54.refs_1_, f32[2,1536]{1,0:T(2,128)} %refs_2_.5, f32[2,1536]{1,0:T(2,128)} %refs_3_.7, f32[2,1536]{1,0:T(2,128)} %refs_4_.5, f32[2,6144]{1,0:T(2,128)} %refs_5_.13, ...), custom_call_target="tpu_custom_call" | custom-call | flops 43486543872 | bytes 9437184 | tf_op jit(solution)/shard_map/mlp/pallas_call | solution.py:469
  144.3 0.0 collective-permute-done.refs_1_.refs_3_
  144.3 0.0 collective-permute-done.1.refs_2_.refs_4_
  144.3 33.3 %qkv.6 = (bf16[1536,4096]{1,0:T(8,128)(2,1)}, bf16[16,4096,128]{2,1,0:T(8,128)(2,1)}, bf16[1536,4096]{1,0:T(8,128)(2,1)}, f32[16,4096]{1,0:T(8,128)}, f32[16,4096]{1,0:T(8,128)}, /*index=5*/bf16[4096,1536]{1,0:T(8,128)(2,1)}) custom-call(s32[1]{0:T(128)} %bitcast.refs_0_, ...), custom_call_target="tpu_custom_call", output_to_operand_aliasing={{0}: (9, {}), {1}: (10, {}), {2}: (11, {}), {3}: (12, {}), ... | custom-call | flops 21743271936 | bytes 23592960 | tf_op jit(solution)/shard_map/qkv/pallas_call | solution.py:196
  177.6 45.6 %attn.4 = (bf16[1536,3072]{1,0:T(8,128)(2,1)}, bf16[13824,1536]{1,0:T(8,128)(2,1)S(1)}) custom-call(bf16[1536,4096]{1,0:T(8,128)(2,1)} %get-tuple-element.57.q_ref, bf16[16,4096,128]{2,1,0:T(8,128)(2,1)} %get-tuple-element.58.k_ref, bf16[1536,4096]{1,0:T(8,128)(2,1)} %get-tuple-element.59.v_ref, f32[16,4096]{1,0:T(8,128)} %get-tuple-element.60.nq_ref, ...), custom_call_target="tpu_custom_call" | custom-call | flops 19327352832 | bytes 42467328 | tf_op jit(solution)/shard_map/attn/pallas_call | solution.py:290
  223.2 144.1 %mlp.4.refs_0_ = bf16[4096,1536]{1,0:T(8,128)(2,1)} custom-call(bf16[4096,1536]{1,0:T(8,128)(2,1)} %get-tuple-element.56.refs_0_, bf16[1536,3072]{1,0:T(8,128)(2,1)} %get-tuple-element.62.refs_1_, f32[2,1536]{1,0:T(2,128)} %refs_2_.5, f32[2,1536]{1,0:T(2,128)} %refs_3_.7, f32[2,1536]{1,0:T(2,128)} %refs_4_.5, ...), custom_call_target="tpu_custom_call", output_to_operand_aliasing={{}: (8, {})} | custom-call | flops 130459631616 | bytes 28311552 | tf_op jit(solution)/shard_map/mlp/pallas_call | solution.py:469
  367.4 73.7 %qkv.7 = (bf16[1536,4096]{1,0:T(8,128)(2,1)}, bf16[16,4096,128]{2,1,0:T(8,128)(2,1)}, bf16[1536,4096]{1,0:T(8,128)(2,1)}, f32[16,4096]{1,0:T(8,128)}, f32[16,4096]{1,0:T(8,128)}) custom-call(s32[1]{0:T(128)} %bitcast.refs_0_, bf16[16,256,1536]{2,1,0:T(8,128)(2,1)} %bitcast.12, bf16[16,256,1536]{2,1,0:T(8,128)(2,1)} %bitcast.13, ...), custom_call_target="tpu_custom_call" | custom-call | flops 57982058496 | bytes 62914560 | tf_op jit(solution)/shard_map/qkv/pallas_call | solution.py:196
  441.1 59.6 %attn.5 = (bf16[1536,4096]{1,0:T(8,128)(2,1)}, bf16[13824,1536]{1,0:T(8,128)(2,1)S(1)}) custom-call(bf16[1536,4096]{1,0:T(8,128)(2,1)} %get-tuple-element.64.q_ref, bf16[16,4096,128]{2,1,0:T(8,128)(2,1)} %get-tuple-element.65.k_ref, bf16[1536,4096]{1,0:T(8,128)(2,1)} %get-tuple-element.66.v_ref, f32[16,4096]{1,0:T(8,128)} %get-tuple-element.67.nq_ref, ...), custom_call_target="tpu_custom_call" | custom-call | flops 25769803776 | bytes 56623104 | tf_op jit(solution)/shard_map/attn/pallas_call | solution.py:290
  500.7 191.9 %mlp.5 = bf16[16,256,1536]{2,1,0:T(8,128)(2,1)} custom-call(bf16[4096,1536]{1,0:T(8,128)(2,1)} %mlp.4.refs_0_, bf16[1536,4096]{1,0:T(8,128)(2,1)} %get-tuple-element.69.refs_1_, f32[2,1536]{1,0:T(2,128)} %refs_2_.5, f32[2,1536]{1,0:T(2,128)} %refs_3_.7, f32[2,1536]{1,0:T(2,128)} %refs_4_.5, f32[2,6144]{1,0:T(2,128)} %refs_5_.13, f32[2,1536]{1,0:T(2,128)} %refs_6_.13, ...), custom_call_target="tpu_custom_call" | custom-call | flops 173946175488 | bytes 37748736 | tf_op jit(solution)/shard_map/mlp/pallas_call | solution.py:469
  692.6 10.5 %copy.41 = bf16[16,256,1536]{2,1,0:T(8,128)(2,1)} copy(bf16[16,256,1536]{2,1,0:T(8,128)(2,1)} %mlp.5) | data formatting | bytes 25165824
Async XLA Ops:
  2.6 51.8 %collective-permute-start.3 = (bf16[1,256,1536]{2,1,0:T(8,128)(2,1)}, bf16[1,256,1536]{2,1,0:T(8,128)(2,1)}, u32[]{:S(2)}, u32[]{:S(2)}) collective-permute-start(bf16[1,256,1536]{2,1,0:T(8,128)(2,1)} %get-tuple-element.71), channel_id=1, source_target_pairs={{0,3},{1,2},{2,1},{3,0},{4,7},{5,6},{6,5},{7,4}} | collective-permute-start | bytes 2359304 | tf_op jit(solution)/shard_map/ppermute | solution.py:494
  5.4 49.0 %collective-permute-start.2 = (bf16[1,256,1536]{2,1,0:T(8,128)(2,1)}, bf16[1,256,1536]{2,1,0:T(8,128)(2,1)}, u32[]{:S(2)}, u32[]{:S(2)}) collective-permute-start(bf16[1,256,1536]{2,1,0:T(8,128)(2,1)} %get-tuple-element.72), channel_id=1, source_target_pairs={{0,2},{1,3},{2,0},{3,1},{4,6},{5,7},{6,4},{7,5}} | collective-permute-start | bytes 2359304 | tf_op jit(solution)/shard_map/ppermute | solution.py:494
  11.7 132.6 %collective-permute-start = (bf16[3,256,1536]{2,1,0:T(8,128)(2,1)}, bf16[3,256,1536]{2,1,0:T(8,128)(2,1)}, u32[]{:S(2)}, u32[]{:S(2)}) collective-permute-start(bf16[3,256,1536]{2,1,0:T(8,128)(2,1)} %get-tuple-element.38), channel_id=1, source_target_pairs={{0,2},{1,3},{2,0},{3,1},{4,6},{5,7},{6,4},{7,5}} | collective-permute-start | bytes 7077896 | tf_op jit(solution)/shard_map/ppermute | solution.py:494
  13.2 131.1 %collective-permute-start.1 = (bf16[3,256,1536]{2,1,0:T(8,128)(2,1)}, bf16[3,256,1536]{2,1,0:T(8,128)(2,1)}, u32[]{:S(2)}, u32[]{:S(2)}) collective-permute-start(bf16[3,256,1536]{2,1,0:T(8,128)(2,1)} %get-tuple-element.39), channel_id=1, source_target_pairs={{0,3},{1,2},{2,1},{3,0},{4,7},{5,6},{6,5},{7,4}} | collective-permute-start | bytes 7077896 | tf_op jit(solution)/shard_map/ppermute | solution.py:494

commit v7 on v6

--- a/solution.py
+++ b/solution.py
@@ -39,6 +39,8 @@
 VMEM = pl.BlockSpec(memory_space=pltpu.VMEM)
 QKV_LIMIT = 50 << 20
 LAYER_LIMIT = 23 << 20
+SEND_LIMIT = 18 << 20
+SLOTS = 3
 
 
 def at_hbm(*arrays):
@@ -284,7 +286,7 @@
         lax.fori_loop(0, hp * (SEQ // qb), body, 0)
 
 
-def attn(q, k, v, nq2, nk2, w_o, w_up, w_down, layer, first, count, hp=8, nq=512, kb=256, lag=3):
+def attn(q, k, v, nq2, nk2, w_o, w_up, w_down, layer, first, count, limit=LAYER_LIMIT, hp=8, nq=512, kb=256, lag=3):
     blk = pl.BlockSpec((hp * HD, SEQ), lambda i, j: (j, first + i))
     nrm = pl.BlockSpec((hp, SEQ), lambda i, j: (j, first + i))
     return pl.pallas_call(
@@ -294,7 +296,7 @@
         in_specs=[blk, pl.BlockSpec((hp, SEQ, 128), lambda i, j: (j, first + i, 0)), blk, nrm, nrm, HBM, HBM, HBM],
         out_specs=(pl.BlockSpec((hp * HD, SEQ), lambda i, j: (j, i)), VMEM),
         scratch_shapes=[pltpu.SemaphoreType.DMA((2 + F // D,))],
-        compiler_params=pltpu.CompilerParams(vmem_limit_bytes=LAYER_LIMIT, dimension_semantics=("arbitrary", "arbitrary")),
+        compiler_params=pltpu.CompilerParams(vmem_limit_bytes=limit, dimension_semantics=("arbitrary", "arbitrary")),
         cost_estimate=pl.CostEstimate(flops=4 * count * SEQ * SEQ * D, bytes_accessed=count * SEQ * D * 9, transcendentals=count * SEQ * SEQ * HEADS),
         name="attn",
     )(*at_hbm(q, k, v, nq2, nk2), w_o, w_up, w_down)
@@ -309,6 +311,8 @@
     (x_hbm, o_hbm, bo_ref, g_ref, s_ref, bu_ref, bd_ref), refs = refs[:7], refs[7:]
     wb, refs = refs[0], refs[1 + alias:]
     out_ref, refs = refs[0], refs[1:]
+    if send:
+        vbuf, refs = refs[0], refs[1:]
     (xb, ob, m_s, n_s, act, acc, xsem, osem), refs = refs[:8], refs[8:]
 
     def w(b, cs):
@@ -321,11 +325,18 @@
     one = slice(layer, layer + 1)
     gain, shift, bo = g_ref[one, :], s_ref[one, :], bo_ref[one, :]
 
+    away = 3 * IMAGES
+
+    def far(g):
+        return g // 3 * 2 + g % 3
+
     def block(g):
         if not send:
             return g
-        p, m = g // IMAGES, g % IMAGES
-        return m * 4 + jnp.where(p < 2, p + 2, 3 - p)
+        f = far(g)
+        k = jnp.where(g >= away, 0, jnp.where(g % 3 == 2, 1, 2 + f // IMAGES))
+        m = jnp.where(g >= away, g - away, jnp.where(g % 3 == 2, g // 3, f % IMAGES))
+        return m * 4 + k
 
     def x_copy(g):
         slot = g % 2
@@ -336,27 +347,24 @@
         return pltpu.make_async_copy(o_hbm.at[:, pl.ds(pl.multiple_of(block(g) * tm, tm), tm)], ob.at[slot], osem.at[slot])
 
     if send:
-        out_v, ssem, rsem = refs
+        ssem, rsem = refs
         dp, me = lax.axis_index("dp"), lax.axis_index("sp")
-        slots = out_v.shape[0]
-
-        def peer(k):
-            return jnp.where(k == 1, me + 1 - 2 * (me % 2), jnp.where(k == 2, lax.rem(me + 2, 4), 3 - me))
-
-        def remote(g):
-            p, m = g // IMAGES, g % IMAGES
-            k = jnp.where(p < 2, p + 2, 3 - p)
+
+        def remote(g, dst, peer):
             return pltpu.make_async_remote_copy(
-                src_ref=out_v.at[g % slots], dst_ref=out_ref.at[me * IMAGES + m], send_sem=ssem.at[g], recv_sem=rsem.at[g],
-                device_id=(dp, peer(k)), device_id_type=MESH)
-
-        def local(g):
-            m = g % IMAGES
-            return pltpu.make_async_copy(out_v.at[g % slots], out_ref.at[me * IMAGES + m], ssem.at[g])
+                src_ref=vbuf.at[g % SLOTS], dst_ref=dst, send_sem=ssem.at[g], recv_sem=rsem.at[g], device_id=(dp, peer), device_id_type=MESH)
+
+        def to_far(g):
+            return remote(g, out_ref.at[far(g)], jnp.where(far(g) < IMAGES, lax.rem(me + 2, 4), 3 - me))
+
+        def to_near(g):
+            return remote(g, out_ref.at[2 * IMAGES + g // 3], me + 1 - 2 * (me % 2))
+
+        slot = jnp.where(i < away, lax.rem(i, SLOTS), SLOTS + i - away)
 
     def put(cs, v):
         if send:
-            out_v[i % slots, :, cs] = v
+            vbuf[slot, :, cs] = v
         else:
             out_ref[:, cs] = v
 
@@ -381,8 +389,8 @@
         o_copy(1).start()
         if send:
             barrier = pltpu.get_barrier_semaphore()
-            for k in range(1, 4):
-                pl.semaphore_signal(barrier, inc=1, device_id=(dp, peer(k)), device_id_type=MESH)
+            for peer in (me + 1 - 2 * (me % 2), lax.rem(me + 2, 4), 3 - me):
+                pl.semaphore_signal(barrier, inc=1, device_id=(dp, peer), device_id_type=MESH)
             pl.semaphore_wait(barrier, 3)
         x_copy(0).wait()
         o_copy(0).wait()
@@ -400,17 +408,19 @@
         o_copy(i + 2).start()
 
     if send:
-        @pl.when(jnp.logical_and(i >= 1, i - 1 < 3 * IMAGES))
+        last = i - 1
+
+        @pl.when(jnp.logical_and(jnp.logical_and(last >= 0, last < away), last % 3 < 2))
         def _():
-            remote(i - 1).start()
-
-        @pl.when(i - 1 >= 3 * IMAGES)
+            to_far(last).start()
+
+        @pl.when(jnp.logical_and(jnp.logical_and(last >= 0, last < away), last % 3 == 2))
         def _():
-            local(i - 1).start()
-
-        @pl.when(i >= slots)
+            to_near(last).start()
+
+        @pl.when(jnp.logical_and(i >= SLOTS, i < away))
         def _():
-            remote(i - slots).wait_send()
+            to_near(i - SLOTS).wait_send()
 
     def up(j, c):
         f0 = j * fc + c * nc
@@ -428,26 +438,22 @@
     for c in range(fc // nc):
         up(0, c)
     for j in range(1, nj):
-        for c in range(max(fc, D) // nc):
-            if c < fc // nc:
-                up(j, c)
-            if c < D // nc:
-                down(j - 1, c)
-    project((i + 1) % 2)
+        if j == nj - 1:
+            project((i + 1) % 2)
+        for c in range(D // nc):
+            up(j, c)
+            down(j - 1, c)
+    norm()
     for c in range(D // nc):
         down(nj - 1, c)
-    norm()
 
     if send:
         @pl.when(i == n - 1)
         def _():
-            local(n - 1).start()
-            for g in range(n - slots, 3 * IMAGES):
-                remote(g).wait_send()
-            for g in range(3 * IMAGES, n):
-                local(g).wait()
-            for g in range(3 * IMAGES):
-                remote(g).wait_recv()
+            for g in range(away - SLOTS, away):
+                to_near(g).wait_send()
+            for g in range(away):
+                (to_near if g % 3 == 2 else to_far)(g).wait_recv()
 
 
 def mlp(x, o, w, bo, g, s, bu, bd, layer, first, count, into=None, send=False, fc=1536, nc=512):
@@ -459,8 +465,9 @@
                dma((2,)), dma((2,))]
     params = dict(dimension_semantics=("arbitrary",))
     if send:
-        scratch += [vm((8, BLK, D), bf16), dma((n,)), dma((3 * IMAGES,))]
-        out_shape, out_spec = jax.ShapeDtypeStruct((4 * IMAGES, BLK, D), bf16), HBM
+        scratch += [dma((3 * IMAGES,)), dma((3 * IMAGES,))]
+        out_shape = (pltpu.HBM((3 * IMAGES, BLK, D), bf16), vm((SLOTS + IMAGES, BLK, D), bf16))
+        out_spec = (HBM, VMEM)
         params.update(collective_id=0, has_side_effects=True)
     else:
         out_shape, out_spec = pltpu.HBM((T, D), bf16), pl.BlockSpec((BLK, D), lambda i: (base + i, 0))
@@ -474,10 +481,42 @@
         out_specs=out_spec,
         scratch_shapes=scratch,
         input_output_aliases={8: 0} if extra else {},
-        compiler_params=pltpu.CompilerParams(vmem_limit_bytes=LAYER_LIMIT, **params),
+        compiler_params=pltpu.CompilerParams(vmem_limit_bytes=SEND_LIMIT if send else LAYER_LIMIT, **params),
         cost_estimate=pl.CostEstimate(flops=2 * tok * D * (2 * F + D), bytes_accessed=tok * D * 6, transcendentals=tok * F),
         name="mlp",
     )(*at_hbm(x, o, bo, g, s, bu, bd), *at_vmem(w), *extra)
+
+
+def finish_kernel(arrived, vbuf, out, buf, in_sem, via_sem, v_sem):
+    me = lax.axis_index("sp")
+    copy = pltpu.make_async_copy
+    owner = (lax.rem(me + 2, 4), 3 - me, me + 1 - 2 * (me % 2))
+    ins = [copy(arrived.at[p * IMAGES:(p + 1) * IMAGES], buf.at[p], in_sem.at[p]) for p in range(3)]
+    outs = [copy(buf.at[p], out.at[pl.ds(o * IMAGES, IMAGES)], via_sem.at[p]) for p, o in enumerate(owner)]
+    own = copy(vbuf.at[SLOTS:], out.at[pl.ds(me * IMAGES, IMAGES)], v_sem)
+    for c in ins:
+        c.start()
+    own.start()
+    for i, o in zip(ins, outs):
+        i.wait()
+        o.start()
+    for c in outs:
+        c.wait()
+    own.wait()
+
+
+def finish(arrived, vbuf):
+    dma = pltpu.SemaphoreType.DMA
+    return pl.pallas_call(
+        finish_kernel,
+        out_shape=jax.ShapeDtypeStruct((4 * IMAGES, BLK, D), bf16),
+        in_specs=[HBM, VMEM],
+        out_specs=HBM,
+        scratch_shapes=[pltpu.VMEM((3, IMAGES, BLK, D), bf16), dma((3,)), dma((3,)), dma(())],
+        compiler_params=pltpu.CompilerParams(vmem_limit_bytes=SEND_LIMIT),
+        cost_estimate=pl.CostEstimate(flops=0, bytes_accessed=24 << 20, transcendentals=0),
+        name="finish",
+    )(*at_hbm(arrived), *at_vmem(vbuf))
 
 
 def solution(mesh):
@@ -516,7 +555,7 @@
         h = post(bufs[5], 0, o, wb, 1, IMAGES - 1, into=h)
         x = h.reshape(4 * IMAGES, BLK, D)
         bufs = qkv(par, x, lambda i, m: 2 * i, x, lambda i, m: 2 * i + 1, *pre, w_t, b_qkv, 1, 2 * IMAGES, lambda i: i, False)
-        o, wb = attn(*bufs[:5], *others, 1, 0, IMAGES)
-        return post(h, 1, o, wb, 0, IMAGES, send=True)
+        o, wb = attn(*bufs[:5], *others, 1, 0, IMAGES, limit=SEND_LIMIT)
+        return finish(*post(h, 1, o, wb, 0, IMAGES, send=True))
 
     return jax.shard_map(device_step, mesh=mesh, in_specs=(token_spec,) + (P(),) * 12, out_specs=token_spec, check_vma=False)

time: 714 us -> 708 us (level)
  local copies, waits for them, and re-layouts: 13.1 us -> 2.64 us
    unnamed x1 -> x0, local copies, waits for them, and re-layouts: 10.5 us -> none
    pallas_call x0 -> x1, Pallas kernels: none -> 8.73 us  [finish(): pl.pallas_call(finish_kernel, out_shape=jax.ShapeDtypeStruct((4 * IMAGES,...]
  transfers between devices with their start and end apart: 4 -> 4, of which waited for: 0 -> 0; matrix products, arithmetic and copies ran while one was open for 0% -> 0% of each run, Pallas kernels for 19% -> 20%
where the time goes in v7:
time: 708 us; the launch traced here: 697 us
  Pallas kernels  689 us (97%)
    pallas_call x3, Pallas kernels, mlp(): pl.pallas_call(functools.partial(mlp_kernel, layer=layer, base=base, n=n,...  384 us
    pallas_call x4, Pallas kernels, qkv(): pl.pallas_call(functools.partial(qkv_kernel, layer=layer, n=n, copy_h=cop...  161 us
    pallas_call x3, Pallas kernels, attn(): pl.pallas_call(functools.partial(attn_kernel, layer=layer, hp=hp, nq=nq,...  130 us
  transfers between devices with their start and end apart: 4, of which 0 were waited for; matrix products, arithmetic and copies ran while one was open for 0% of the time, Pallas kernels for 20%

profile of v7, /device:TPU:0, one launch (start us, length us, event | category | flops | bytes accessed | tf_op | source)
XLA Modules:
  0.0 697.5 jit_solution(14308998369636796315)
XLA Ops:
  0.0 2.6 constant_dynamic-slice_fusion
  2.6 2.8 collective-permute-start.3
  5.4 0.6 collective-permute-start.2
  6.0 5.7 start.1
  11.7 1.6 collective-permute-start
  13.2 0.0 collective-permute-start.1
  13.2 41.2 %qkv.4 = (bf16[1536,4096]{1,0:T(8,128)(2,1)}, bf16[16,4096,128]{2,1,0:T(8,128)(2,1)}, bf16[1536,4096]{1,0:T(8,128)(2,1)}, f32[16,4096]{1,0:T(8,128)}, f32[16,409...) custom-call(s32[1]{0:T(128)} %bitcast.refs_0_, bf16[16,256,1536]{2,1,0:T(8,128)(2,1)} %refs_3_.4, ...), custom_call_target="tpu_custom_call" | custom-call | flops 28991029248 | bytes 31457280 | tf_op jit(solution)/shard_map/qkv/pallas_call | solution.py:198
  54.4 0.0 collective-permute-done.3.refs_2_.refs_4_
  54.4 0.0 collective-permute-done.2.refs_1_.refs_3_
  54.4 12.8 %qkv.5 = (bf16[1536,4096]{1,0:T(8,128)(2,1)}, bf16[16,4096,128]{2,1,0:T(8,128)(2,1)}, bf16[1536,4096]{1,0:T(8,128)(2,1)}, f32[16,4096]{1,0:T(8,128)}, f32[16,4096]{1,0:T(8,128)}, /*index=5*/bf16[4096,1536]{1,0:T(8,128)(2,1)}) custom-call(s32[1]{0:T(128)} %bitcast.refs_0_, ...), custom_call_target="tpu_custom_call", output_to_operand_aliasing={{0}: (9, {}), {1}: (10, {}), {2}: (11, {}), {3}: (12, {}), ... | custom-call | flops 7247757312 | bytes 7864320 | tf_op jit(solution)/shard_map/qkv/pallas_call | solution.py:198
  67.3 25.1 %attn.3 = (bf16[1536,1024]{1,0:T(8,128)(2,1)}, bf16[13824,1536]{1,0:T(8,128)(2,1)S(1)}) custom-call(bf16[1536,4096]{1,0:T(8,128)(2,1)} %get-tuple-element.50.q_ref.refs_9_, bf16[16,4096,128]{2,1,0:T(8,128)(2,1)} %get-tuple-element.51.k_ref.refs_10_, bf16[1536,4096]{1,0:T(8,128)(2,1)} %get-tuple-element.52.v_ref.refs_11_, ...), custom_call_target="tpu_custom_call" | custom-call | flops 6442450944 | bytes 14155776 | tf_op jit(solution)/shard_map/attn/pallas_call | solution.py:292
  92.4 51.3 %mlp.3.refs_15_.refs_8_ = bf16[4096,1536]{1,0:T(8,128)(2,1)} custom-call(bf16[4096,1536]{1,0:T(8,128)(2,1)} %get-tuple-element.55.refs_0_.refs_14_, bf16[1536,1024]{1,0:T(8,128)(2,1)} %get-tuple-element.56.refs_1_, f32[2,1536]{1,0:T(2,128)} %refs_2_.5, f32[2,1536]{1,0:T(2,128)} %refs_3_.7, f32[2,1536]{1,0:T(2,128)} %refs_4_.5, f32[2,6144]{1,0:T(2,128)} %refs_5_.13, ...), custom_call_target="tpu_custom_call" | custom-call | flops 43486543872 | bytes 9437184 | tf_op jit(solution)/shard_map/mlp/pallas_call | solution.py:476
  143.7 0.0 collective-permute-done.refs_1_.refs_3_
  143.7 0.0 collective-permute-done.1.refs_2_.refs_4_
  143.7 33.3 %qkv.6 = (bf16[1536,4096]{1,0:T(8,128)(2,1)}, bf16[16,4096,128]{2,1,0:T(8,128)(2,1)}, bf16[1536,4096]{1,0:T(8,128)(2,1)}, f32[16,4096]{1,0:T(8,128)}, f32[16,4096]{1,0:T(8,128)}, /*index=5*/bf16[4096,1536]{1,0:T(8,128)(2,1)}) custom-call(s32[1]{0:T(128)} %bitcast.refs_0_, ...), custom_call_target="tpu_custom_call", output_to_operand_aliasing={{0}: (9, {}), {1}: (10, {}), {2}: (11, {}), {3}: (12, {}), ... | custom-call | flops 21743271936 | bytes 23592960 | tf_op jit(solution)/shard_map/qkv/pallas_call | solution.py:198
  177.0 45.6 %attn.4 = (bf16[1536,3072]{1,0:T(8,128)(2,1)}, bf16[13824,1536]{1,0:T(8,128)(2,1)S(1)}) custom-call(bf16[1536,4096]{1,0:T(8,128)(2,1)} %get-tuple-element.59.q_ref, bf16[16,4096,128]{2,1,0:T(8,128)(2,1)} %get-tuple-element.60.k_ref, bf16[1536,4096]{1,0:T(8,128)(2,1)} %get-tuple-element.61.v_ref, f32[16,4096]{1,0:T(8,128)} %get-tuple-element.62.nq_ref, ...), custom_call_target="tpu_custom_call" | custom-call | flops 19327352832 | bytes 42467328 | tf_op jit(solution)/shard_map/attn/pallas_call | solution.py:292
  222.6 142.8 %mlp.4.refs_0_ = bf16[4096,1536]{1,0:T(8,128)(2,1)} custom-call(bf16[4096,1536]{1,0:T(8,128)(2,1)} %get-tuple-element.58.refs_0_, bf16[1536,3072]{1,0:T(8,128)(2,1)} %get-tuple-element.64.refs_1_, f32[2,1536]{1,0:T(2,128)} %refs_2_.5, f32[2,1536]{1,0:T(2,128)} %refs_3_.7, f32[2,1536]{1,0:T(2,128)} %refs_4_.5, ...), custom_call_target="tpu_custom_call", output_to_operand_aliasing={{}: (8, {})} | custom-call | flops 130459631616 | bytes 28311552 | tf_op jit(solution)/shard_map/mlp/pallas_call | solution.py:476
  365.5 73.7 %qkv.7 = (bf16[1536,4096]{1,0:T(8,128)(2,1)}, bf16[16,4096,128]{2,1,0:T(8,128)(2,1)}, bf16[1536,4096]{1,0:T(8,128)(2,1)}, f32[16,4096]{1,0:T(8,128)}, f32[16,4096]{1,0:T(8,128)}) custom-call(s32[1]{0:T(128)} %bitcast.refs_0_, bf16[16,256,1536]{2,1,0:T(8,128)(2,1)} %bitcast.12, bf16[16,256,1536]{2,1,0:T(8,128)(2,1)} %bitcast.13, ...), custom_call_target="tpu_custom_call" | custom-call | flops 57982058496 | bytes 62914560 | tf_op jit(solution)/shard_map/qkv/pallas_call | solution.py:198
  439.2 59.5 %attn.5 = (bf16[1536,4096]{1,0:T(8,128)(2,1)}, bf16[13824,1536]{1,0:T(8,128)(2,1)S(1)}) custom-call(bf16[1536,4096]{1,0:T(8,128)(2,1)} %get-tuple-element.66.q_ref, bf16[16,4096,128]{2,1,0:T(8,128)(2,1)} %get-tuple-element.67.k_ref, bf16[1536,4096]{1,0:T(8,128)(2,1)} %get-tuple-element.68.v_ref, f32[16,4096]{1,0:T(8,128)} %get-tuple-element.69.nq_ref, ...), custom_call_target="tpu_custom_call" | custom-call | flops 25769803776 | bytes 56623104 | tf_op jit(solution)/shard_map/attn/pallas_call | solution.py:292
  498.8 189.6 %mlp.5 = (bf16[12,256,1536]{2,1,0:T(8,128)(2,1)}, bf16[7,256,1536]{2,1,0:T(8,128)(2,1)S(1)}) custom-call(bf16[4096,1536]{1,0:T(8,128)(2,1)} %mlp.4.refs_0_, bf16[1536,4096]{1,0:T(8,128)(2,1)} %get-tuple-element.71.refs_1_, f32[2,1536]{1,0:T(2,128)} %refs_2_.5, f32[2,1536]{1,0:T(2,128)} %refs_3_.7, f32[2,1536]{1,0:T(2,128)} %refs_4_.5, f32[2,6144]{1,0:T(2,128)} %refs_5_.13, ...), custom_call_target="tpu_custom_call" | custom-call | flops 173946175488 | bytes 37748736 | tf_op jit(solution)/shard_map/mlp/pallas_call | solution.py:476
  688.3 8.7 %finish.1 = bf16[16,256,1536]{2,1,0:T(8,128)(2,1)} custom-call(bf16[12,256,1536]{2,1,0:T(8,128)(2,1)} %get-tuple-element.73.arrived, bf16[7,256,1536]{2,1,0:T(8,128)(2,1)S(1)} %get-tuple-element.74.vbuf), custom_call_target="tpu_custom_call" | custom-call | bytes 25165824 | tf_op jit(solution)/shard_map/finish/pallas_call | solution.py:510
Async XLA Ops:
  2.6 51.8 %collective-permute-start.3 = (bf16[1,256,1536]{2,1,0:T(8,128)(2,1)}, bf16[1,256,1536]{2,1,0:T(8,128)(2,1)}, u32[]{:S(2)}, u32[]{:S(2)}) collective-permute-start(bf16[1,256,1536]{2,1,0:T(8,128)(2,1)} %get-tuple-element.75), channel_id=1, source_target_pairs={{0,3},{1,2},{2,1},{3,0},{4,7},{5,6},{6,5},{7,4}} | collective-permute-start | bytes 2359304 | tf_op jit(solution)/shard_map/ppermute | solution.py:533
  5.4 49.0 %collective-permute-start.2 = (bf16[1,256,1536]{2,1,0:T(8,128)(2,1)}, bf16[1,256,1536]{2,1,0:T(8,128)(2,1)}, u32[]{:S(2)}, u32[]{:S(2)}) collective-permute-start(bf16[1,256,1536]{2,1,0:T(8,128)(2,1)} %get-tuple-element.76), channel_id=1, source_target_pairs={{0,2},{1,3},{2,0},{3,1},{4,6},{5,7},{6,4},{7,5}} | collective-permute-start | bytes 2359304 | tf_op jit(solution)/shard_map/ppermute | solution.py:533
  11.7 132.1 %collective-permute-start = (bf16[3,256,1536]{2,1,0:T(8,128)(2,1)}, bf16[3,256,1536]{2,1,0:T(8,128)(2,1)}, u32[]{:S(2)}, u32[]{:S(2)}) collective-permute-start(bf16[3,256,1536]{2,1,0:T(8,128)(2,1)} %get-tuple-element.40), channel_id=1, source_target_pairs={{0,2},{1,3},{2,0},{3,1},{4,6},{5,7},{6,4},{7,5}} | collective-permute-start | bytes 7077896 | tf_op jit(solution)/shard_map/ppermute | solution.py:533
  13.2 130.5 %collective-permute-start.1 = (bf16[3,256,1536]{2,1,0:T(8,128)(2,1)}, bf16[3,256,1536]{2,1,0:T(8,128)(2,1)}, u32[]{:S(2)}, u32[]{:S(2)}) collective-permute-start(bf16[3,256,1536]{2,1,0:T(8,128)(2,1)} %get-tuple-element.41), channel_id=1, source_target_pairs={{0,3},{1,2},{2,1},{3,0},{4,7},{5,6},{6,5},{7,4}} | collective-permute-start | bytes 7077896 | tf_op jit(solution)/shard_map/ppermute | solution.py:533

commit v8 on v7

--- a/solution.py
+++ b/solution.py
@@ -40,6 +40,7 @@
 QKV_LIMIT = 50 << 20
 LAYER_LIMIT = 23 << 20
 SEND_LIMIT = 18 << 20
+TURNS = 2
 SLOTS = 3
 
 
@@ -109,72 +110,119 @@
         h_ref, refs = refs[0], refs[1:]
     if hand:
         w_hbm, w, refs = w, refs[0], refs[1:]
-    n_s, n_next, sem = refs[:3]
-    if not given and not hand:
-        w_hbm, w = w, refs[3]
+    both, sem = refs[:2]
+    if hand:
+        ahead = refs[2]
+    elif not given:
+        w_hbm, w = w, refs[2]
     i = pl.program_id(0)
     tm = 2 * BLK
     per = D // CH
     order = (1, 0, 2)
     gain, shift = g_ref[layer:layer + 1, :], s_ref[layer:layer + 1, :]
-    copies = []
-    if not given:
-        parts = ((order[0] * D, CH), (order[0] * D + CH, D - CH), (order[1] * D, D), (order[2] * D, D))
-        copies = [pltpu.make_async_copy(w_hbm.at[layer, r:r + m], w.at[r:r + m], sem.at[p]) for p, (r, m) in enumerate(parts)]
-    def norm(a, b, dst, start, rows):
+
+    def w_copy(p, t, row, rows):
+        r = pl.ds(t * D + row, rows)
+        return pltpu.make_async_copy(w_hbm.at[layer, r], w.at[r], sem.at[p])
+
+    def chunk(c, size):
+        return c * size if isinstance(c, int) else pl.multiple_of(c * size, size)
+
+    def norm(src, dst, slot, src_row, dst_row):
         def load(r, m):
-            return a[0, r:r + m, :] if r < BLK else b[0, r - BLK:r - BLK + m, :]
+            return src[0, pl.ds(src_row, m), :]
         def store(r, m, v):
-            dst[r:r + m, :] = v
-        ln_rows(load, store, gain, shift, start, rows)
-
-    def project(o, c):
-        t = order[o]
-        r0, rw = c * CH, t * D + c * CH
-        y = dot_nt(w[rw:rw + CH, :], n_s[...])
-        heads = range(c * (CH // HD), (c + 1) * (CH // HD))
-        bias = b_ref[layer, t].T
-        bias = jnp.concatenate([jnp.broadcast_to(bias[:, h:h + 1], (HD, tm)) for h in heads], axis=0)
+            dst[slot, pl.ds(dst_row, m), :] = v
+        ln_rows(load, store, gain, shift, 0, 16)
+
+    def norm_all(a, b, dst, slot):
+        for r in range(0, BLK, 16):
+            norm(a, dst, slot, r, r)
+        for r in range(0, BLK, 16):
+            norm(b, dst, slot, r, r + BLK)
+
+    def project(t, c, slot):
+        y = dot_nt(w[pl.ds(chunk(c, CH) + t * D, CH), :], both[slot])
+        heads = CH // HD
+        bias = b_ref[layer, t, pl.ds(chunk(c, heads), heads), :].T
+        bias = jnp.concatenate([jnp.broadcast_to(bias[:, h:h + 1], (HD, tm)) for h in range(heads)], axis=0)
         yb = (y + bias).astype(bf16)
+        r0 = pl.ds(chunk(c, CH), CH)
         if t == 2:
-            v_ref[r0:r0 + CH, :] = yb
+            v_ref[r0, :] = yb
             return
         if t == 0:
-            q_ref[r0:r0 + CH, :] = yb
-        for h, hh in enumerate(heads):
+            q_ref[r0, :] = yb
+        for h in range(heads):
             yh = yb[h * HD:(h + 1) * HD, :]
             yf = yh.astype(f32)
             nn = jnp.sum(yf * yf, axis=0, keepdims=True)
             if t == 0:
-                nq_ref[hh:hh + 1, :] = nn
+                nq_ref[pl.ds(c * heads + h, 1), :] = nn
             else:
-                nk_ref[hh:hh + 1, :] = nn
+                nk_ref[pl.ds(c * heads + h, 1), :] = nn
                 one = (lax.broadcasted_iota(jnp.int32, (128 - HD, tm), 0) == 0).astype(f32).astype(bf16)
-                k_ref[hh] = jnp.concatenate([yh, one], axis=0).T
-
-    def body(first):
-        for p in range(3 * per):
-            if first and not given and p in (0, 1, per, 2 * per):
-                copies[(0, 1, per, 2 * per).index(p)].wait()
-            project(p // per, p % per)
-            if n > 1 and 0 <= p - 2 < 8:
-                norm(xan, xbn, n_next, (p - 2) * (tm // 8), tm // 8)
+                k_ref[c * heads + h] = jnp.concatenate([yh, one], axis=0).T
+
+    def keep():
         if copy_h:
             h_ref[:BLK, :] = xa[0]
             h_ref[BLK:, :] = xb[0]
 
+    if hand:
+        copies = lambda part: [w_copy(part * 3 + t, t, part * (D // TURNS), D // TURNS) for t in range(3)]
+
+        @pl.when(i == 0)
+        def _():
+            for part in range(TURNS):
+                for c in copies(part):
+                    c.start()
+            norm_all(xa, xb, ahead, 0)
+
+        both[0] = ahead[0]
+
+        def turn(part, carry):
+            @pl.when(i == 0)
+            def _():
+                for c in copies(part):
+                    c.wait()
+            products = [(t, c) for c in range(per // TURNS) for t in order]
+            half = BLK // TURNS // 16
+            for p, (t, c) in enumerate(products):
+                project(t, part * (per // TURNS) + c, 0)
+                for g in range(p * 2 * half // len(products), (p + 1) * 2 * half // len(products)):
+                    src, base = (xan, 0) if g < half else (xbn, BLK)
+                    at = pl.multiple_of(part * (BLK // TURNS) + g % half * 16, 16)
+                    norm(src, ahead, 0, at, pl.multiple_of(base + at, 16))
+            return carry
+        lax.fori_loop(0, TURNS, turn, 0)
+        keep()
+        return
+
+    parts = {} if given else {0: w_copy(0, order[0], 0, CH), 1: w_copy(1, order[0], CH, D - CH),
+                              per: w_copy(2, order[1], 0, D), 2 * per: w_copy(3, order[2], 0, D)}
+
+    def body(first, now, later):
+        for p in range(3 * per):
+            if first and p in parts:
+                parts[p].wait()
+            project(order[p // per], p % per, now)
+            if n > 1 and 0 <= p - 2 < 8:
+                for r in range((p - 2) * (tm // 8), (p - 1) * (tm // 8), 16):
+                    norm(xan if r < BLK else xbn, both, later, r % BLK, r)
+        keep()
+
     @pl.when(i == 0)
     def _():
-        for c in copies:
+        for c in parts.values():
             c.start()
-        norm(xa, xb, n_s, 0, tm)
-        body(True)
+        norm_all(xa, xb, both, 0)
+        body(True, 0, 1)
 
     if n > 1:
         @pl.when(i > 0)
         def _():
-            n_s[...] = n_next[...]
-            body(False)
+            body(False, lax.rem(i, 2), lax.rem(i + 1, 2))
 
 
 def qkv(par, xa, xa_map, xb, xb_map, g, s, w, b, layer, n, out_block, copy_h, into=None, after=None, given=False, hand=False):
@@ -187,10 +235,11 @@
     if copy_h:
         shapes.append(pltpu.HBM((T, D), bf16))
         specs.append(pl.BlockSpec((tm, D), lambda i, m: (out_block(i), 0)))
-    scratch = [pltpu.VMEM((tm, D), bf16), pltpu.VMEM((tm, D), bf16), pltpu.SemaphoreType.DMA((4,))]
+    scratch = [pltpu.VMEM((1 if hand else 2, tm, D), bf16), pltpu.SemaphoreType.DMA((3 * TURNS if hand else 4,))]
     if hand:
         shapes.append(pltpu.VMEM((3 * D, D), bf16))
         specs.append(VMEM)
+        scratch.append(pltpu.VMEM((1, tm, D), bf16))
     elif not given:
         scratch.append(pltpu.VMEM((3 * D, D), bf16))
     into = list(into or ())

time: 708 us -> 702 us (level)
  no operation moved by 1% of the time
where the time goes in v8:
time: 702 us; the launch traced here: 698 us
  Pallas kernels  689 us (98%)
    pallas_call x3, Pallas kernels, mlp(): pl.pallas_call(functools.partial(mlp_kernel, layer=layer, base=base, n=n,...  384 us
    pallas_call x4, Pallas kernels, qkv(): pl.pallas_call(functools.partial(qkv_kernel, layer=layer, n=n, copy_h=cop...  161 us
    pallas_call x3, Pallas kernels, attn(): pl.pallas_call(functools.partial(attn_kernel, layer=layer, hp=hp, nq=nq,...  130 us
  transfers between devices with their start and end apart: 4, of which 0 were waited for; matrix products, arithmetic and copies ran while one was open for 0% of the time, Pallas kernels for 20%

profile of v8, /device:TPU:0, one launch (start us, length us, event | category | flops | bytes accessed | tf_op | source)
XLA Modules:
  0.0 697.5 jit_solution(11361860579645906151)
XLA Ops:
  0.0 2.6 constant_dynamic-slice_fusion
  2.6 2.8 collective-permute-start.3
  5.4 0.6 collective-permute-start.2
  6.0 5.7 start.1
  11.7 1.6 collective-permute-start
  13.2 0.0 collective-permute-start.1
  13.2 42.4 %qkv.4 = (bf16[1536,4096]{1,0:T(8,128)(2,1)}, bf16[16,4096,128]{2,1,0:T(8,128)(2,1)}, bf16[1536,4096]{1,0:T(8,128)(2,1)}, f32[16,4096]{1,0:T(8,128)}, f32[16,409...) custom-call(s32[1]{0:T(128)} %bitcast.refs_0_, bf16[16,256,1536]{2,1,0:T(8,128)(2,1)} %refs_3_.4, ...), custom_call_target="tpu_custom_call" | custom-call | flops 28991029248 | bytes 31457280 | tf_op jit(solution)/shard_map/qkv/pallas_call | solution.py:247
  55.6 0.0 collective-permute-done.3.refs_2_.refs_4_
  55.6 0.0 collective-permute-done.2.refs_1_.refs_3_
  55.6 12.8 %qkv.5 = (bf16[1536,4096]{1,0:T(8,128)(2,1)}, bf16[16,4096,128]{2,1,0:T(8,128)(2,1)}, bf16[1536,4096]{1,0:T(8,128)(2,1)}, f32[16,4096]{1,0:T(8,128)}, f32[16,4096]{1,0:T(8,128)}, /*index=5*/bf16[4096,1536]{1,0:T(8,128)(2,1)}) custom-call(s32[1]{0:T(128)} %bitcast.refs_0_, ...), custom_call_target="tpu_custom_call", output_to_operand_aliasing={{0}: (9, {}), {1}: (10, {}), {2}: (11, {}), {3}: (12, {}), ... | custom-call | flops 7247757312 | bytes 7864320 | tf_op jit(solution)/shard_map/qkv/pallas_call | solution.py:247
  68.5 25.4 %attn.3 = (bf16[1536,1024]{1,0:T(8,128)(2,1)}, bf16[13824,1536]{1,0:T(8,128)(2,1)S(1)}) custom-call(bf16[1536,4096]{1,0:T(8,128)(2,1)} %get-tuple-element.50.q_ref.refs_9_, bf16[16,4096,128]{2,1,0:T(8,128)(2,1)} %get-tuple-element.51.k_ref.refs_10_, bf16[1536,4096]{1,0:T(8,128)(2,1)} %get-tuple-element.52.v_ref.refs_11_, ...), custom_call_target="tpu_custom_call" | custom-call | flops 6442450944 | bytes 14155776 | tf_op jit(solution)/shard_map/attn/pallas_call | solution.py:341
  93.9 51.4 %mlp.3.refs_15_.refs_8_ = bf16[4096,1536]{1,0:T(8,128)(2,1)} custom-call(bf16[4096,1536]{1,0:T(8,128)(2,1)} %get-tuple-element.55.refs_0_.refs_14_, bf16[1536,1024]{1,0:T(8,128)(2,1)} %get-tuple-element.56.refs_1_, f32[2,1536]{1,0:T(2,128)} %refs_2_.5, f32[2,1536]{1,0:T(2,128)} %refs_3_.7, f32[2,1536]{1,0:T(2,128)} %refs_4_.5, f32[2,6144]{1,0:T(2,128)} %refs_5_.13, ...), custom_call_target="tpu_custom_call" | custom-call | flops 43486543872 | bytes 9437184 | tf_op jit(solution)/shard_map/mlp/pallas_call | solution.py:525
  145.2 0.0 collective-permute-done.refs_1_.refs_3_
  145.2 0.0 collective-permute-done.1.refs_2_.refs_4_
  145.2 32.9 %qkv.6 = (bf16[1536,4096]{1,0:T(8,128)(2,1)}, bf16[16,4096,128]{2,1,0:T(8,128)(2,1)}, bf16[1536,4096]{1,0:T(8,128)(2,1)}, f32[16,4096]{1,0:T(8,128)}, f32[16,4096]{1,0:T(8,128)}, /*index=5*/bf16[4096,1536]{1,0:T(8,128)(2,1)}) custom-call(s32[1]{0:T(128)} %bitcast.refs_0_, ...), custom_call_target="tpu_custom_call", output_to_operand_aliasing={{0}: (9, {}), {1}: (10, {}), {2}: (11, {}), {3}: (12, {}), ... | custom-call | flops 21743271936 | bytes 23592960 | tf_op jit(solution)/shard_map/qkv/pallas_call | solution.py:247
  178.1 45.6 %attn.4 = (bf16[1536,3072]{1,0:T(8,128)(2,1)}, bf16[13824,1536]{1,0:T(8,128)(2,1)S(1)}) custom-call(bf16[1536,4096]{1,0:T(8,128)(2,1)} %get-tuple-element.59.q_ref, bf16[16,4096,128]{2,1,0:T(8,128)(2,1)} %get-tuple-element.60.k_ref, bf16[1536,4096]{1,0:T(8,128)(2,1)} %get-tuple-element.61.v_ref, f32[16,4096]{1,0:T(8,128)} %get-tuple-element.62.nq_ref, ...), custom_call_target="tpu_custom_call" | custom-call | flops 19327352832 | bytes 42467328 | tf_op jit(solution)/shard_map/attn/pallas_call | solution.py:341
  223.7 142.8 %mlp.4.refs_0_ = bf16[4096,1536]{1,0:T(8,128)(2,1)} custom-call(bf16[4096,1536]{1,0:T(8,128)(2,1)} %get-tuple-element.58.refs_0_, bf16[1536,3072]{1,0:T(8,128)(2,1)} %get-tuple-element.64.refs_1_, f32[2,1536]{1,0:T(2,128)} %refs_2_.5, f32[2,1536]{1,0:T(2,128)} %refs_3_.7, f32[2,1536]{1,0:T(2,128)} %refs_4_.5, ...), custom_call_target="tpu_custom_call", output_to_operand_aliasing={{}: (8, {})} | custom-call | flops 130459631616 | bytes 28311552 | tf_op jit(solution)/shard_map/mlp/pallas_call | solution.py:525
  366.5 72.7 %qkv.7 = (bf16[1536,4096]{1,0:T(8,128)(2,1)}, bf16[16,4096,128]{2,1,0:T(8,128)(2,1)}, bf16[1536,4096]{1,0:T(8,128)(2,1)}, f32[16,4096]{1,0:T(8,128)}, f32[16,4096]{1,0:T(8,128)}) custom-call(s32[1]{0:T(128)} %bitcast.refs_0_, bf16[16,256,1536]{2,1,0:T(8,128)(2,1)} %bitcast.12, bf16[16,256,1536]{2,1,0:T(8,128)(2,1)} %bitcast.13, ...), custom_call_target="tpu_custom_call" | custom-call | flops 57982058496 | bytes 62914560 | tf_op jit(solution)/shard_map/qkv/pallas_call | solution.py:247
  439.3 59.5 %attn.5 = (bf16[1536,4096]{1,0:T(8,128)(2,1)}, bf16[13824,1536]{1,0:T(8,128)(2,1)S(1)}) custom-call(bf16[1536,4096]{1,0:T(8,128)(2,1)} %get-tuple-element.66.q_ref, bf16[16,4096,128]{2,1,0:T(8,128)(2,1)} %get-tuple-element.67.k_ref, bf16[1536,4096]{1,0:T(8,128)(2,1)} %get-tuple-element.68.v_ref, f32[16,4096]{1,0:T(8,128)} %get-tuple-element.69.nq_ref, ...), custom_call_target="tpu_custom_call" | custom-call | flops 25769803776 | bytes 56623104 | tf_op jit(solution)/shard_map/attn/pallas_call | solution.py:341
  498.8 189.6 %mlp.5 = (bf16[12,256,1536]{2,1,0:T(8,128)(2,1)}, bf16[7,256,1536]{2,1,0:T(8,128)(2,1)S(1)}) custom-call(bf16[4096,1536]{1,0:T(8,128)(2,1)} %mlp.4.refs_0_, bf16[1536,4096]{1,0:T(8,128)(2,1)} %get-tuple-element.71.refs_1_, f32[2,1536]{1,0:T(2,128)} %refs_2_.5, f32[2,1536]{1,0:T(2,128)} %refs_3_.7, f32[2,1536]{1,0:T(2,128)} %refs_4_.5, f32[2,6144]{1,0:T(2,128)} %refs_5_.13, ...), custom_call_target="tpu_custom_call" | custom-call | flops 173946175488 | bytes 37748736 | tf_op jit(solution)/shard_map/mlp/pallas_call | solution.py:525
  688.4 8.7 %finish.1 = bf16[16,256,1536]{2,1,0:T(8,128)(2,1)} custom-call(bf16[12,256,1536]{2,1,0:T(8,128)(2,1)} %get-tuple-element.73.arrived, bf16[7,256,1536]{2,1,0:T(8,128)(2,1)S(1)} %get-tuple-element.74.vbuf), custom_call_target="tpu_custom_call" | custom-call | bytes 25165824 | tf_op jit(solution)/shard_map/finish/pallas_call | solution.py:559
Async XLA Ops:
  2.6 53.0 %collective-permute-start.3 = (bf16[1,256,1536]{2,1,0:T(8,128)(2,1)}, bf16[1,256,1536]{2,1,0:T(8,128)(2,1)}, u32[]{:S(2)}, u32[]{:S(2)}) collective-permute-start(bf16[1,256,1536]{2,1,0:T(8,128)(2,1)} %get-tuple-element.75), channel_id=1, source_target_pairs={{0,3},{1,2},{2,1},{3,0},{4,7},{5,6},{6,5},{7,4}} | collective-permute-start | bytes 2359304 | tf_op jit(solution)/shard_map/ppermute | solution.py:582
  5.4 50.2 %collective-permute-start.2 = (bf16[1,256,1536]{2,1,0:T(8,128)(2,1)}, bf16[1,256,1536]{2,1,0:T(8,128)(2,1)}, u32[]{:S(2)}, u32[]{:S(2)}) collective-permute-start(bf16[1,256,1536]{2,1,0:T(8,128)(2,1)} %get-tuple-element.76), channel_id=1, source_target_pairs={{0,2},{1,3},{2,0},{3,1},{4,6},{5,7},{6,4},{7,5}} | collective-permute-start | bytes 2359304 | tf_op jit(solution)/shard_map/ppermute | solution.py:582
  11.7 133.6 %collective-permute-start = (bf16[3,256,1536]{2,1,0:T(8,128)(2,1)}, bf16[3,256,1536]{2,1,0:T(8,128)(2,1)}, u32[]{:S(2)}, u32[]{:S(2)}) collective-permute-start(bf16[3,256,1536]{2,1,0:T(8,128)(2,1)} %get-tuple-element.40), channel_id=1, source_target_pairs={{0,2},{1,3},{2,0},{3,1},{4,6},{5,7},{6,4},{7,5}} | collective-permute-start | bytes 7077896 | tf_op jit(solution)/shard_map/ppermute | solution.py:582
  13.2 132.0 %collective-permute-start.1 = (bf16[3,256,1536]{2,1,0:T(8,128)(2,1)}, bf16[3,256,1536]{2,1,0:T(8,128)(2,1)}, u32[]{:S(2)}, u32[]{:S(2)}) collective-permute-start(bf16[3,256,1536]{2,1,0:T(8,128)(2,1)} %get-tuple-element.41), channel_id=1, source_target_pairs={{0,3},{1,2},{2,1},{3,0},{4,7},{5,6},{6,5},{7,4}} | collective-permute-start | bytes 7077896 | tf_op jit(solution)/shard_map/ppermute | solution.py:582

commit v9 on v8

--- a/solution.py
+++ b/solution.py
@@ -37,8 +37,8 @@
 
 
 VMEM = pl.BlockSpec(memory_space=pltpu.VMEM)
-QKV_LIMIT = 50 << 20
-LAYER_LIMIT = 23 << 20
+LAYER_LIMIT = 93 << 18
+EARLY = 6
 SEND_LIMIT = 18 << 20
 TURNS = 2
 SLOTS = 3
@@ -50,6 +50,11 @@
 
 def at_vmem(*arrays):
     return tuple(pltpu.with_memory_space_constraint(a, pltpu.VMEM) for a in arrays)
+
+
+def layer_blocks(layer, wo, wu, wd):
+    cuts = [slice(c * D, (c + 1) * D) for c in range(F // D)]
+    return [wo.at[layer]] + [wu.at[layer, :, c] for c in cuts] + [wd.at[layer, c] for c in cuts]
 
 
 def whole(shape):
@@ -102,17 +107,24 @@
     )(*at_hbm(tokens))
 
 
-def qkv_kernel(*refs, layer, n, copy_h, alias, given, hand):
-    (_, xa, xb, xan, xbn, g_ref, s_ref, w, b_ref), refs = refs[:9], refs[9:]
+def qkv_kernel(*refs, layer, n, copy_h, alias, given, hand, out_block):
+    (_, xa, xb, xan, xbn, g_ref, s_ref), refs = refs[:7], refs[7:]
+    (w, b_ref), refs = refs[given:2 + given], refs[2 + given:]
+    if hand:
+        others, refs = refs[:3], refs[3:]
     refs = refs[alias:]
     (q_ref, k_ref, v_ref, nq_ref, nk_ref), refs = refs[:5], refs[5:]
     if copy_h:
         h_ref, refs = refs[0], refs[1:]
     if hand:
-        w_hbm, w, refs = w, refs[0], refs[1:]
+        w_hbm, wa, w, refs = w, refs[0], refs[1], refs[2:]
+    refs = refs[given:]
+    if copy_h and not given:
+        h_sem, refs = refs[0], refs[1:]
     both, sem = refs[:2]
     if hand:
-        ahead = refs[2]
+        ahead, early_sem = refs[2:]
+        early = [pltpu.make_async_copy(p, wa.at[c * D:(c + 1) * D], early_sem.at[c]) for c, p in enumerate(layer_blocks(layer, *others)[:EARLY])]
     elif not given:
         w_hbm, w = w, refs[2]
     i = pl.program_id(0)
@@ -130,10 +142,10 @@
 
     def norm(src, dst, slot, src_row, dst_row):
         def load(r, m):
-            return src[0, pl.ds(src_row, m), :]
+            return src[0, pl.ds(src_row + r, m), :]
         def store(r, m, v):
-            dst[slot, pl.ds(dst_row, m), :] = v
-        ln_rows(load, store, gain, shift, 0, 16)
+            dst[slot, pl.ds(dst_row + r, m), :] = v
+        ln_rows(load, store, gain, shift, 0, 16, 8 if given else 16)
 
     def norm_all(a, b, dst, slot):
         for r in range(0, BLK, 16):
@@ -164,10 +176,19 @@
                 one = (lax.broadcasted_iota(jnp.int32, (128 - HD, tm), 0) == 0).astype(f32).astype(bf16)
                 k_ref[c * heads + h] = jnp.concatenate([yh, one], axis=0).T
 
+    if copy_h and not given:
+        row = pl.multiple_of(out_block(i) * tm, tm)
+        h_copies = [pltpu.make_async_copy(x.at[0], h_ref.at[pl.ds(row + p * BLK, BLK)], h_sem.at[p]) for p, x in enumerate((xa, xb))]
+        for c in h_copies:
+            c.start()
+
     def keep():
-        if copy_h:
+        if given:
             h_ref[:BLK, :] = xa[0]
             h_ref[BLK:, :] = xb[0]
+        elif copy_h:
+            for c in h_copies:
+                c.wait()
 
     if hand:
         copies = lambda part: [w_copy(part * 3 + t, t, part * (D // TURNS), D // TURNS) for t in range(3)]
@@ -177,6 +198,8 @@
             for part in range(TURNS):
                 for c in copies(part):
                     c.start()
+            for c in early:
+                c.start(priority=1)
             norm_all(xa, xb, ahead, 0)
 
         both[0] = ahead[0]
@@ -197,6 +220,11 @@
             return carry
         lax.fori_loop(0, TURNS, turn, 0)
         keep()
+
+        @pl.when(i == n - 1)
+        def _():
+            for c in early:
+                c.wait()
         return
 
     parts = {} if given else {0: w_copy(0, order[0], 0, CH), 1: w_copy(1, order[0], CH, D - CH),
@@ -214,9 +242,12 @@
 
     @pl.when(i == 0)
     def _():
-        for c in parts.values():
-            c.start()
+        for p in parts:
+            if p < 2 * per:
+                parts[p].start()
         norm_all(xa, xb, both, 0)
+        if not given:
+            parts[2 * per].start()
         body(True, 0, 1)
 
     if n > 1:
@@ -225,45 +256,56 @@
             body(False, lax.rem(i, 2), lax.rem(i + 1, 2))
 
 
-def qkv(par, xa, xa_map, xb, xb_map, g, s, w, b, layer, n, out_block, copy_h, into=None, after=None, given=False, hand=False):
+def qkv(par, xa, xa_map, xb, xb_map, g, s, w, b, layer, n, out_block, copy_h, into=None, after=None, given=None, hand=()):
     tm = 2 * BLK
     last = n - 1
-    piece = lambda f, d: pl.BlockSpec((1, BLK, D), lambda i, m: (f(jnp.minimum(i + d, last), m), 0, 0))
+    held = [] if given is None else [given]
+    chain = bool(held or hand)
+    once = dict(pipeline_mode=pl.Buffered(1))
+    piece = lambda f, d: pl.BlockSpec((1, BLK, D), lambda i, m: (f(jnp.minimum(i + d, last), m), 0, 0), **(once if n == 1 else {}))
     col = lambda r: pl.BlockSpec((r, tm), lambda i, m: (0, out_block(i)))
     shapes = [pltpu.HBM((D, T), bf16), pltpu.HBM((HEADS, T, 128), bf16), pltpu.HBM((D, T), bf16), pltpu.HBM((HEADS, T), f32), pltpu.HBM((HEADS, T), f32)]
     specs = [col(D), pl.BlockSpec((HEADS, tm, 128), lambda i, m: (0, out_block(i), 0)), col(D), col(HEADS), col(HEADS)]
     if copy_h:
         shapes.append(pltpu.HBM((T, D), bf16))
-        specs.append(pl.BlockSpec((tm, D), lambda i, m: (out_block(i), 0)))
-    scratch = [pltpu.VMEM((1 if hand else 2, tm, D), bf16), pltpu.SemaphoreType.DMA((3 * TURNS if hand else 4,))]
+        specs.append(pl.BlockSpec((tm, D), lambda i, m: (out_block(i), 0)) if held else HBM)
+    dma = pltpu.SemaphoreType.DMA
+    scratch = [dma((2,))] * (copy_h and not held) + [pltpu.VMEM((1 if chain else 2, tm, D), bf16), dma((3 * TURNS if hand else 4,))]
     if hand:
-        shapes.append(pltpu.VMEM((3 * D, D), bf16))
+        shapes += [pltpu.VMEM((EARLY * D, D), bf16), pltpu.VMEM((3 * D, D), bf16)]
+        specs += [VMEM, VMEM]
+        scratch += [pltpu.VMEM((1, tm, D), bf16), dma((EARLY,))]
+    elif held:
+        shapes.append(pltpu.VMEM(given.shape, bf16))
         specs.append(VMEM)
-        scratch.append(pltpu.VMEM((1, tm, D), bf16))
-    elif not given:
+    else:
         scratch.append(pltpu.VMEM((3 * D, D), bf16))
     into = list(into or ())
     extra = into + ([after] if after is not None else [])
+    alias = {9 + len(held) + len(hand) + a: a for a in range(len(into))}
+    if held:
+        alias[7] = len(shapes) - 1
     return pl.pallas_call(
-        functools.partial(qkv_kernel, layer=layer, n=n, copy_h=copy_h, alias=len(extra), given=given, hand=hand),
+        functools.partial(qkv_kernel, layer=layer, n=n, copy_h=copy_h, alias=len(extra), given=len(held), hand=bool(hand), out_block=out_block),
         out_shape=tuple(shapes),
         grid_spec=pltpu.PrefetchScalarGridSpec(
             num_scalar_prefetch=1, grid=(n,),
-            in_specs=[piece(xa_map, 0), piece(xb_map, 0), piece(xa_map, 1), piece(xb_map, 1), whole((2, D)), whole((2, D)), VMEM if given else HBM,
-                      whole(b.shape)] + [HBM] * len(extra),
+            in_specs=[piece(xa_map, 0), piece(xb_map, 0), piece(xa_map, 1), piece(xb_map, 1), whole((2, D)), whole((2, D))]
+            + ([VMEM, VMEM] if held else [HBM]) + [whole(b.shape)] + [HBM] * (len(hand) + len(extra)),
             out_specs=tuple(specs),
             scratch_shapes=scratch),
-        input_output_aliases={9 + a: a for a in range(len(into))},
-        compiler_params=pltpu.CompilerParams(vmem_limit_bytes=QKV_LIMIT if given or hand else 63 << 20, dimension_semantics=("arbitrary",)),
+        input_output_aliases=alias,
+        compiler_params=pltpu.CompilerParams(vmem_limit_bytes=LAYER_LIMIT if chain else 63 << 20, dimension_semantics=("arbitrary",)),
         cost_estimate=pl.CostEstimate(flops=2 * n * tm * D * 3 * D, bytes_accessed=n * tm * D * 10, transcendentals=0),
         name="qkv",
-    )(par, *at_hbm(xa, xb, xa, xb, g, s), *(at_vmem(w) if given else at_hbm(w)), *at_hbm(b), *extra)
-
-
-def attn_kernel(q_ref, k_ref, v_ref, nq_ref, nk_ref, wo_hbm, wu_hbm, wd_hbm, o_ref, wb, sem, *, layer, hp, nq, kb, lag):
+    )(par, *at_hbm(xa, xb, xa, xb, g, s), *(at_vmem(*held, w) if held else at_hbm(w)), *at_hbm(b, *hand), *extra)
+
+
+def attn_kernel(q_ref, k_ref, v_ref, nq_ref, nk_ref, wo_hbm, wu_hbm, wd_hbm, *refs, layer, have, hp, nq, kb, lag):
+    o_ref, wb, sem = (refs[1], refs[3], refs[4]) if have else refs
     step = pl.program_id(0) * pl.num_programs(1) + pl.program_id(1)
-    parts = [wo_hbm.at[layer]] + [wu_hbm.at[layer, :, c * D:(c + 1) * D] for c in range(F // D)] + [wd_hbm.at[layer]]
-    copies = [pltpu.make_async_copy(p, wb.at[c * D:(c + 1) * D] if c < len(parts) - 1 else wb.at[c * D:], sem.at[c]) for c, p in enumerate(parts)]
+    parts = layer_blocks(layer, wo_hbm, wu_hbm, wd_hbm)[have:]
+    copies = [pltpu.make_async_copy(p, wb.at[c * D:(c + 1) * D], sem.at[c]) for c, p in enumerate(parts)]
 
     @pl.when(step == 0)
     def _():
@@ -335,20 +377,23 @@
         lax.fori_loop(0, hp * (SEQ // qb), body, 0)
 
 
-def attn(q, k, v, nq2, nk2, w_o, w_up, w_down, layer, first, count, limit=LAYER_LIMIT, hp=8, nq=512, kb=256, lag=3):
+def attn(q, k, v, nq2, nk2, w_o, w_up, w_down, layer, first, count, limit=LAYER_LIMIT, keep=None, hp=8, nq=512, kb=256, lag=3):
+    held = [] if keep is None else [keep]
+    have = EARLY if held else 0
     blk = pl.BlockSpec((hp * HD, SEQ), lambda i, j: (j, first + i))
     nrm = pl.BlockSpec((hp, SEQ), lambda i, j: (j, first + i))
     return pl.pallas_call(
-        functools.partial(attn_kernel, layer=layer, hp=hp, nq=nq, kb=kb, lag=lag),
-        out_shape=(pltpu.HBM((D, count * SEQ), bf16), pltpu.VMEM((D + 2 * F, D), bf16)),
+        functools.partial(attn_kernel, layer=layer, have=have, hp=hp, nq=nq, kb=kb, lag=lag),
+        out_shape=(pltpu.HBM((D, count * SEQ), bf16), *(pltpu.VMEM(a.shape, bf16) for a in held), pltpu.VMEM((D + 2 * F - have * D, D), bf16)),
         grid=(count, HEADS // hp),
-        in_specs=[blk, pl.BlockSpec((hp, SEQ, 128), lambda i, j: (j, first + i, 0)), blk, nrm, nrm, HBM, HBM, HBM],
-        out_specs=(pl.BlockSpec((hp * HD, SEQ), lambda i, j: (j, i)), VMEM),
-        scratch_shapes=[pltpu.SemaphoreType.DMA((2 + F // D,))],
+        in_specs=[blk, pl.BlockSpec((hp, SEQ, 128), lambda i, j: (j, first + i, 0)), blk, nrm, nrm, HBM, HBM, HBM] + [VMEM] * len(held),
+        out_specs=(pl.BlockSpec((hp * HD, SEQ), lambda i, j: (j, i)),) + (VMEM,) * (1 + len(held)),
+        input_output_aliases={8: 1} if held else {},
+        scratch_shapes=[pltpu.SemaphoreType.DMA((1 + 2 * F // D,))],
         compiler_params=pltpu.CompilerParams(vmem_limit_bytes=limit, dimension_semantics=("arbitrary", "arbitrary")),
         cost_estimate=pl.CostEstimate(flops=4 * count * SEQ * SEQ * D, bytes_accessed=count * SEQ * D * 9, transcendentals=count * SEQ * SEQ * HEADS),
         name="attn",
-    )(*at_hbm(q, k, v, nq2, nk2), w_o, w_up, w_down)
+    )(*at_hbm(q, k, v, nq2, nk2), w_o, w_up, w_down, *at_vmem(*held))
 
 
 def gelu(u):
@@ -356,16 +401,19 @@
     return (0.5 * u) * (1.0 + jnp.tanh(u * (c + (c * 0.044715) * (u * u))))
 
 
-def mlp_kernel(*refs, layer, base, n, fc, nc, alias, send):
+def mlp_kernel(*refs, layer, base, n, fc, nc, alias, send, count):
     (x_hbm, o_hbm, bo_ref, g_ref, s_ref, bu_ref, bd_ref), refs = refs[:7], refs[7:]
-    wb, refs = refs[0], refs[1 + alias:]
+    weights, refs = refs[:count], refs[count + alias:]
     out_ref, refs = refs[0], refs[1:]
     if send:
         vbuf, refs = refs[0], refs[1:]
     (xb, ob, m_s, n_s, act, acc, xsem, osem), refs = refs[:8], refs[8:]
 
     def w(b, cs):
-        return wb[b * D:(b + 1) * D, cs]
+        if count == 2:
+            ref, b = (weights[0], b) if b < EARLY else (weights[1], b - EARLY)
+            return ref[b * D:(b + 1) * D, cs]
+        return weights[0][b * D:(b + 1) * D, cs]
 
     i = pl.program_id(0)
     tm = BLK
@@ -432,17 +480,17 @@
 
     @pl.when(i == 0)
     def _():
+        o_copy(0).start()
         x_copy(0).start()
-        o_copy(0).start()
-        x_copy(1).start()
-        o_copy(1).start()
         if send:
             barrier = pltpu.get_barrier_semaphore()
             for peer in (me + 1 - 2 * (me % 2), lax.rem(me + 2, 4), 3 - me):
                 pl.semaphore_signal(barrier, inc=1, device_id=(dp, peer), device_id_type=MESH)
             pl.semaphore_wait(barrier, 3)
+        o_copy(0).wait()
         x_copy(0).wait()
-        o_copy(0).wait()
+        o_copy(1).start()
+        x_copy(1).start()
         project(0)
         norm()
 
@@ -523,25 +571,26 @@
     extra = [] if into is None else [into]
     tok = n * BLK
     return pl.pallas_call(
-        functools.partial(mlp_kernel, layer=layer, base=base, n=n, fc=fc, nc=nc, alias=len(extra), send=send),
+        functools.partial(mlp_kernel, layer=layer, base=base, n=n, fc=fc, nc=nc, alias=len(extra), send=send, count=len(w)),
         out_shape=out_shape,
         grid=(n,),
-        in_specs=[HBM, HBM, whole((2, D)), whole((2, D)), whole((2, D)), whole((2, F)), whole((2, D))] + [VMEM] + [HBM] * len(extra),
+        in_specs=[HBM, HBM, whole((2, D)), whole((2, D)), whole((2, D)), whole((2, F)), whole((2, D))] + [VMEM] * len(w) + [HBM] * len(extra),
         out_specs=out_spec,
         scratch_shapes=scratch,
-        input_output_aliases={8: 0} if extra else {},
+        input_output_aliases={7 + len(w): 0} if extra else {},
         compiler_params=pltpu.CompilerParams(vmem_limit_bytes=SEND_LIMIT if send else LAYER_LIMIT, **params),
         cost_estimate=pl.CostEstimate(flops=2 * tok * D * (2 * F + D), bytes_accessed=tok * D * 6, transcendentals=tok * F),
         name="mlp",
-    )(*at_hbm(x, o, bo, g, s, bu, bd), *at_vmem(w), *extra)
+    )(*at_hbm(x, o, bo, g, s, bu, bd), *at_vmem(*w), *extra)
 
 
 def finish_kernel(arrived, vbuf, out, buf, in_sem, via_sem, v_sem):
     me = lax.axis_index("sp")
     copy = pltpu.make_async_copy
     owner = (lax.rem(me + 2, 4), 3 - me, me + 1 - 2 * (me % 2))
-    ins = [copy(arrived.at[p * IMAGES:(p + 1) * IMAGES], buf.at[p], in_sem.at[p]) for p in range(3)]
-    outs = [copy(buf.at[p], out.at[pl.ds(o * IMAGES, IMAGES)], via_sem.at[p]) for p, o in enumerate(owner)]
+    blocks = range(3 * IMAGES)
+    ins = [copy(arrived.at[p], buf.at[p], in_sem.at[p]) for p in blocks]
+    outs = [copy(buf.at[p], out.at[owner[p // IMAGES] * IMAGES + p % IMAGES], via_sem.at[p]) for p in blocks]
     own = copy(vbuf.at[SLOTS:], out.at[pl.ds(me * IMAGES, IMAGES)], v_sem)
     for c in ins:
         c.start()
@@ -561,7 +610,7 @@
         out_shape=jax.ShapeDtypeStruct((4 * IMAGES, BLK, D), bf16),
         in_specs=[HBM, VMEM],
         out_specs=HBM,
-        scratch_shapes=[pltpu.VMEM((3, IMAGES, BLK, D), bf16), dma((3,)), dma((3,)), dma(())],
+        scratch_shapes=[pltpu.VMEM((3 * IMAGES, BLK, D), bf16), dma((3 * IMAGES,)), dma((3 * IMAGES,)), dma(())],
         compiler_params=pltpu.CompilerParams(vmem_limit_bytes=SEND_LIMIT),
         cost_estimate=pl.CostEstimate(flops=0, bytes_accessed=24 << 20, transcendentals=0),
         name="finish",
@@ -595,16 +644,17 @@
         def post(x, l, o, w, *place, **kw):
             return mlp(x, o, w, b_out, ln2_gain, ln2_shift, b_up, b_down, l, *place, **kw)
 
-        *bufs, wq = qkv(par, image_tokens, lambda i, m: m[0] * IMAGES + i, near, here, *pre, w_t, b_qkv, 0, IMAGES, lambda i: 2 * i, True, hand=True)
-        bufs = qkv(par, far_a, here, far_b, here, *pre, wq, b_qkv, 0, 1, lambda i: 1, True, into=bufs, given=True)
-        o, wb = attn(*bufs[:5], *others, 0, 0, 1)
-        h = post(bufs[5], 0, o, wb, 0, 1)
+        *bufs, wa, wq = qkv(par, image_tokens, lambda i, m: m[0] * IMAGES + i, near, here, *pre, w_t, b_qkv, 0, IMAGES, lambda i: 2 * i, True,
+                            hand=others)
+        *bufs, wa = qkv(par, far_a, here, far_b, here, *pre, wq, b_qkv, 0, 1, lambda i: 1, True, into=bufs, given=wa)
+        o, *w = attn(*bufs[:5], *others, 0, 0, 1, keep=wa)
+        h = post(bufs[5], 0, o, w, 0, 1)
         bufs = qkv(par, rest_a, here, rest_b, here, *pre, w_t, b_qkv, 0, IMAGES - 1, lambda i: 2 * i + 3, True, into=bufs, after=h)
-        o, wb = attn(*bufs[:5], *others, 0, 1, IMAGES - 1)
-        h = post(bufs[5], 0, o, wb, 1, IMAGES - 1, into=h)
+        o, *w = attn(*bufs[:5], *others, 0, 1, IMAGES - 1)
+        h = post(bufs[5], 0, o, w, 1, IMAGES - 1, into=h)
         x = h.reshape(4 * IMAGES, BLK, D)
         bufs = qkv(par, x, lambda i, m: 2 * i, x, lambda i, m: 2 * i + 1, *pre, w_t, b_qkv, 1, 2 * IMAGES, lambda i: i, False)
-        o, wb = attn(*bufs[:5], *others, 1, 0, IMAGES, limit=SEND_LIMIT)
-        return finish(*post(h, 1, o, wb, 0, IMAGES, send=True))
+        o, *w = attn(*bufs[:5], *others, 1, 0, IMAGES, limit=SEND_LIMIT)
+        return finish(*post(h, 1, o, w, 0, IMAGES, send=True))
 
     return jax.shard_map(device_step, mesh=mesh, in_specs=(token_spec,) + (P(),) * 12, out_specs=token_spec, check_vma=False)

time: 702 us -> 698 us (level)
    pallas_call x3, Pallas kernels: 130 us -> 123 us  [attn(): pl.pallas_call(functools.partial(attn_kernel, layer=layer, have=have, hp=...]
  transfers between devices with their start and end apart: 4 -> 4, of which waited for: 0 -> 1; matrix products, arithmetic and copies ran while one was open for 0% -> 0% of each run, Pallas kernels for 20% -> 19%
where the time goes in v9:
time: 698 us; the launch traced here: 694 us
  Pallas kernels  683 us (98%)
    pallas_call x3, Pallas kernels, mlp(): pl.pallas_call(functools.partial(mlp_kernel, layer=layer, base=base, n=n,...  385 us
    pallas_call x4, Pallas kernels, qkv(): pl.pallas_call(functools.partial(qkv_kernel, layer=layer, n=n, copy_h=cop...  161 us
    pallas_call x3, Pallas kernels, attn(): pl.pallas_call(functools.partial(attn_kernel, layer=layer, have=have, hp=...  123 us
  transfers between devices with their start and end apart: 4, of which 1 were waited for; matrix products, arithmetic and copies ran while one was open for 0% of the time, Pallas kernels for 19%

profile of v9, /device:TPU:0, one launch (start us, length us, event | category | flops | bytes accessed | tf_op | source)
XLA Modules:
  0.0 693.9 jit_solution(9429707067830609590)
XLA Ops:
  0.0 2.6 constant_dynamic-slice_fusion
  2.6 2.8 collective-permute-start.3
  5.4 0.6 collective-permute-start.2
  6.0 5.7 start.1
  11.7 1.6 collective-permute-start
  13.2 0.0 collective-permute-start.1
  13.2 42.7 %qkv.4 = (bf16[1536,4096]{1,0:T(8,128)(2,1)}, bf16[16,4096,128]{2,1,0:T(8,128)(2,1)}, bf16[1536,4096]{1,0:T(8,128)(2,1)}, f32[16,4096]{1,0:T(8,128)}, f32[16,409...) custom-call(s32[1]{0:T(128)} %bitcast.refs_0_, ...), custom_call_target="tpu_custom_call" | custom-call | flops 28991029248 | bytes 31457280 | tf_op jit(solution)/shard_map/qkv/pallas_call | solution.py:288
  55.9 0.0 collective-permute-done.3.refs_2_.refs_4_
  55.9 0.0 collective-permute-done.2.refs_1_.refs_3_
  55.9 12.8 %qkv.5 = (bf16[1536,4096]{1,0:T(8,128)(2,1)}, bf16[16,4096,128]{2,1,0:T(8,128)(2,1)}, bf16[1536,4096]{1,0:T(8,128)(2,1)}, f32[16,4096]{1,0:T(8,128)}, f32[16,409...) custom-call(s32[1]{0:T(128)} %bitcast.refs_0_, ...), custom_call_target="tpu_custom_call", output_to_operand_aliasing={{0}: (10, {}), {1}: (11, {}), {2}: (12, {}), {3}: (13, {}),... | custom-call | flops 7247757312 | bytes 7864320 | tf_op jit(solution)/shard_map/qkv/pallas_call | solution.py:288
  68.7 17.9 %attn.3 = (bf16[1536,1024]{1,0:T(8,128)(2,1)}, bf16[9216,1536]{1,0:T(8,128)(2,1)S(1)}, bf16[4608,1536]{1,0:T(8,128)(2,1)S(1)}) custom-call(bf16[1536,4096]{1,0:T(8,128)(2,1)} %get-tuple-element.54.q_ref.refs_9_, bf16[16,4096,128]{2,1,0:T(8,128)(2,1)} %get-tuple-element.55.k_ref.refs_10_, ...), custom_call_target="tpu_custom_call", output_to_operand_aliasing={{1}: (8, {})} | custom-call | flops 6442450944 | bytes 14155776 | tf_op jit(solution)/shard_map/attn/pallas_call | solution.py:385
  86.6 51.4 %mlp.3.refs_15_.refs_8_ = bf16[4096,1536]{1,0:T(8,128)(2,1)} custom-call(bf16[4096,1536]{1,0:T(8,128)(2,1)} %get-tuple-element.59.refs_0_.refs_14_, bf16[1536,1024]{1,0:T(8,128)(2,1)} %get-tuple-element.61.refs_1_, f32[2,1536]{1,0:T(2,128)} %refs_2_.5, f32[2,1536]{1,0:T(2,128)} %refs_3_.7, f32[2,1536]{1,0:T(2,128)} %refs_4_.5, f32[2,6144]{1,0:T(2,128)} %refs_5_.13, ...), custom_call_target="tpu_custom_call" | custom-call | flops 43486543872 | bytes 9437184 | tf_op jit(solution)/shard_map/mlp/pallas_call | solution.py:573
  138.0 0.0 collective-permute-done.refs_1_.refs_3_
  138.0 3.3 collective-permute-done.1.refs_2_.refs_4_
  141.3 32.8 %qkv.6 = (bf16[1536,4096]{1,0:T(8,128)(2,1)}, bf16[16,4096,128]{2,1,0:T(8,128)(2,1)}, bf16[1536,4096]{1,0:T(8,128)(2,1)}, f32[16,4096]{1,0:T(8,128)}, f32[16,4096]{1,0:T(8,128)}, /*index=5*/bf16[4096,1536]{1,0:T(8,128)(2,1)}) custom-call(s32[1]{0:T(128)} %bitcast.refs_0_, ...), custom_call_target="tpu_custom_call", output_to_operand_aliasing={{0}: (9, {}), {1}: (10, {}), {2}: (11, {}), {3}: (12, {}), ... | custom-call | flops 21743271936 | bytes 23592960 | tf_op jit(solution)/shard_map/qkv/pallas_call | solution.py:288
  174.1 45.6 %attn.4 = (bf16[1536,3072]{1,0:T(8,128)(2,1)}, bf16[13824,1536]{1,0:T(8,128)(2,1)S(1)}) custom-call(bf16[1536,4096]{1,0:T(8,128)(2,1)} %get-tuple-element.65.q_ref, bf16[16,4096,128]{2,1,0:T(8,128)(2,1)} %get-tuple-element.66.k_ref, bf16[1536,4096]{1,0:T(8,128)(2,1)} %get-tuple-element.67.v_ref, f32[16,4096]{1,0:T(8,128)} %get-tuple-element.68.nq_ref, ...), custom_call_target="tpu_custom_call" | custom-call | flops 19327352832 | bytes 42467328 | tf_op jit(solution)/shard_map/attn/pallas_call | solution.py:385
  219.7 142.8 %mlp.4.refs_0_ = bf16[4096,1536]{1,0:T(8,128)(2,1)} custom-call(bf16[4096,1536]{1,0:T(8,128)(2,1)} %get-tuple-element.64.refs_0_, bf16[1536,3072]{1,0:T(8,128)(2,1)} %get-tuple-element.70.refs_1_, f32[2,1536]{1,0:T(2,128)} %refs_2_.5, f32[2,1536]{1,0:T(2,128)} %refs_3_.7, f32[2,1536]{1,0:T(2,128)} %refs_4_.5, ...), custom_call_target="tpu_custom_call", output_to_operand_aliasing={{}: (8, {})} | custom-call | flops 130459631616 | bytes 28311552 | tf_op jit(solution)/shard_map/mlp/pallas_call | solution.py:573
  362.6 72.7 %qkv.7 = (bf16[1536,4096]{1,0:T(8,128)(2,1)}, bf16[16,4096,128]{2,1,0:T(8,128)(2,1)}, bf16[1536,4096]{1,0:T(8,128)(2,1)}, f32[16,4096]{1,0:T(8,128)}, f32[16,4096]{1,0:T(8,128)}) custom-call(s32[1]{0:T(128)} %bitcast.refs_0_, bf16[16,256,1536]{2,1,0:T(8,128)(2,1)} %bitcast.13, bf16[16,256,1536]{2,1,0:T(8,128)(2,1)} %bitcast.14, ...), custom_call_target="tpu_custom_call" | custom-call | flops 57982058496 | bytes 62914560 | tf_op jit(solution)/shard_map/qkv/pallas_call | solution.py:288
  435.3 59.6 %attn.5 = (bf16[1536,4096]{1,0:T(8,128)(2,1)}, bf16[13824,1536]{1,0:T(8,128)(2,1)S(1)}) custom-call(bf16[1536,4096]{1,0:T(8,128)(2,1)} %get-tuple-element.72.q_ref, bf16[16,4096,128]{2,1,0:T(8,128)(2,1)} %get-tuple-element.73.k_ref, bf16[1536,4096]{1,0:T(8,128)(2,1)} %get-tuple-element.74.v_ref, f32[16,4096]{1,0:T(8,128)} %get-tuple-element.75.nq_ref, ...), custom_call_target="tpu_custom_call" | custom-call | flops 25769803776 | bytes 56623104 | tf_op jit(solution)/shard_map/attn/pallas_call | solution.py:385
  494.9 190.3 %mlp.5 = (bf16[12,256,1536]{2,1,0:T(8,128)(2,1)}, bf16[7,256,1536]{2,1,0:T(8,128)(2,1)S(1)}) custom-call(bf16[4096,1536]{1,0:T(8,128)(2,1)} %mlp.4.refs_0_, bf16[1536,4096]{1,0:T(8,128)(2,1)} %get-tuple-element.77.refs_1_, f32[2,1536]{1,0:T(2,128)} %refs_2_.5, f32[2,1536]{1,0:T(2,128)} %refs_3_.7, f32[2,1536]{1,0:T(2,128)} %refs_4_.5, f32[2,6144]{1,0:T(2,128)} %refs_5_.13, ...), custom_call_target="tpu_custom_call" | custom-call | flops 173946175488 | bytes 37748736 | tf_op jit(solution)/shard_map/mlp/pallas_call | solution.py:573
  685.2 8.3 %finish.1 = bf16[16,256,1536]{2,1,0:T(8,128)(2,1)} custom-call(bf16[12,256,1536]{2,1,0:T(8,128)(2,1)} %get-tuple-element.79.arrived, bf16[7,256,1536]{2,1,0:T(8,128)(2,1)S(1)} %get-tuple-element.80.vbuf), custom_call_target="tpu_custom_call" | custom-call | bytes 25165824 | tf_op jit(solution)/shard_map/finish/pallas_call | solution.py:608
Async XLA Ops:
  2.6 53.2 %collective-permute-start.3 = (bf16[1,256,1536]{2,1,0:T(8,128)(2,1)}, bf16[1,256,1536]{2,1,0:T(8,128)(2,1)}, u32[]{:S(2)}, u32[]{:S(2)}) collective-permute-start(bf16[1,256,1536]{2,1,0:T(8,128)(2,1)} %get-tuple-element.81), channel_id=1, source_target_pairs={{0,3},{1,2},{2,1},{3,0},{4,7},{5,6},{6,5},{7,4}} | collective-permute-start | bytes 2359304 | tf_op jit(solution)/shard_map/ppermute | solution.py:631
  5.4 50.5 %collective-permute-start.2 = (bf16[1,256,1536]{2,1,0:T(8,128)(2,1)}, bf16[1,256,1536]{2,1,0:T(8,128)(2,1)}, u32[]{:S(2)}, u32[]{:S(2)}) collective-permute-start(bf16[1,256,1536]{2,1,0:T(8,128)(2,1)} %get-tuple-element.82), channel_id=1, source_target_pairs={{0,2},{1,3},{2,0},{3,1},{4,6},{5,7},{6,4},{7,5}} | collective-permute-start | bytes 2359304 | tf_op jit(solution)/shard_map/ppermute | solution.py:631
  11.7 126.4 %collective-permute-start = (bf16[3,256,1536]{2,1,0:T(8,128)(2,1)}, bf16[3,256,1536]{2,1,0:T(8,128)(2,1)}, u32[]{:S(2)}, u32[]{:S(2)}) collective-permute-start(bf16[3,256,1536]{2,1,0:T(8,128)(2,1)} %get-tuple-element.43), channel_id=1, source_target_pairs={{0,2},{1,3},{2,0},{3,1},{4,6},{5,7},{6,4},{7,5}} | collective-permute-start | bytes 7077896 | tf_op jit(solution)/shard_map/ppermute | solution.py:631
  13.2 128.1 %collective-permute-start.1 = (bf16[3,256,1536]{2,1,0:T(8,128)(2,1)}, bf16[3,256,1536]{2,1,0:T(8,128)(2,1)}, u32[]{:S(2)}, u32[]{:S(2)}) collective-permute-start(bf16[3,256,1536]{2,1,0:T(8,128)(2,1)} %get-tuple-element.44), channel_id=1, source_target_pairs={{0,3},{1,2},{2,1},{3,0},{4,7},{5,6},{6,5},{7,4}} | collective-permute-start | bytes 7077896 | tf_op jit(solution)/shard_map/ppermute | solution.py:631

commit v10 on v9

--- a/solution.py
+++ b/solution.py
@@ -40,7 +40,7 @@
 LAYER_LIMIT = 93 << 18
 EARLY = 6
 SEND_LIMIT = 18 << 20
-TURNS = 2
+TURNS = 4
 SLOTS = 3
 
 
@@ -129,7 +129,8 @@
         w_hbm, w = w, refs[2]
     i = pl.program_id(0)
     tm = 2 * BLK
-    per = D // CH
+    ch = CH // 2 if given else CH
+    per = D // ch
     order = (1, 0, 2)
     gain, shift = g_ref[layer:layer + 1, :], s_ref[layer:layer + 1, :]
 
@@ -154,12 +155,12 @@
             norm(b, dst, slot, r, r + BLK)
 
     def project(t, c, slot):
-        y = dot_nt(w[pl.ds(chunk(c, CH) + t * D, CH), :], both[slot])
-        heads = CH // HD
+        y = dot_nt(w[pl.ds(chunk(c, ch) + t * D, ch), :], both[slot])
+        heads = ch // HD
         bias = b_ref[layer, t, pl.ds(chunk(c, heads), heads), :].T
         bias = jnp.concatenate([jnp.broadcast_to(bias[:, h:h + 1], (HD, tm)) for h in range(heads)], axis=0)
         yb = (y + bias).astype(bf16)
-        r0 = pl.ds(chunk(c, CH), CH)
+        r0 = pl.ds(chunk(c, ch), ch)
         if t == 2:
             v_ref[r0, :] = yb
             return

time: 698 us -> 698 us (level)
  transfers between devices with their start and end apart: 4 -> 4, of which waited for: 1 -> 0; matrix products, arithmetic and copies ran while one was open for 0% -> 0% of each run, Pallas kernels for 19% -> 19%
where the time goes in v10:
time: 698 us; the launch traced here: 695 us
  Pallas kernels  687 us (98%)
    pallas_call x3, Pallas kernels, mlp(): pl.pallas_call(functools.partial(mlp_kernel, layer=layer, base=base, n=n,...  384 us
    pallas_call x4, Pallas kernels, qkv(): pl.pallas_call(functools.partial(qkv_kernel, layer=layer, n=n, copy_h=cop...  166 us
    pallas_call x3, Pallas kernels, attn(): pl.pallas_call(functools.partial(attn_kernel, layer=layer, have=have, hp=...  123 us
  transfers between devices with their start and end apart: 4, of which 0 were waited for; matrix products, arithmetic and copies ran while one was open for 0% of the time, Pallas kernels for 19%

profile of v10, /device:TPU:0, one launch (start us, length us, event | category | flops | bytes accessed | tf_op | source)
XLA Modules:
  0.0 694.8 jit_solution(3322150775377560121)
XLA Ops:
  0.0 2.6 constant_dynamic-slice_fusion
  2.6 2.8 collective-permute-start.3
  5.4 0.6 collective-permute-start.2
  6.0 5.7 start.1
  11.7 1.6 collective-permute-start
  13.2 0.0 collective-permute-start.1
  13.2 43.0 %qkv.4 = (bf16[1536,4096]{1,0:T(8,128)(2,1)}, bf16[16,4096,128]{2,1,0:T(8,128)(2,1)}, bf16[1536,4096]{1,0:T(8,128)(2,1)}, f32[16,4096]{1,0:T(8,128)}, f32[16,409...) custom-call(s32[1]{0:T(128)} %bitcast.refs_0_, ...), custom_call_target="tpu_custom_call" | custom-call | flops 28991029248 | bytes 31457280 | tf_op jit(solution)/shard_map/qkv/pallas_call | solution.py:289
  56.2 0.0 collective-permute-done.3.refs_2_.refs_4_
  56.2 0.0 collective-permute-done.2.refs_1_.refs_3_
  56.3 17.3 %qkv.5 = (bf16[1536,4096]{1,0:T(8,128)(2,1)}, bf16[16,4096,128]{2,1,0:T(8,128)(2,1)}, bf16[1536,4096]{1,0:T(8,128)(2,1)}, f32[16,4096]{1,0:T(8,128)}, f32[16,409...) custom-call(s32[1]{0:T(128)} %bitcast.refs_0_, ...), custom_call_target="tpu_custom_call", output_to_operand_aliasing={{0}: (10, {}), {1}: (11, {}), {2}: (12, {}), {3}: (13, {}),... | custom-call | flops 7247757312 | bytes 7864320 | tf_op jit(solution)/shard_map/qkv/pallas_call | solution.py:289
  73.6 17.9 %attn.3 = (bf16[1536,1024]{1,0:T(8,128)(2,1)}, bf16[9216,1536]{1,0:T(8,128)(2,1)S(1)}, bf16[4608,1536]{1,0:T(8,128)(2,1)S(1)}) custom-call(bf16[1536,4096]{1,0:T(8,128)(2,1)} %get-tuple-element.54.q_ref.refs_9_, bf16[16,4096,128]{2,1,0:T(8,128)(2,1)} %get-tuple-element.55.k_ref.refs_10_, ...), custom_call_target="tpu_custom_call", output_to_operand_aliasing={{1}: (8, {})} | custom-call | flops 6442450944 | bytes 14155776 | tf_op jit(solution)/shard_map/attn/pallas_call | solution.py:386
  91.5 51.4 %mlp.3.refs_15_.refs_8_ = bf16[4096,1536]{1,0:T(8,128)(2,1)} custom-call(bf16[4096,1536]{1,0:T(8,128)(2,1)} %get-tuple-element.59.refs_0_.refs_14_, bf16[1536,1024]{1,0:T(8,128)(2,1)} %get-tuple-element.61.refs_1_, f32[2,1536]{1,0:T(2,128)} %refs_2_.5, f32[2,1536]{1,0:T(2,128)} %refs_3_.7, f32[2,1536]{1,0:T(2,128)} %refs_4_.5, f32[2,6144]{1,0:T(2,128)} %refs_5_.13, ...), custom_call_target="tpu_custom_call" | custom-call | flops 43486543872 | bytes 9437184 | tf_op jit(solution)/shard_map/mlp/pallas_call | solution.py:574
  142.9 0.0 collective-permute-done.refs_1_.refs_3_
  142.9 0.0 collective-permute-done.1.refs_2_.refs_4_
  142.9 32.8 %qkv.6 = (bf16[1536,4096]{1,0:T(8,128)(2,1)}, bf16[16,4096,128]{2,1,0:T(8,128)(2,1)}, bf16[1536,4096]{1,0:T(8,128)(2,1)}, f32[16,4096]{1,0:T(8,128)}, f32[16,4096]{1,0:T(8,128)}, /*index=5*/bf16[4096,1536]{1,0:T(8,128)(2,1)}) custom-call(s32[1]{0:T(128)} %bitcast.refs_0_, ...), custom_call_target="tpu_custom_call", output_to_operand_aliasing={{0}: (9, {}), {1}: (10, {}), {2}: (11, {}), {3}: (12, {}), ... | custom-call | flops 21743271936 | bytes 23592960 | tf_op jit(solution)/shard_map/qkv/pallas_call | solution.py:289
  175.8 45.6 %attn.4 = (bf16[1536,3072]{1,0:T(8,128)(2,1)}, bf16[13824,1536]{1,0:T(8,128)(2,1)S(1)}) custom-call(bf16[1536,4096]{1,0:T(8,128)(2,1)} %get-tuple-element.65.q_ref, bf16[16,4096,128]{2,1,0:T(8,128)(2,1)} %get-tuple-element.66.k_ref, bf16[1536,4096]{1,0:T(8,128)(2,1)} %get-tuple-element.67.v_ref, f32[16,4096]{1,0:T(8,128)} %get-tuple-element.68.nq_ref, ...), custom_call_target="tpu_custom_call" | custom-call | flops 19327352832 | bytes 42467328 | tf_op jit(solution)/shard_map/attn/pallas_call | solution.py:386
  221.4 142.8 %mlp.4.refs_0_ = bf16[4096,1536]{1,0:T(8,128)(2,1)} custom-call(bf16[4096,1536]{1,0:T(8,128)(2,1)} %get-tuple-element.64.refs_0_, bf16[1536,3072]{1,0:T(8,128)(2,1)} %get-tuple-element.70.refs_1_, f32[2,1536]{1,0:T(2,128)} %refs_2_.5, f32[2,1536]{1,0:T(2,128)} %refs_3_.7, f32[2,1536]{1,0:T(2,128)} %refs_4_.5, ...), custom_call_target="tpu_custom_call", output_to_operand_aliasing={{}: (8, {})} | custom-call | flops 130459631616 | bytes 28311552 | tf_op jit(solution)/shard_map/mlp/pallas_call | solution.py:574
  364.2 72.7 %qkv.7 = (bf16[1536,4096]{1,0:T(8,128)(2,1)}, bf16[16,4096,128]{2,1,0:T(8,128)(2,1)}, bf16[1536,4096]{1,0:T(8,128)(2,1)}, f32[16,4096]{1,0:T(8,128)}, f32[16,4096]{1,0:T(8,128)}) custom-call(s32[1]{0:T(128)} %bitcast.refs_0_, bf16[16,256,1536]{2,1,0:T(8,128)(2,1)} %bitcast.13, bf16[16,256,1536]{2,1,0:T(8,128)(2,1)} %bitcast.14, ...), custom_call_target="tpu_custom_call" | custom-call | flops 57982058496 | bytes 62914560 | tf_op jit(solution)/shard_map/qkv/pallas_call | solution.py:289
  437.0 59.6 %attn.5 = (bf16[1536,4096]{1,0:T(8,128)(2,1)}, bf16[13824,1536]{1,0:T(8,128)(2,1)S(1)}) custom-call(bf16[1536,4096]{1,0:T(8,128)(2,1)} %get-tuple-element.72.q_ref, bf16[16,4096,128]{2,1,0:T(8,128)(2,1)} %get-tuple-element.73.k_ref, bf16[1536,4096]{1,0:T(8,128)(2,1)} %get-tuple-element.74.v_ref, f32[16,4096]{1,0:T(8,128)} %get-tuple-element.75.nq_ref, ...), custom_call_target="tpu_custom_call" | custom-call | flops 25769803776 | bytes 56623104 | tf_op jit(solution)/shard_map/attn/pallas_call | solution.py:386
  496.5 189.5 %mlp.5 = (bf16[12,256,1536]{2,1,0:T(8,128)(2,1)}, bf16[7,256,1536]{2,1,0:T(8,128)(2,1)S(1)}) custom-call(bf16[4096,1536]{1,0:T(8,128)(2,1)} %mlp.4.refs_0_, bf16[1536,4096]{1,0:T(8,128)(2,1)} %get-tuple-element.77.refs_1_, f32[2,1536]{1,0:T(2,128)} %refs_2_.5, f32[2,1536]{1,0:T(2,128)} %refs_3_.7, f32[2,1536]{1,0:T(2,128)} %refs_4_.5, f32[2,6144]{1,0:T(2,128)} %refs_5_.13, ...), custom_call_target="tpu_custom_call" | custom-call | flops 173946175488 | bytes 37748736 | tf_op jit(solution)/shard_map/mlp/pallas_call | solution.py:574
  686.0 8.3 %finish.1 = bf16[16,256,1536]{2,1,0:T(8,128)(2,1)} custom-call(bf16[12,256,1536]{2,1,0:T(8,128)(2,1)} %get-tuple-element.79.arrived, bf16[7,256,1536]{2,1,0:T(8,128)(2,1)S(1)} %get-tuple-element.80.vbuf), custom_call_target="tpu_custom_call" | custom-call | bytes 25165824 | tf_op jit(solution)/shard_map/finish/pallas_call | solution.py:609
Async XLA Ops:
  2.6 53.6 %collective-permute-start.3 = (bf16[1,256,1536]{2,1,0:T(8,128)(2,1)}, bf16[1,256,1536]{2,1,0:T(8,128)(2,1)}, u32[]{:S(2)}, u32[]{:S(2)}) collective-permute-start(bf16[1,256,1536]{2,1,0:T(8,128)(2,1)} %get-tuple-element.81), channel_id=1, source_target_pairs={{0,3},{1,2},{2,1},{3,0},{4,7},{5,6},{6,5},{7,4}} | collective-permute-start | bytes 2359304 | tf_op jit(solution)/shard_map/ppermute | solution.py:632
  5.4 50.8 %collective-permute-start.2 = (bf16[1,256,1536]{2,1,0:T(8,128)(2,1)}, bf16[1,256,1536]{2,1,0:T(8,128)(2,1)}, u32[]{:S(2)}, u32[]{:S(2)}) collective-permute-start(bf16[1,256,1536]{2,1,0:T(8,128)(2,1)} %get-tuple-element.82), channel_id=1, source_target_pairs={{0,2},{1,3},{2,0},{3,1},{4,6},{5,7},{6,4},{7,5}} | collective-permute-start | bytes 2359304 | tf_op jit(solution)/shard_map/ppermute | solution.py:632
  11.7 131.3 %collective-permute-start = (bf16[3,256,1536]{2,1,0:T(8,128)(2,1)}, bf16[3,256,1536]{2,1,0:T(8,128)(2,1)}, u32[]{:S(2)}, u32[]{:S(2)}) collective-permute-start(bf16[3,256,1536]{2,1,0:T(8,128)(2,1)} %get-tuple-element.43), channel_id=1, source_target_pairs={{0,2},{1,3},{2,0},{3,1},{4,6},{5,7},{6,4},{7,5}} | collective-permute-start | bytes 7077896 | tf_op jit(solution)/shard_map/ppermute | solution.py:632
  13.2 129.7 %collective-permute-start.1 = (bf16[3,256,1536]{2,1,0:T(8,128)(2,1)}, bf16[3,256,1536]{2,1,0:T(8,128)(2,1)}, u32[]{:S(2)}, u32[]{:S(2)}) collective-permute-start(bf16[3,256,1536]{2,1,0:T(8,128)(2,1)} %get-tuple-element.44), channel_id=1, source_target_pairs={{0,3},{1,2},{2,1},{3,0},{4,7},{5,6},{6,5},{7,4}} | collective-permute-start | bytes 7077896 | tf_op jit(solution)/shard_map/ppermute | solution.py:632
